TPU v7x, 16 devices: a 4x2x1 block of a 4x4x8 slice. The times are simulated.
16 devices in a mesh: dp: 2 (over y, z), tp: 8 (over x, core).
Axes of the slice: x: 4, y: 2, z: 1, core: 2. Of those that a mesh axis runs over, the one named last changes fastest.
The devices are a block of a 4x4x8 slice.
Arguments:
- x_in: bfloat16 [4, 1024, 3840], P('dp', 'tp'), parts along dimension 0
- positions: int32 [4, 1024], P('dp'), parts along dimension 0
- w_q: bfloat16 [3840, 16, 256], P(None, 'tp')
- w_k: bfloat16 [3840, 8, 256], P(None, 'tp')
- w_v: bfloat16 [3840, 8, 256], P(None, 'tp')
- w_o: bfloat16 [16, 256, 3840], P('tp')
- w_gate: bfloat16 [3840, 15360], P(None, 'tp')
- w_up: bfloat16 [3840, 15360], P(None, 'tp')
- w_down: bfloat16 [15360, 3840], P('tp')
- gain_attn: float32 [3840], replicated
- gain_mlp: float32 [3840], replicated
- d_out: bfloat16 [4, 1024, 3840], P('dp', 'tp'), parts along dimension 0
Outputs:
- output 1: bfloat16 [4, 1024, 3840], P('dp', 'tp'), parts along dimension 0
- output 2: bfloat16 [4, 1024, 3840], P('dp', 'tp'), parts along dimension 0
- output 3: bfloat16 [7680, 16, 256], P('dp', 'tp'), parts along dimension 0
- output 4: bfloat16 [7680, 8, 256], P('dp', 'tp'), parts along dimension 0
- output 5: bfloat16 [7680, 8, 256], P('dp', 'tp'), parts along dimension 0
- output 6: bfloat16 [32, 256, 3840], P(('dp', 'tp')), parts along dimension 0
- output 7: bfloat16 [7680, 15360], P('dp', 'tp'), parts along dimension 0
- output 8: bfloat16 [7680, 15360], P('dp', 'tp'), parts along dimension 0
- output 9: bfloat16 [30720, 3840], P(('dp', 'tp')), parts along dimension 0
- output 10: float32 [7680], P('dp'), parts along dimension 0
- output 11: float32 [7680], P('dp'), parts along dimension 0
There are 2 independent parts. A program takes and returns all parts, laid end to end along the dimension named above; an argument that names none is the same for every part.
All inputs are finite; a program needn't handle non-finite values.
Results may differ from a plain program's by a relative error of at most 0.02.
Values are sent between devices in bfloat16 or wider.
A program may use at most 768 MiB of HBM per device.

v0:
```python
import jax
import jax.numpy as jnp
from jax import lax
from jax.sharding import PartitionSpec as P

EPS = 1e-6
ROPE_THETA = 10000.0


def rms_norm(vals, gain):
    vals_f32 = vals.astype(jnp.float32)
    inv_rms = lax.rsqrt(jnp.mean(vals_f32 * vals_f32, axis=-1, keepdims=True) + EPS)
    return (vals_f32 * inv_rms * (1.0 + gain)).astype(jnp.bfloat16)


def rope_tables(positions, head_dim):
    half_dim = head_dim // 2
    inv_freq = ROPE_THETA ** (-2.0 * jnp.arange(half_dim, dtype=jnp.float32) / head_dim)
    angles = positions.astype(jnp.float32)[:, :, None] * inv_freq
    return jnp.cos(angles)[:, :, None, :], jnp.sin(angles)[:, :, None, :]


def apply_rope(heads_in, cos_t, sin_t):
    half_dim = heads_in.shape[-1] // 2
    vals_f32 = heads_in.astype(jnp.float32)
    first_half = vals_f32[..., :half_dim]
    second_half = vals_f32[..., half_dim:]
    return jnp.concatenate([first_half * cos_t - second_half * sin_t, second_half * cos_t + first_half * sin_t], axis=-1)


def attend(q_rot, k_rot, v_rot, q_start):
    batch_size, q_len, n_heads, head_dim = q_rot.shape
    kv_heads = k_rot.shape[2]
    k_len = k_rot.shape[1]
    q_grp = q_rot.reshape(batch_size, q_len, kv_heads, n_heads // kv_heads, head_dim)
    scores = jnp.einsum("bqkgh,bskh->bkgqs", q_grp, k_rot, preferred_element_type=jnp.float32)
    causal = (q_start + jnp.arange(q_len))[:, None] >= jnp.arange(k_len)[None, :]
    scores = jnp.where(causal, scores, -1e30)
    attn_probs = jax.nn.softmax(scores, axis=-1).astype(jnp.bfloat16)
    attn_rows = jnp.einsum("bkgqs,bskh->bqkgh", attn_probs, v_rot, preferred_element_type=jnp.float32)
    return attn_rows.astype(jnp.bfloat16).reshape(batch_size, q_len, n_heads, head_dim)


def gated_act(gate_pre, up_pre):
    return (jax.nn.gelu(gate_pre.astype(jnp.float32), approximate=True) * up_pre.astype(jnp.float32)).astype(jnp.bfloat16)


def project_heads(acts, weight_mat):
    return jnp.einsum("bsd,dnh->bsnh", acts, weight_mat, preferred_element_type=jnp.float32).astype(jnp.bfloat16)


def solution(mesh):
    act_spec = P("dp", "tp", None)
    head_spec = P(None, "tp", None)
    in_specs = (act_spec, P("dp", None), head_spec, head_spec, head_spec, P("tp", None, None),
                P(None, "tp"), P(None, "tp"), P("tp", None), P(None), P(None), act_spec)
    out_specs = (act_spec, act_spec, P("dp", "tp", None), P("dp", "tp", None), P("dp", "tp", None),
                 P(("dp", "tp"), None, None), P("dp", "tp"), P("dp", "tp"), P(("dp", "tp"), None), P("dp"), P("dp"))

    def local_step(x_in, positions, w_q, w_k, w_v, w_o, w_gate, w_up, w_down, gain_attn, gain_mlp, d_out):
        head_dim = w_q.shape[2]
        q_scale = head_dim ** -0.5
        cos_t, sin_t = rope_tables(positions, head_dim)

        def attn_block(q_raw, k_raw, v_raw):
            q_rot = (apply_rope(q_raw, cos_t, sin_t) * q_scale).astype(jnp.bfloat16)
            k_rot = apply_rope(k_raw, cos_t, sin_t).astype(jnp.bfloat16)
            return attend(q_rot, k_rot, v_raw, 0)

        normed, norm_attn_pull = jax.vjp(rms_norm, x_in, gain_attn)
        normed_all = lax.all_gather(normed, "tp", axis=1, tiled=True)
        q_raw = project_heads(normed_all, w_q)
        k_raw = project_heads(normed_all, w_k)
        v_raw = project_heads(normed_all, w_v)
        attn_out, attn_pull = jax.vjp(attn_block, q_raw, k_raw, v_raw)
        attn_part = jnp.einsum("bsnh,nhd->bsd", attn_out, w_o, preferred_element_type=jnp.float32).astype(jnp.bfloat16)
        attn_proj = lax.psum_scatter(attn_part, "tp", scatter_dimension=1, tiled=True)
        hidden = (x_in.astype(jnp.float32) + attn_proj.astype(jnp.float32)).astype(jnp.bfloat16)
        mlp_in, norm_mlp_pull = jax.vjp(rms_norm, hidden, gain_mlp)
        mlp_all = lax.all_gather(mlp_in, "tp", axis=1, tiled=True)
        gate_pre = jnp.einsum("bsd,df->bsf", mlp_all, w_gate, preferred_element_type=jnp.float32).astype(jnp.bfloat16)
        up_pre = jnp.einsum("bsd,df->bsf", mlp_all, w_up, preferred_element_type=jnp.float32).astype(jnp.bfloat16)
        act_out, act_pull = jax.vjp(gated_act, gate_pre, up_pre)
        down_part = jnp.einsum("bsf,fd->bsd", act_out, w_down, preferred_element_type=jnp.float32).astype(jnp.bfloat16)
        down_out = lax.psum_scatter(down_part, "tp", scatter_dimension=1, tiled=True)
        y_out = (hidden.astype(jnp.float32) + down_out.astype(jnp.float32)).astype(jnp.bfloat16)

        dout_all = lax.all_gather(d_out, "tp", axis=1, tiled=True)
        d_act = jnp.einsum("bsd,fd->bsf", dout_all, w_down, preferred_element_type=jnp.float32).astype(jnp.bfloat16)
        grad_wdown = jnp.einsum("bsf,bsd->fd", act_out, dout_all, preferred_element_type=jnp.float32).astype(jnp.bfloat16)
        d_gate, d_up = act_pull(d_act)
        d_mlp_part = (jnp.einsum("bsf,df->bsd", d_gate, w_gate, preferred_element_type=jnp.float32)
                      + jnp.einsum("bsf,df->bsd", d_up, w_up, preferred_element_type=jnp.float32)).astype(jnp.bfloat16)
        grad_wgate = jnp.einsum("bsd,bsf->df", mlp_all, d_gate, preferred_element_type=jnp.float32).astype(jnp.bfloat16)
        grad_wup = jnp.einsum("bsd,bsf->df", mlp_all, d_up, preferred_element_type=jnp.float32).astype(jnp.bfloat16)
        d_mlp_in = lax.psum_scatter(d_mlp_part, "tp", scatter_dimension=1, tiled=True)
        d_hidden_norm, gain_mlp_part = norm_mlp_pull(d_mlp_in)
        d_hidden = d_out + d_hidden_norm
        d_hidden_all = lax.all_gather(d_hidden, "tp", axis=1, tiled=True)
        d_attn_out = jnp.einsum("bsd,nhd->bsnh", d_hidden_all, w_o, preferred_element_type=jnp.float32).astype(jnp.bfloat16)
        grad_wo = jnp.einsum("bsnh,bsd->nhd", attn_out, d_hidden_all, preferred_element_type=jnp.float32).astype(jnp.bfloat16)
        d_qraw, d_kraw, d_vraw = attn_pull(d_attn_out)
        d_normed_part = (jnp.einsum("bsnh,dnh->bsd", d_qraw, w_q, preferred_element_type=jnp.float32)
                         + jnp.einsum("bsnh,dnh->bsd", d_kraw, w_k, preferred_element_type=jnp.float32)
                         + jnp.einsum("bsnh,dnh->bsd", d_vraw, w_v, preferred_element_type=jnp.float32)).astype(jnp.bfloat16)
        grad_wq = jnp.einsum("bsd,bsnh->dnh", normed_all, d_qraw, preferred_element_type=jnp.float32).astype(jnp.bfloat16)
        grad_wk = jnp.einsum("bsd,bsnh->dnh", normed_all, d_kraw, preferred_element_type=jnp.float32).astype(jnp.bfloat16)
        grad_wv = jnp.einsum("bsd,bsnh->dnh", normed_all, d_vraw, preferred_element_type=jnp.float32).astype(jnp.bfloat16)
        d_normed = lax.psum_scatter(d_normed_part, "tp", scatter_dimension=1, tiled=True)
        d_x_norm, gain_attn_part = norm_attn_pull(d_normed)
        grad_x = d_hidden + d_x_norm
        grad_gain_mlp = lax.psum(gain_mlp_part, "tp")
        grad_gain_attn = lax.psum(gain_attn_part, "tp")
        return (y_out, grad_x, grad_wq, grad_wk, grad_wv, grad_wo, grad_wgate, grad_wup, grad_wdown,
                grad_gain_attn, grad_gain_mlp)

    return jax.shard_map(local_step, mesh=mesh, in_specs=in_specs, out_specs=out_specs, check_vma=False)
```

profile of v0, /device:TPU:112, one launch (start us, length us, event | category | flops | bytes accessed | tf_op | source)
XLA Modules:
  0.0 1143.4 jit_solution(7170694618118584668)
XLA Ops:
  7.3 2.1 fusion.83
  9.4 0.6 copy-done.46
  10.0 0.7 broadcast_add_fusion.1
  10.7 0.6 copy-done.30
  11.3 3.4 fusion.78
  14.8 0.1 reduce-scatter.5.cloned.1.call-start
  14.8 0.7 convert_element_type.200
  15.5 10.4 copy.24
  26.0 1.3 iota_compare_fusion
  27.2 4.7 multiply_cosine_fusion
  31.9 62.5 %all-gather.5.cloned.1.call-done = bf16[2,1024,3840]{2,1,0:T(8,128)(2,1)} async-done(((bf16[2,128,3840]{2,1,0:T(8,128)(2,1)}), bf16[2,1024,3840]{2,1,0:T(8,128)(2,1)}) %all-gather.5.cloned.1.call-update) | async-done | bytes 15728656 | tf_op jit(solution)/shard_map/all_gather | solution.py:71
  94.4 9.4 fusion.145
  103.8 5.3 fusion.171
  109.1 13.3 %convert_convert_fusion = f32[2,1024,2,256]{1,3,2,0:T(8,128)S(1)} fusion(bf16[3840,2,256]{0,2,1:T(8,128)(2,1)} %copy.24, bf16[2,1024,3840]{2,1,0:T(8,128)(2,1)} %all-gather.5.cloned.1.call-done), kind=kOutput, calls=%fused_computation.134 | convolution fusion | flops 8055160832 | bytes 23855104 | tf_op jit(solution)/shard_map/bsd,dnh->bsnh/dot_general | solution.py:49
  122.4 0.8 multiply_subtract_fusion
  123.3 0.4 copy-done.14
  123.6 7.8 fusion.11
  131.5 8.8 fusion.190
  140.3 10.5 fusion.148
  150.7 0.3 copy-done.3
  151.1 5.3 fusion.119
  156.4 1.3 copy-done.55
  157.7 13.8 %bitcast_convert_fusion = bf16[2,1024,3840]{2,1,0:T(8,128)(2,1)} fusion(bf16[2,256,3840]{2,1,0:T(8,128)(2,1)} %param.17, bf16[2,256,2,1024]{3,1,2,0:T(8,128)(2,1)S(1)} %fusion.119), kind=kOutput, calls=%fused_computation.3 | convolution fusion | flops 8060928000 | bytes 21757952 | tf_op jit(solution)/shard_map/bsnh,nhd->bsd/dot_general | solution.py:76
  171.6 0.1 all-gather.7.cloned.1.call-start
  171.6 0.6 copy-done.43
  172.2 83.3 %reduce-scatter.5.cloned.1.call-done = bf16[2,128,3840]{2,1,0:T(8,128)(2,1)} async-done(((bf16[2,1024,3840]{2,1,0:T(8,128)(2,1)}), bf16[2,128,3840]{2,1,0:T(8,128)(2,1)}) %reduce-scatter.5.cloned.1.call-update) | async-done | bytes 1966096 | tf_op jit(solution)/shard_map/reduce_scatter | solution.py:77
  255.5 3.0 fusion.86
  258.5 0.6 copy-done.48
  259.1 0.7 copy-done.1
  259.8 1.8 fusion.77
  261.7 0.6 all-gather.9.cloned.1.call-update
  262.4 75.8 %all-gather.7.cloned.1.call-done = bf16[2,1024,3840]{2,1,0:T(8,128)(2,1)} async-done(((bf16[2,128,3840]{2,1,0:T(8,128)(2,1)}), bf16[2,1024,3840]{2,1,0:T(8,128)(2,1)}) %all-gather.7.cloned.1.call-update) | async-done | bytes 15728656 | tf_op jit(solution)/shard_map/all_gather | solution.py:80
  338.1 41.1 %fusion.59 = bf16[2,1024,1920]{2,1,0:T(8,128)(2,1)} fusion(bf16[2,1024,3840]{2,1,0:T(8,128)(2,1)} %all-gather.7.cloned.1.call-done, bf16[3840,1920]{1,0:T(8,128)(2,1)} %param.18), kind=kOutput, calls=%fused_computation.84 | convolution fusion | flops 30202920960 | bytes 38338560 | tf_op jit(solution)/shard_map/bsd,df->bsf/dot_general | solution.py:81
  379.2 38.3 %fusion.62 = bf16[2,1024,1920]{2,1,0:T(8,128)(2,1)} fusion(bf16[2,1024,3840]{2,1,0:T(8,128)(2,1)S(1)} %copy-done.52, bf16[3840,1920]{1,0:T(8,128)(2,1)} %param.19), kind=kOutput, calls=%fused_computation.85 | convolution fusion | flops 30202920960 | bytes 38338560 | tf_op jit(solution)/shard_map/bsd,df->bsf/dot_general | solution.py:82
  417.5 45.8 %fusion.42 = bf16[2,1024,3840]{2,1,0:T(8,128)(2,1)} fusion(bf16[1920,3840]{1,0:T(8,128)(2,1)} %param.20, bf16[2,1024,1920]{2,1,0:T(8,128)(2,1)} %fusion.62, bf16[2,1024,1920]{2,1,0:T(8,128)(2,1)} %fusion.59), kind=kOutput, calls=%fused_computation.61 | convolution fusion | flops 30254039040 | bytes 46202880 | tf_op jit(solution)/shard_map/bsf,fd->bsd/dot_general | solution.py:84
  463.5 40.9 %fusion.65 = bf16[2,1024,1920]{2,1,0:T(8,128)(2,1)} fusion(bf16[2,1024,3840]{2,1,0:T(8,128)(2,1)} %all-gather.9.cloned.1.call-done, bf16[1920,3840]{1,0:T(8,128)(2,1)} %param.20), kind=kOutput, calls=%fused_computation.86 | convolution fusion | flops 30202920960 | bytes 38338560 | tf_op jit(solution)/shard_map/bsd,fd->bsf/dot_general | solution.py:89
  504.4 46.6 %fusion.34 = f32[2,1024,3840]{2,1,0:T(8,128)} fusion(bf16[3840,1920]{1,0:T(8,128)(2,1)} %param.19, bf16[2,1024,1920]{2,1,0:T(8,128)(2,1)} %fusion.65, bf16[2,1024,1920]{2,1,0:T(8,128)(2,1)} %fusion.59), kind=kOutput, calls=%fused_computation.53 | convolution fusion | flops 30246174720 | bytes 61931520 | tf_op jit(solution)/shard_map/bsf,df->bsd/dot_general | solution.py:93
  551.0 59.9 %add_convert_fusion = bf16[2,1024,3840]{2,1,0:T(8,128)(2,1)} fusion(f32[2,1024,3840]{2,1,0:T(8,128)} %fusion.34, bf16[3840,1920]{1,0:T(8,128)(2,1)} %param.18, bf16[2,1024,1920]{2,1,0:T(8,128)(2,1)} %fusion.59, bf16[2,1024,1920]{2,1,0:T(8,128)(2,1)} %fusion.62, bf16[2,1024,1920]{2,1,0:T(8,128)(2,1)} %fusion.65), kind=kOutput, calls=%fused_computation.4 | convolution fusion | flops 30309089280 | bytes 85524480 | tf_op jit(solution)/shard_map/bsf,df->bsd/dot_general | solution.py:92
  611.1 83.8 %reduce-scatter.9.cloned.1.call-done = bf16[2,128,3840]{2,1,0:T(8,128)(2,1)} async-done(((bf16[2,1024,3840]{2,1,0:T(8,128)(2,1)}), bf16[2,128,3840]{2,1,0:T(8,128)(2,1)}) %reduce-scatter.9.cloned.1.call-update) | async-done | bytes 1966096 | tf_op jit(solution)/shard_map/reduce_scatter | solution.py:96
  695.0 6.6 fusion.79
  701.6 2.7 fusion.100
  704.4 0.1 reduce-scatter.11.cloned.1.call-start
  704.5 76.3 %all-gather.11.cloned.1.call-done = bf16[2,1024,3840]{2,1,0:T(8,128)(2,1)} async-done(((bf16[2,128,3840]{2,1,0:T(8,128)(2,1)}), bf16[2,1024,3840]{2,1,0:T(8,128)(2,1)}) %all-gather.11.cloned.1.call-update) | async-done | bytes 15728656 | tf_op jit(solution)/shard_map/all_gather | solution.py:99
  780.9 13.0 %fusion.110 = bf16[2,1024,2,256]{3,1,2,0:T(8,128)(2,1)S(1)} fusion(bf16[2,256,3840]{2,1,0:T(8,128)(2,1)} %param.17, bf16[2,1024,3840]{2,1,0:T(8,128)(2,1)} %all-gather.11.cloned.1.call-done), kind=kOutput, calls=%fused_computation.144 | convolution fusion | flops 8054112256 | bytes 21757952 | tf_op jit(solution)/shard_map/bsd,nhd->bsnh/dot_general | solution.py:100
  794.0 9.9 fusion.151
  803.8 11.2 fusion.10
  815.1 13.0 %fusion.159 = f32[2,1024,1,256]{1,3,0,2:T(8,128)} fusion(bf16[2,2,1024,1024]{2,3,1,0:T(8,128)(2,1)} %get-tuple-element.44, f32[2,2,1024]{2,1,0:T(2,128)S(1)} %neg.13, f32[2,2,1024]{2,1,0:T(2,128)S(1)} %copy-done.38, pred[1024,1024]{0,1:T(8,128)(4,1)S(1)} %copy-done.16, f32[2,1024,2,128]{1,3,2,0:T(8,128)} %copy-done.19, ...), kind=kOutput, calls=%fused_computation.165 | convolution fusion | flops 2181038080 | bytes 32555008 | tf_op jit(solution)/shard_map/transpose(jvp(bqkgh,bskh->bkgqs))/dot_general | solution.py:36
  828.1 11.6 %convert_multiply_fusion.20 = f32[2,1024,2,256]{1,3,2,0:T(8,128)S(1)} fusion(bf16[2,2,1024,1024]{2,3,1,0:T(8,128)(2,1)} %get-tuple-element.44, f32[2,2,1024]{2,1,0:T(2,128)S(1)} %neg.13, f32[2,2,1024]{2,1,0:T(2,128)S(1)} %copy-done.38, pred[1024,1024]{0,1:T(8,128)(4,1)S(1)} %copy-done.16, bf16[2,1024,128]{1,2,0:T(8,128)(2,1)S(1)} %copy-done.29, ...), kind=kOutput, calls=%fused_computation.103 | convolution fusion | flops 2182086656 | bytes 31506432 | tf_op jit(solution)/shard_map/transpose(jvp(bqkgh,bskh->bkgqs))/dot_general | solution.py:36
  839.7 2.1 multiply_add_fusion.1
  841.8 4.2 fusion.166
  846.1 17.7 %fusion.89 = f32[2,1024,3840,1]{2,1,3,0:T(8,128)} fusion(bf16[3840,2,256]{2,1,0:T(2,128)(2,1)} %param.14, f32[2,1024,2,128]{1,3,2,0:T(8,128)} %get-tuple-element.31, f32[2,1024,2,128]{1,3,2,0:T(8,128)S(1)} %get-tuple-element.30), kind=kOutput, calls=%fused_computation.117 | convolution fusion | flops 8055160832 | bytes 39583744 | tf_op jit(solution)/shard_map/bsnh,dnh->bsd/dot_general | solution.py:103
  863.9 12.5 %fusion.101 = f32[2,1024,3840]{2,1,0:T(8,128)} fusion(bf16[3840,1,256]{2,0,1:T(8,128)(2,1)S(1)} %copy-done, f32[2,1024,1,128]{1,3,0,2:T(8,128)S(1)} %get-tuple-element.35, f32[2,1024,1,128]{1,3,0,2:T(8,128)S(1)} %get-tuple-element.34), kind=kOutput, calls=%fused_computation.137 | convolution fusion | flops 4027580416 | bytes 35520512 | tf_op jit(solution)/shard_map/bsnh,dnh->bsd/dot_general | solution.py:104
  876.4 27.5 %fusion.1 = bf16[2,1024,3840]{2,1,0:T(8,128)(2,1)} fusion(f32[2,1024,3840]{2,1,0:T(8,128)} %fusion.101, f32[2,1024,3840,1]{2,1,3,0:T(8,128)} %fusion.89, bf16[2,1024,256]{1,2,0:T(8,128)(2,1)S(1)} %copy-done.24, bf16[3840,1,256]{2,0,1:T(8,128)(2,1)} %param.16), kind=kOutput, calls=%fused_computation.2 | convolution fusion | flops 4050124800 | bytes 81657856 | tf_op jit(solution)/shard_map/bsnh,dnh->bsd/dot_general | solution.py:105
  903.9 41.9 %bitcast_convert_fusion.1 = bf16[1920,3840]{1,0:T(8,128)(2,1)} fusion(bf16[2,1024,3840]{2,1,0:T(8,128)(2,1)} %all-gather.9.cloned.1.call-done, bf16[2,1024,1920]{2,1,0:T(8,128)(2,1)} %fusion.62, bf16[2,1024,1920]{2,1,0:T(8,128)(2,1)} %fusion.59), kind=kOutput, calls=%fused_computation.10 | convolution fusion | flops 30253547520 | bytes 46202880 | tf_op jit(solution)/shard_map/bsf,bsd->fd/dot_general | solution.py:90
  945.8 43.2 %bitcast_convert_fusion.2 = bf16[3840,1920]{1,0:T(8,128)(2,1)} fusion(bf16[2,1024,3840]{2,1,0:T(8,128)(2,1)} %all-gather.7.cloned.1.call-done, bf16[2,1024,1920]{2,1,0:T(8,128)(2,1)} %fusion.65, bf16[2,1024,1920]{2,1,0:T(8,128)(2,1)} %fusion.59), kind=kOutput, calls=%fused_computation.11 | convolution fusion | flops 30253547520 | bytes 46202880 | tf_op jit(solution)/shard_map/bsd,bsf->df/dot_general | solution.py:95
  989.0 44.8 %bitcast_convert_fusion.3 = bf16[3840,1920]{1,0:T(8,128)(2,1)} fusion(bf16[2,1024,3840]{2,1,0:T(8,128)(2,1)} %all-gather.7.cloned.1.call-done, bf16[2,1024,1920]{2,1,0:T(8,128)(2,1)} %fusion.59, bf16[2,1024,1920]{2,1,0:T(8,128)(2,1)} %fusion.62, bf16[2,1024,1920]{2,1,0:T(8,128)(2,1)} %fusion.65), kind=kOutput, calls=%fused_computation.12 | convolution fusion | flops 30300733440 | bytes 54067200 | tf_op jit(solution)/shard_map/bsd,bsf->df/dot_general | solution.py:94
  1033.8 12.3 %bitcast_convert_fusion.4 = bf16[3840,2,256]{2,0,1:T(8,128)(2,1)S(1)} fusion(bf16[2,1024,3840]{2,1,0:T(8,128)(2,1)} %all-gather.5.cloned.1.call-done, f32[2,1024,2,128]{1,3,2,0:T(8,128)S(1)} %copy-done.22, f32[2,1024,2,128]{1,3,2,0:T(8,128)S(1)} %copy-done.21), kind=kOutput, calls=%fused_computation.66 | convolution fusion | flops 8057126912 | bytes 23855104 | tf_op jit(solution)/shard_map/bsd,bsnh->dnh/dot_general | solution.py:106
  1046.1 25.6 %copy.52 = bf16[3840,2,256]{2,1,0:T(2,128)(2,1)} copy(bf16[3840,2,256]{2,0,1:T(8,128)(2,1)S(1)} %bitcast_convert_fusion.4) | data formatting | bytes 7864320
  1071.8 9.4 fusion.70
  1081.2 9.6 fusion.71
  1090.9 10.3 bitcast_convert_fusion.5
  1101.3 4.4 fusion.80
  1105.7 25.1 %all-reduce.4 = (f32[3840]{0:T(1024)}, f32[3840]{0:T(1024)}) all-reduce(f32[3840]{0:T(1024)S(1)} %get-tuple-element.24, f32[3840]{0:T(1024)S(1)} %copy-done.36), channel_id=1, replica_groups=mesh['dp'=2,'tp'=8] {'tp'}, use_global_device_ids=true, to_apply=%region_12.13 | all-reduce | flops 7680 | bytes 61440 | tf_op jit(solution)/shard_map/psum | solution.py:113
  1130.7 5.4 fusion.99
  (138 shorter events, 1.1 us)
Async XLA Ops:
  7.2 87.2 %copy-start = (bf16[3840,1,256]{2,0,1:T(8,128)(2,1)S(1)}, bf16[3840,1,256]{2,0,1:T(8,128)(2,1)}, u32[]{:S(2)}) copy-start(bf16[3840,1,256]{2,0,1:T(8,128)(2,1)} %param.15) | copy-start | bytes 5898244
  7.2 87.2 %all-gather.5.cloned.1.call-start = ((), (), s32[]{:S(2)}) async-start(), calls=%async_computation.4 | async-start | bytes 17694720 | tf_op jit(solution)/shard_map/all_gather | solution.py:71
  10.0 0.7 copy-start.39
  14.8 240.8 %reduce-scatter.5.cloned.1.call-start = ((), (), s32[]{:S(2)}) async-start(), calls=%async_computation.5 | async-start | bytes 17694720 | tf_op jit(solution)/shard_map/reduce_scatter | solution.py:77
  15.5 88.2 %copy-start.34 = (f32[2,1024]{1,0:T(2,128)}, f32[2,1024]{1,0:T(2,128)S(1)}, u32[]{:S(2)}) copy-start(f32[2,1024]{1,0:T(2,128)S(1)} %convert_element_type.200) | copy-start | bytes 24580
  26.0 77.8 %copy-start.50 = (f32[128]{0:T(128)}, f32[128]{0:T(128)S(1)}, u32[]{:S(2)}) copy-start(f32[128]{0:T(128)S(1)} %multiply_power_fusion) | copy-start | bytes 1540
  31.9 90.5 %copy-start.4 = (f32[2,1024,128]{1,2,0:T(8,128)}, f32[2,1024,128]{1,2,0:T(8,128)S(1)}, u32[]{:S(2)}) copy-start(f32[2,1024,128]{1,2,0:T(8,128)S(1)} %get-tuple-element.39) | copy-start | bytes 3145732
  109.1 14.2 %copy-start.26 = (bf16[2,1024,128]{1,2,0:T(8,128)(2,1)}, bf16[2,1024,128]{1,2,0:T(8,128)(2,1)S(1)}, u32[]{:S(2)}) copy-start(bf16[2,1024,128]{1,2,0:T(8,128)(2,1)S(1)} %get-tuple-element.36) | copy-start | bytes 1572868
  109.1 14.2 %copy-start.28 = (bf16[2,1024,128]{1,2,0:T(8,128)(2,1)}, bf16[2,1024,128]{1,2,0:T(8,128)(2,1)S(1)}, u32[]{:S(2)}) copy-start(bf16[2,1024,128]{1,2,0:T(8,128)(2,1)S(1)} %get-tuple-element.37) | copy-start | bytes 1572868
  109.1 13.3 %copy-start.6 = (f32[2,1024,128]{1,2,0:T(8,128)S(1)}, f32[2,1024,128]{1,2,0:T(8,128)}, u32[]{:S(2)}) copy-start(f32[2,1024,128]{1,2,0:T(8,128)} %get-tuple-element.40) | copy-start | bytes 3145732
  122.4 1.2 copy-start.14
  123.2 8.2 copy-start.17
  123.2 8.2 copy-start.19
  123.6 7.8 copy-start.15
  131.4 19.3 %copy-start.44 = (f32[2,2,1024]{2,1,0:T(2,128)}, f32[2,2,1024]{2,1,0:T(2,128)S(1)}, u32[]{:S(2)}) copy-start(f32[2,2,1024]{2,1,0:T(2,128)S(1)} %get-tuple-element.41) | copy-start | bytes 49156
  140.2 10.5 copy-start.37
  140.2 10.8 copy-start.3
  151.1 5.3 copy-start.53
  156.4 1.3 copy-start.55
  171.6 166.6 %all-gather.7.cloned.1.call-start = ((), (), s32[]{:S(2)}) async-start(), calls=%async_computation.6 | async-start | bytes 17694720 | tf_op jit(solution)/shard_map/all_gather | solution.py:80
  172.2 207.0 %copy-start.32 = (f32[3840]{0:T(1024)}, f32[3840]{0:T(1024)S(1)}, u32[]{:S(2)}) copy-start(f32[3840]{0:T(1024)S(1)} %broadcast_add_fusion) | copy-start | bytes 46084
  258.5 1.3 copy-start.1
  261.7 201.9 %all-gather.9.cloned.1.call-start = ((), (), s32[]{:S(2)}) async-start(), calls=%async_computation.8 | async-start | bytes 17694720 | tf_op jit(solution)/shard_map/all_gather | solution.py:88
  262.3 348.8 %reduce-scatter.7.cloned.1.call-start = ((), (), s32[]{:S(2)}) async-start(), calls=%async_computation.7 | async-start | bytes 17694720 | tf_op jit(solution)/shard_map/reduce_scatter | solution.py:85
  338.1 41.1 %copy-start.52 = (bf16[2,1024,3840]{2,1,0:T(8,128)(2,1)S(1)}, bf16[2,1024,3840]{2,1,0:T(8,128)(2,1)}, u32[]{:S(2)}) copy-start(bf16[2,1024,3840]{2,1,0:T(8,128)(2,1)} %all-gather.7.cloned.1.call-done) | copy-start | bytes 47185924
  463.4 231.5 %reduce-scatter.9.cloned.1.call-start = ((), (), s32[]{:S(2)}) async-start(), calls=%async_computation.9 | async-start | bytes 17694720 | tf_op jit(solution)/shard_map/reduce_scatter | solution.py:96
  610.9 84.0 %copy-start.33 = (f32[3840]{0:T(1024)S(1)}, f32[3840]{0:T(1024)}, u32[]{:S(2)}) copy-start(f32[3840]{0:T(1024)} %copy-done.32) | copy-start | bytes 46084
  610.9 84.0 %copy-start.42 = (f32[2,128]{1,0:T(2,128)S(1)}, f32[2,128]{1,0:T(2,128)}, u32[]{:S(2)}) copy-start(f32[2,128]{1,0:T(2,128)} %copy-done.41) | copy-start | bytes 3076
  610.9 90.6 %copy-start.49 = (f32[2,128]{1,0:T(2,128)S(1)}, f32[2,128]{1,0:T(2,128)}, u32[]{:S(2)}) copy-start(f32[2,128]{1,0:T(2,128)} %copy-done.48) | copy-start | bytes 3076
  611.0 93.5 %copy-start.38 = (f32[2,2,1024]{2,1,0:T(2,128)S(1)}, f32[2,2,1024]{2,1,0:T(2,128)}, u32[]{:S(2)}) copy-start(f32[2,2,1024]{2,1,0:T(2,128)} %copy-done.37) | copy-start | bytes 49156
  611.0 169.9 %all-gather.11.cloned.1.call-start = ((), (), s32[]{:S(2)}) async-start(), calls=%async_computation.10 | async-start | bytes 17694720 | tf_op jit(solution)/shard_map/all_gather | solution.py:99
  695.0 6.6 copy-start.2
  695.0 6.6 copy-start.8
  695.0 6.6 copy-start.9
  704.4 396.9 %reduce-scatter.11.cloned.1.call-start = ((), (), s32[]{:S(2)}) async-start(), calls=%async_computation.11 | async-start | bytes 17694720 | tf_op jit(solution)/shard_map/reduce_scatter | solution.py:109
  704.5 89.4 %copy-start.16 = (pred[1024,1024]{0,1:T(8,128)(4,1)S(1)}, pred[1024,1024]{0,1:T(8,128)(4,1)}, u32[]{:S(2)}) copy-start(pred[1024,1024]{0,1:T(8,128)(4,1)} %iota_compare_fusion) | copy-start | bytes 3145732
  704.5 89.4 %copy-start.45 = (f32[2,2,1024]{2,1,0:T(2,128)S(1)}, f32[2,2,1024]{2,1,0:T(2,128)}, u32[]{:S(2)}) copy-start(f32[2,2,1024]{2,1,0:T(2,128)} %copy-done.44) | copy-start | bytes 49156
  793.9 9.9 copy-start.54
  803.8 11.2 copy-start.18
  815.0 13.1 %copy-start.27 = (bf16[2,1024,128]{1,2,0:T(8,128)(2,1)S(1)}, bf16[2,1024,128]{1,2,0:T(8,128)(2,1)}, u32[]{:S(2)}) copy-start(bf16[2,1024,128]{1,2,0:T(8,128)(2,1)} %copy-done.26) | copy-start | bytes 1572868
  815.0 13.0 %copy-start.29 = (bf16[2,1024,128]{1,2,0:T(8,128)(2,1)S(1)}, bf16[2,1024,128]{1,2,0:T(8,128)(2,1)}, u32[]{:S(2)}) copy-start(bf16[2,1024,128]{1,2,0:T(8,128)(2,1)} %copy-done.28) | copy-start | bytes 1572868
  828.1 11.6 %copy-start.5 = (f32[2,1024,128]{1,2,0:T(8,128)S(1)}, f32[2,1024,128]{1,2,0:T(8,128)}, u32[]{:S(2)}) copy-start(f32[2,1024,128]{1,2,0:T(8,128)} %copy-done.4) | copy-start | bytes 3145732
  828.1 11.6 %copy-start.7 = (f32[2,1024,128]{1,2,0:T(8,128)S(1)}, f32[2,1024,128]{1,2,0:T(8,128)}, u32[]{:S(2)}) copy-start(f32[2,1024,128]{1,2,0:T(8,128)} %get-tuple-element.40) | copy-start | bytes 3145732
  839.7 2.1 copy-start.23
  839.7 2.1 copy-start.35
  839.7 2.1 copy-start.51
  841.8 22.0 %copy-start.20 = (f32[2,1024,2,128]{1,3,2,0:T(8,128)}, f32[2,1024,2,128]{1,3,2,0:T(8,128)S(1)}, u32[]{:S(2)}) copy-start(f32[2,1024,2,128]{1,3,2,0:T(8,128)S(1)} %get-tuple-element.30) | copy-start | bytes 6291460
  846.1 17.7 %copy-start.10 = (f32[2,1024,1,128]{1,3,0,2:T(8,128)}, f32[2,1024,1,128]{1,3,0,2:T(8,128)S(1)}, u32[]{:S(2)}) copy-start(f32[2,1024,1,128]{1,3,0,2:T(8,128)S(1)} %get-tuple-element.34) | copy-start | bytes 3145732
  846.1 17.7 %copy-start.12 = (f32[2,1024,1,128]{1,3,0,2:T(8,128)}, f32[2,1024,1,128]{1,3,0,2:T(8,128)S(1)}, u32[]{:S(2)}) copy-start(f32[2,1024,1,128]{1,3,0,2:T(8,128)S(1)} %get-tuple-element.35) | copy-start | bytes 3145732
  863.8 12.5 %copy-start.24 = (bf16[2,1024,256]{1,2,0:T(8,128)(2,1)S(1)}, bf16[2,1024,256]{1,2,0:T(8,128)(2,1)}, u32[]{:S(2)}) copy-start(bf16[2,1024,256]{1,2,0:T(8,128)(2,1)} %fusion.151) | copy-start | bytes 3145732
  989.0 44.8 %copy-start.21 = (f32[2,1024,2,128]{1,3,2,0:T(8,128)S(1)}, f32[2,1024,2,128]{1,3,2,0:T(8,128)}, u32[]{:S(2)}) copy-start(f32[2,1024,2,128]{1,3,2,0:T(8,128)} %copy-done.20) | copy-start | bytes 6291460
  989.0 44.8 %copy-start.22 = (f32[2,1024,2,128]{1,3,2,0:T(8,128)S(1)}, f32[2,1024,2,128]{1,3,2,0:T(8,128)}, u32[]{:S(2)}) copy-start(f32[2,1024,2,128]{1,3,2,0:T(8,128)} %get-tuple-element.31) | copy-start | bytes 6291460
  1033.8 37.9 %copy-start.25 = (bf16[2,1024,256]{1,2,0:T(8,128)(2,1)S(1)}, bf16[2,1024,256]{1,2,0:T(8,128)(2,1)}, u32[]{:S(2)}) copy-start(bf16[2,1024,256]{1,2,0:T(8,128)(2,1)} %fusion.151) | copy-start | bytes 3145732
  1071.7 9.4 copy-start.11
  1071.7 9.4 copy-start.13
  1071.7 19.1 %slice-start = ((s8[15728640]{0:T(1024)(128)(4,1)}), s8[3145728]{0:T(1024)(128)(4,1)S(1)}, s32[]{:S(2)}) async-start(s8[15728640]{0:T(1024)(128)(4,1)} %bitcast.293), calls=%async_computation.12 | async-start | bytes 6291456
  1071.8 19.1 %slice-start.1 = ((s8[15728640]{0:T(1024)(128)(4,1)}), s8[4194304]{0:T(1024)(128)(4,1)S(1)}, s32[]{:S(2)}) async-start(s8[15728640]{0:T(1024)(128)(4,1)} %bitcast.293), calls=%async_computation.13 | async-start | bytes 8388608
  1081.2 9.7 slice-start.2
  1081.2 9.7 slice-start.3
  1081.2 9.7 copy-start.56
  1090.9 10.4 copy-start.31
  1090.9 10.4 copy-start.40
  1090.9 14.7 %copy-start.47 = (f32[2,128]{1,0:T(2,128)S(1)}, f32[2,128]{1,0:T(2,128)}, u32[]{:S(2)}) copy-start(f32[2,128]{1,0:T(2,128)} %copy-done.46) | copy-start | bytes 3076
  1090.9 14.7 %copy-start.36 = (f32[3840]{0:T(1024)S(1)}, f32[3840]{0:T(1024)}, u32[]{:S(2)}) copy-start(f32[3840]{0:T(1024)} %get-tuple-element.22) | copy-start | bytes 46084
  (5 other events, 3.2 us)
Sparse Core Ops, SparseCore 0:
  14.9 79.4 all-gather.4
  171.7 83.7 reduce-scatter.4
  261.8 76.3 all-gather.6
  339.6 77.1 all-gather.8
  463.6 83.7 reduce-scatter.6
  611.1 83.7 reduce-scatter.8
  704.5 76.3 all-gather.10
  904.1 83.7 reduce-scatter.10
where the time goes:
time: 1150 us; the launch traced here: 1140 us
  matrix products  621 us (54%)
  waiting for transfers between devices  383 us (33%)
  other arithmetic  58 us (5%)
  local copies, waits for them, and re-layouts  41.3 us (4%)
  blocking collectives  25.1 us (2%)
  between operations  15.3 us (1%)
    reduce_scatter x1, waiting for transfers between devices, local_step(): lax.psum_scatter(d_mlp_part, 'tp', scatter_dimension=1, tiled=True)  83.8 us
    reduce_scatter x1, waiting for transfers between devices, local_step(): lax.psum_scatter(attn_part, 'tp', scatter_dimension=1, tiled=True)  83.3 us
    all_gather x1, waiting for transfers between devices, local_step(): d_hidden_all = lax.all_gather(d_hidden, 'tp', axis=1, tiled=True)  76.3 us
    all_gather x1, waiting for transfers between devices, local_step(): mlp_all = lax.all_gather(mlp_in, 'tp', axis=1, tiled=True)  75.8 us
    all_gather x1, waiting for transfers between devices, local_step(): normed_all = lax.all_gather(normed, 'tp', axis=1, tiled=True)  62.5 us
    dot_general x1, matrix products, local_step(): jnp.einsum('bsf,df->bsd', d_gate, w_gate, preferred_element_type=jnp.floa...  59.9 us
    dot_general x1, matrix products, local_step(): jnp.einsum('bsf,df->bsd', d_up, w_up, preferred_element_type=jnp.float32)  46.6 us
    dot_general x1, matrix products, local_step(): jnp.einsum('bsf,fd->bsd', act_out, w_down, preferred_element_type=jnp.flo...  45.8 us
  transfers between devices with their start and end apart: 8, of which 5 were waited for; matrix products, arithmetic and copies ran while one was open for 43% of the time, Pallas kernels for 0%

commit v1 on v0

v1 whole, which is shorter than its diff:
```python
import functools

import jax
import jax.numpy as jnp
from jax import lax
from jax.experimental import pallas as pl
from jax.experimental.pallas import tpu as pltpu
from jax.sharding import PartitionSpec as P

EPS = 1e-6
ROPE_THETA = 10000.0
BF = jnp.bfloat16
F32 = jnp.float32
GELU_C = 0.7978845608028654
GELU_A = 0.044715
VMEM_LIMIT = 60 * 1024 * 1024

NN = (((1,), (0,)), ((), ()))
NT = (((1,), (1,)), ((), ()))
TN = (((0,), (0,)), ((), ()))


def rms_norm(vals, gain):
    vals_f32 = vals.astype(F32)
    inv_rms = lax.rsqrt(jnp.mean(vals_f32 * vals_f32, axis=-1, keepdims=True) + EPS)
    return (vals_f32 * inv_rms * (1.0 + gain)).astype(BF)


def rope_tables(positions, head_dim):
    half_dim = head_dim // 2
    inv_freq = ROPE_THETA ** (-2.0 * jnp.arange(half_dim, dtype=F32) / head_dim)
    angles = positions.astype(F32)[:, :, None] * inv_freq
    return jnp.cos(angles), jnp.sin(angles)


def dot(lhs, rhs, dims):
    return lax.dot_general(lhs, rhs, dims, preferred_element_type=F32)


def after(value, *deps):
    return lax.optimization_barrier((value,) + deps)[0]


def join(parts, axis):
    return parts[0] if len(parts) == 1 else jnp.concatenate(parts, axis=axis)


def call(body, grid, in_specs, out_specs, out_shape, flops, nbytes, name, scratch=()):
    return pl.pallas_call(
        body,
        grid=grid,
        in_specs=in_specs,
        out_specs=out_specs,
        out_shape=out_shape,
        scratch_shapes=scratch,
        compiler_params=pltpu.CompilerParams(vmem_limit_bytes=VMEM_LIMIT),
        cost_estimate=pl.CostEstimate(flops=int(flops), bytes_accessed=int(nbytes), transcendentals=0),
        name=name,
    )


def whole(arr):
    zeros = (0,) * arr.ndim
    return pl.BlockSpec(arr.shape, lambda *_: zeros, pipeline_mode=pl.Buffered(1))


def rows_times_weights(acts, weights, kind, tile, name, m_tile=256):
    n_rows = acts[0].shape[0]
    nt = kind == "nt"
    n_cols = weights[0].shape[0 if nt else 1]
    depth = sum(a.shape[1] for a in acts)
    n_in = len(acts)
    grid = (pl.cdiv(n_cols, tile),)

    def body(*refs):
        a_refs, w_refs, out = refs[:n_in], refs[n_in:-1], refs[-1]
        rhs = join([w[...] for w in w_refs], 1 if nt else 0)
        for start in range(0, n_rows, m_tile):
            rows = pl.ds(start, m_tile)
            lhs = join([a[rows, :] for a in a_refs], 1)
            out[rows, :] = dot(lhs, rhs, NT if nt else NN).astype(BF)

    if nt:
        w_specs = [pl.BlockSpec((tile, w.shape[1]), lambda i: (i, 0)) for w in weights]
    else:
        w_specs = [pl.BlockSpec((w.shape[0], tile), lambda i: (0, i)) for w in weights]
    return call(
        body, grid, [whole(a) for a in acts] + w_specs,
        pl.BlockSpec((n_rows, tile), lambda i: (0, i)),
        jax.ShapeDtypeStruct((n_rows, n_cols), BF),
        2 * n_rows * depth * n_cols, 2 * (n_rows * depth + depth * n_cols + n_rows * n_cols), name,
    )(*acts, *weights)


def qkv_proj(acts, w_q, w_k, w_v):
    n_rows, depth = acts.shape
    m_tile = 256
    widths = (w_q.shape[1], w_k.shape[1], w_v.shape[1])

    def body(a_ref, wq, wk, wv, q, k, v):
        lhs = a_ref[...]
        q[...] = dot(lhs, wq[...], NN).astype(BF)
        kv = dot(lhs, jnp.concatenate([wk[...], wv[...]], axis=1), NN).astype(BF)
        k[...] = kv[:, : widths[1]]
        v[...] = kv[:, widths[1]:]

    return call(
        body, (n_rows // m_tile,),
        [pl.BlockSpec((m_tile, depth), lambda i: (i, 0)), whole(w_q), whole(w_k), whole(w_v)],
        [pl.BlockSpec((m_tile, w), lambda i: (i, 0)) for w in widths],
        [jax.ShapeDtypeStruct((n_rows, w), BF) for w in widths],
        2 * n_rows * depth * sum(widths), 2 * (n_rows * depth + depth * sum(widths) + n_rows * sum(widths)), "qkv",
    )(acts, w_q, w_k, w_v)


def rotate(vals, cos_t, sin_t):
    half = cos_t.shape[1]
    first, second = vals[:, :half].astype(F32), vals[:, half:].astype(F32)
    return jnp.concatenate([first * cos_t - second * sin_t, second * cos_t + first * sin_t], axis=1)


def unrotate(vals, cos_t, sin_t):
    half = cos_t.shape[1]
    first, second = vals[:, :half], vals[:, half:]
    return jnp.concatenate([first * cos_t + second * sin_t, second * cos_t - first * sin_t], axis=1)


def causal_probs(q_rows, k_rot, start, tile, n_rep):
    end = start + tile
    scores = dot(q_rows, k_rot[:end], NT)
    row = lax.broadcasted_iota(jnp.int32, (n_rep * tile, end), 0)
    col = lax.broadcasted_iota(jnp.int32, (n_rep * tile, end), 1)
    scores = jnp.where(lax.rem(row, tile) + start >= col, scores, -1e30)
    probs = jnp.exp(scores - jnp.max(scores, axis=1, keepdims=True))
    return probs / jnp.sum(probs, axis=1, keepdims=True)


def attention_fwd(q_raw, k_raw, v_raw, cos_t, sin_t, scale):
    n_rows, head = k_raw.shape
    n_rep = q_raw.shape[1] // head
    tile = 256

    def body(q, k, v, cos_ref, sin_ref, out, q_rot, k_rot):
        k_rot[...] = rotate(k[...], cos_ref[...], sin_ref[...]).astype(BF)
        for h in range(n_rep):
            cols = pl.ds(h * head, head)
            q_rot[:, cols] = (rotate(q[:, cols], cos_ref[...], sin_ref[...]) * scale).astype(BF)
        for start in range(0, n_rows, tile):
            rows = pl.ds(start, tile)
            q_rows = join([q_rot[rows, pl.ds(h * head, head)] for h in range(n_rep)], 0)
            probs = causal_probs(q_rows, k_rot, start, tile, n_rep).astype(BF)
            mixed = dot(probs, v[: start + tile], NN).astype(BF)
            for h in range(n_rep):
                out[rows, pl.ds(h * head, head)] = mixed[h * tile:(h + 1) * tile]

    ins = (q_raw, k_raw, v_raw, cos_t, sin_t)
    outs = [jax.ShapeDtypeStruct(a.shape, BF) for a in (q_raw, q_raw, k_raw)]
    return call(
        body, (1,), [whole(a) for a in ins], [whole(a) for a in outs], outs,
        4e9, 8e6, "attn_fwd",
    )(*ins)


def attention_bwd(q_rot, k_rot, v_raw, d_out, cos_t, sin_t, scale):
    n_rows, head = k_rot.shape
    n_rep = q_rot.shape[1] // head
    tile = 256

    def body(q, k, v, d_o, cos_ref, sin_ref, d_q, d_k, d_v, dk_acc, dv_acc):
        for start in reversed(range(0, n_rows, tile)):
            end = start + tile
            rows = pl.ds(start, tile)
            q_rows = join([q[rows, pl.ds(h * head, head)] for h in range(n_rep)], 0)
            do_rows = join([d_o[rows, pl.ds(h * head, head)] for h in range(n_rep)], 0)
            probs = causal_probs(q_rows, k, start, tile, n_rep)
            d_probs = dot(do_rows, v[:end], NT)
            d_scores = (probs * (d_probs - jnp.sum(d_probs * probs, axis=1, keepdims=True))).astype(BF)
            dv_part = dot(probs.astype(BF), do_rows, TN)
            dk_part = dot(d_scores, q_rows, TN)
            if end == n_rows:
                dv_acc[...] = dv_part
                dk_acc[...] = dk_part
            else:
                dv_acc[:end] += dv_part
                dk_acc[:end] += dk_part
            dq_rows = dot(d_scores, k[:end], NN).astype(BF).astype(F32) * scale
            for h in range(n_rep):
                part = dq_rows[h * tile:(h + 1) * tile]
                d_q[rows, pl.ds(h * head, head)] = unrotate(part, cos_ref[rows, :], sin_ref[rows, :]).astype(BF)
        d_v[...] = dv_acc[...].astype(BF)
        d_k[...] = unrotate(dk_acc[...].astype(BF).astype(F32), cos_ref[...], sin_ref[...]).astype(BF)

    ins = (q_rot, k_rot, v_raw, d_out, cos_t, sin_t)
    outs = [jax.ShapeDtypeStruct(a.shape, BF) for a in (q_rot, k_rot, v_raw)]
    return call(
        body, (1,), [whole(a) for a in ins], [whole(a) for a in outs], outs,
        8e9, 8e6, "attn_bwd", [pltpu.VMEM((n_rows, head), F32)] * 2,
    )(*ins)


def gated_mlp(acts, w_gate, w_up, d_act):
    n_rows, depth = acts.shape
    width = w_gate.shape[1]
    tile, m_tile = 384, 256

    def body(a_ref, wg, wu, dz_ref, z_ref, dg_ref, du_ref):
        rhs = jnp.concatenate([wg[...], wu[...]], axis=1)
        for start in range(0, n_rows, m_tile):
            rows = pl.ds(start, m_tile)
            both = dot(a_ref[rows, :], rhs, NN)
            gate = both[:, :tile].astype(BF).astype(F32)
            up = both[:, tile:].astype(BF).astype(F32)
            d_z = dz_ref[rows, :].astype(F32)
            square = gate * gate
            tanh = jnp.tanh(gate * (GELU_C + (GELU_C * GELU_A) * square))
            half = 0.5 + 0.5 * tanh
            act = gate * half
            slope = half + (0.5 * gate) * (1.0 - tanh * tanh) * (GELU_C + (3.0 * GELU_C * GELU_A) * square)
            z_ref[rows, :] = (act * up).astype(BF)
            du_ref[rows, :] = (d_z * act).astype(BF)
            dg_ref[rows, :] = (d_z * up * slope).astype(BF)

    w_spec = pl.BlockSpec((depth, tile), lambda i: (0, i))
    o_spec = pl.BlockSpec((n_rows, tile), lambda i: (0, i))
    return call(
        body, (width // tile,), [whole(acts), w_spec, w_spec, o_spec], [o_spec] * 3,
        [jax.ShapeDtypeStruct((n_rows, width), BF)] * 3,
        4 * n_rows * depth * width, 2 * (n_rows * depth + 2 * depth * width + 4 * n_rows * width), "gated_mlp",
    )(acts, w_gate, w_up, d_act)


def weight_grad(lhs, rhs_groups, out_widths, tile, name, stream):
    n_seq, n_tok = len(lhs), lhs[0].shape[0]
    n_out = lhs[0].shape[1]
    rhs = [r for group in rhs_groups for r in group]
    n_groups = len(rhs_groups)

    def body(*refs):
        l_refs, r_refs, o_refs = refs[:n_seq], refs[n_seq:n_seq + n_seq * n_groups], refs[n_seq + n_seq * n_groups:]
        left = join([l[...] for l in l_refs], 0)
        right = join([join([r_refs[g * n_seq + s][...] for s in range(n_seq)], 0) for g in range(n_groups)], 1)
        acc = dot(left, right, TN)
        at = 0
        for o in o_refs:
            o[...] = acc[:, at:at + o.shape[1]].astype(BF)
            at += o.shape[1]

    if stream == "rows":
        grid = (n_out // tile,)
        l_specs = [pl.BlockSpec((n_tok, tile), lambda i: (0, i)) for _ in lhs]
        r_specs = [whole(r) for r in rhs]
        o_specs = [pl.BlockSpec((tile, w), lambda i: (i, 0)) for w in out_widths]
    else:
        grid = (out_widths[0] // tile,)
        l_specs = [whole(l) for l in lhs]
        r_specs = [pl.BlockSpec((n_tok, tile), lambda i: (0, i)) for _ in rhs]
        o_specs = [pl.BlockSpec((n_out, tile), lambda i: (0, i)) for _ in out_widths]
    total = sum(out_widths)
    return call(
        body, grid, l_specs + r_specs, o_specs,
        [jax.ShapeDtypeStruct((n_out, w), BF) for w in out_widths],
        2 * n_seq * n_tok * n_out * total, 2 * (n_seq * n_tok * (n_out + total) + n_out * total), name,
    )(*lhs, *rhs)


def tp_sum(part, n_tp):
    def body(x_ref, out_ref, slots, send_sem, recv_sem):
        me = lax.axis_index("tp")
        barrier = pltpu.get_barrier_semaphore()
        for step in range(1, n_tp):
            pl.semaphore_signal(barrier, inc=1, device_id={"tp": lax.rem(me + step, n_tp)},
                                device_id_type=pl.DeviceIdType.MESH)
        pl.semaphore_wait(barrier, n_tp - 1)
        copies = []
        for step in range(1, n_tp):
            copies.append(pltpu.make_async_remote_copy(
                src_ref=x_ref, dst_ref=slots.at[me], send_sem=send_sem.at[step], recv_sem=recv_sem.at[step],
                device_id={"tp": lax.rem(me + step, n_tp)}, device_id_type=pl.DeviceIdType.MESH))
            copies[-1].start()
        slots[me] = x_ref[...]
        for copy in copies:
            copy.wait()
        total = slots[0]
        for step in range(1, n_tp):
            total = total + slots[step]
        out_ref[...] = total

    return pl.pallas_call(
        body,
        out_shape=jax.ShapeDtypeStruct(part.shape, F32),
        in_specs=[pl.BlockSpec(memory_space=pltpu.VMEM)],
        out_specs=pl.BlockSpec(memory_space=pltpu.VMEM),
        scratch_shapes=[pltpu.VMEM((n_tp,) + part.shape, F32), pltpu.SemaphoreType.DMA((n_tp,)),
                        pltpu.SemaphoreType.DMA((n_tp,))],
        compiler_params=pltpu.CompilerParams(collective_id=0, has_side_effects=True),
        cost_estimate=pl.CostEstimate(flops=5_000_000_000, bytes_accessed=1_000_000, transcendentals=0),
        name="tp_sum",
    )(part)


def solution(mesh):
    n_tp = mesh.shape["tp"]
    act_spec = P("dp", "tp", None)
    head_spec = P(None, "tp", None)
    in_specs = (act_spec, P("dp", None), head_spec, head_spec, head_spec, P("tp", None, None),
                P(None, "tp"), P(None, "tp"), P("tp", None), P(None), P(None), act_spec)
    out_specs = (act_spec, act_spec, P("dp", "tp", None), P("dp", "tp", None), P("dp", "tp", None),
                 P(("dp", "tp"), None, None), P("dp", "tp"), P("dp", "tp"), P(("dp", "tp"), None), P("dp"), P("dp"))

    def gather(part):
        return lax.all_gather(part, "tp", axis=0, tiled=True)

    def scatter(part):
        return lax.psum_scatter(part, "tp", scatter_dimension=0, tiled=True)

    def local_step(x_in, positions, w_q, w_k, w_v, w_o, w_gate, w_up, w_down, gain_attn, gain_mlp, d_out):
        n_seq = x_in.shape[0]
        seqs = range(n_seq)
        depth, n_q, head = w_q.shape
        scale = head ** -0.5
        wq2, wk2, wv2 = (w.reshape(depth, -1) for w in (w_q, w_k, w_v))
        wo2 = w_o.reshape(-1, depth)
        cos_t, sin_t = rope_tables(positions, head)

        x = [x_in[s] for s in seqs]
        d_y = [d_out[s] for s in seqs]
        latest = []

        def run(fn, first, *rest):
            out = fn(after(first, *latest), *rest)
            latest[:] = jax.tree.leaves(out)[:1]
            return out

        def norm(vals, gain):
            return jax.vjp(rms_norm, vals, gain)

        def mid_norm(proj, vals):
            total = (vals.astype(F32) + proj.astype(F32)).astype(BF)
            return norm(total, gain_mlp) + (total,)

        def project(acts):
            return qkv_proj(acts, wq2, wk2, wv2)

        def attend(q_raw, k_raw, v_raw, s):
            return attention_fwd(q_raw, k_raw, v_raw, cos_t[s], sin_t[s], scale)

        def out_proj(acts):
            return rows_times_weights([acts], [wo2], "nn", 768, "o_proj")

        def act_grad(cot):
            return rows_times_weights([cot], [w_down], "nt", 1024, "d_act")

        def mlp_grad(d_g, d_u):
            return rows_times_weights([d_g, d_u], [w_gate, w_up], "nt", 768, "d_mlp")

        def down_proj(acts):
            return rows_times_weights([acts], [w_down], "nn", 768, "down")

        def norm_back(cot, pull, skip):
            d_vals, d_gain = pull(cot)
            return skip + d_vals, d_gain

        def attn_grads(cot, s):
            d_o = rows_times_weights([cot], [wo2], "nt", 256, "d_attn")
            grads = attention_bwd(attn[s][1], attn[s][2], qkv[s][2], d_o, cos_t[s], sin_t[s], scale)
            part = rows_times_weights(list(grads), [wq2, wk2, wv2], "nt", 768, "d_normed")
            return part, grads

        def add_out(part, vals):
            return (vals.astype(F32) + part.astype(F32)).astype(BF)

        none = [None] * n_seq
        normed_all, dout_all, qkv, attn, attn_proj, mlp_all = (list(none) for _ in range(6))
        norm_attn_pull, norm_mlp_pull, hidden, d_act, gated, d_mlp_in = (list(none) for _ in range(6))
        down_out, d_hidden, gain_mlp_part, d_hidden_all, d_qkv, d_normed = (list(none) for _ in range(6))
        grad_x, gain_attn_part, y_out = (list(none) for _ in range(3))

        for s in seqs:
            out, norm_attn_pull[s] = run(norm, x[s], gain_attn)
            normed_all[s] = gather(out)
        for s in seqs:
            qkv[s] = run(project, normed_all[s])
            attn[s] = run(attend, *qkv[s], s)
            attn_proj[s] = scatter(run(out_proj, attn[s][0]))
        dout_all[0] = gather(after(d_y[0], *latest))
        for s in seqs:
            out, norm_mlp_pull[s], hidden[s] = run(mid_norm, attn_proj[s], x[s])
            mlp_all[s] = gather(out)
        for s in seqs[1:]:
            dout_all[s] = gather(after(d_y[s], *latest))

        def mlp_half(s):
            d_act[s] = run(act_grad, dout_all[s])
            gated[s] = run(gated_mlp, mlp_all[s], w_gate, w_up, d_act[s])

        def mlp_rest(s):
            d_mlp_in[s] = scatter(run(mlp_grad, gated[s][1], gated[s][2]))
            down_out[s] = scatter(run(down_proj, gated[s][0]))

        def mid_back(s):
            d_hidden[s], gain_mlp_part[s] = run(norm_back, d_mlp_in[s], norm_mlp_pull[s], d_y[s])
            d_hidden_all[s] = gather(d_hidden[s])

        def attn_back(s):
            part, d_qkv[s] = run(attn_grads, d_hidden_all[s], s)
            d_normed[s] = scatter(part)

        def last_back(s):
            grad_x[s], gain_attn_part[s] = run(norm_back, d_normed[s], norm_attn_pull[s], d_hidden[s])

        mlp_half(0)
        mlp_rest(0)
        mlp_half(1)
        mid_back(0)
        mlp_rest(1)
        y_out[0] = run(add_out, down_out[0], hidden[0])
        act_out, d_gate, d_up = zip(*gated)
        (grad_wdown,) = run(lambda first: weight_grad([first, act_out[1]], [dout_all], (depth,), 768, "g_down", "cols"),
                            act_out[0])
        attn_back(0)
        mid_back(1)
        grad_wgate, grad_wup = run(lambda first: weight_grad(
            [first, mlp_all[1]], [d_gate, d_up], (w_gate.shape[1],) * 2, 384, "g_gate_up", "rows"), mlp_all[0])
        attn_back(1)
        (grad_wo,) = run(lambda first: weight_grad([first, attn[1][0]], [d_hidden_all], (depth,), 768, "g_o", "cols"),
                         attn[0][0])
        d_q, d_k, d_v = zip(*d_qkv)
        grad_wq, grad_wk, grad_wv = run(lambda first: weight_grad(
            [first, normed_all[1]], [d_q, d_k, d_v], tuple(w.shape[1] for w in (wq2, wk2, wv2)), 384, "g_qkv", "rows"),
            normed_all[0])
        last_back(0)
        y_out[1] = run(add_out, down_out[1], hidden[1])
        last_back(1)
        back_attn, back_mlp = gain_attn_part, gain_mlp_part
        gain_parts = jnp.stack([functools.reduce(jnp.add, back) for back in (back_attn, back_mlp)])
        gains = tp_sum(gain_parts, n_tp)
        return (jnp.stack(y_out), jnp.stack(grad_x), grad_wq.reshape(w_q.shape), grad_wk.reshape(w_k.shape),
                grad_wv.reshape(w_v.shape), grad_wo.reshape(w_o.shape), grad_wgate, grad_wup, grad_wdown,
                gains[0], gains[1])

    return jax.shard_map(local_step, mesh=mesh, in_specs=in_specs, out_specs=out_specs, check_vma=False)
```

time: 1150 us -> 816 us (0.71)
  matrix products: 621 us -> 0 us
  Pallas kernels: 0 us -> 518 us
  waiting for transfers between devices: 383 us -> 210 us
  blocking collectives: 25.1 us -> 0 us
  other arithmetic: 58 us -> 36.5 us
  local copies, waits for them, and re-layouts: 41.3 us -> 24.8 us
    dot_general x27 -> x0, matrix products: 621 us -> none  [the longest x1 59.9 us: local_step(): jnp.einsum('bsf,df->bsd', d_gate, w_gate, preferred_element_type=jnp.floa...]
    pallas_call x0 -> x25, Pallas kernels: none -> 518 us  [the longest x12 228 us: rows_times_weights(): call(body, grid, [whole(a) for a in acts] + w_specs, pl.BlockSpec((n_rows...]
    all_gather x4 -> x8, waiting for transfers between devices: 215 us -> 112 us  [gather(): return lax.all_gather(part, 'tp', axis=0, tiled=True)]
    reduce_scatter x4 -> x8, waiting for transfers between devices: 167 us -> 95.6 us  [scatter(): return lax.psum_scatter(part, 'tp', scatter_dimension=0, tiled=True)]
    unnamed x124 -> x67, local copies, waits for them, and re-layouts: 41.3 us -> 9.04 us
    psum x1 -> x0, blocking collectives: 25.1 us -> none  [local_step(): grad_gain_attn = lax.psum(gain_attn_part, 'tp')]
  transfers between devices with their start and end apart: 8 -> 16, of which waited for: 5 -> 7; matrix products, arithmetic and copies ran while one was open for 43% -> 5% of each run, Pallas kernels for 0% -> 63%
where the time goes in v1:
time: 816 us; the launch traced here: 806 us
  Pallas kernels  518 us (63%)
  waiting for transfers between devices  210 us (26%)
  other arithmetic  36.5 us (4%)
  local copies, waits for them, and re-layouts  24.8 us (3%)
  between operations  14.8 us (2%)
    pallas_call x12, Pallas kernels, rows_times_weights(): call(body, grid, [whole(a) for a in acts] + w_specs, pl.BlockSpec((n_rows...  228 us
    pallas_call x4, Pallas kernels, weight_grad(): call(body, grid, l_specs + r_specs, o_specs, [jax.ShapeDtypeStruct((n_out...  144 us
    all_gather x8, waiting for transfers between devices, gather(): return lax.all_gather(part, 'tp', axis=0, tiled=True)  112 us
    reduce_scatter x8, waiting for transfers between devices, scatter(): return lax.psum_scatter(part, 'tp', scatter_dimension=0, tiled=True)  95.6 us
    pallas_call x2, Pallas kernels, gated_mlp(): call(body, (width // tile,), [whole(acts), w_spec, w_spec, o_spec], [o_sp...  81.9 us
    pallas_call x2, Pallas kernels, qkv_proj(): call(body, (n_rows // m_tile,), [pl.BlockSpec((m_tile, depth), lambda i:...  26.8 us
    pallas_call x2, Pallas kernels, attention_bwd(): call(body, (1,), [whole(a) for a in ins], [whole(a) for a in outs], outs,...  17.6 us
  transfers between devices with their start and end apart: 16, of which 7 were waited for; matrix products, arithmetic and copies ran while one was open for 5% of the time, Pallas kernels for 63%

profile of v1, /device:TPU:112, one launch (start us, length us, event | category | flops | bytes accessed | tf_op | source)
XLA Modules:
  0.0 805.9 jit_solution(9535536976018881173)
XLA Ops:
  7.3 0.7 broadcast_add_fusion.1
  8.0 1.6 slice_bitcast_fusion.3
  9.9 0.8 copy-done.29
  11.2 1.2 fusion.11
  12.9 0.6 copy-done.27
  14.0 1.2 fusion.10
  15.4 4.7 copy.23
  20.1 3.7 multiply_sine_fusion
  23.8 1.4 slice_bitcast_fusion.4
  25.2 33.6 %all-gather.9.cloned.1.call-done.a_ref.refs_0_ = bf16[1024,3840]{1,0:T(8,128)(2,1)} async-done(((bf16[128,3840]{1,0:T(8,128)(2,1)}), bf16[1024,3840]{1,0:T(8,128)(2,1)}) %all-gather.9.cloned.1.call-update) | async-done | bytes 7864336 | tf_op jit(solution)/shard_map/all_gather | solution.py:311
  58.7 13.4 %qkv.2 = (bf16[1024,512]{1,0:T(8,128)(2,1)}, bf16[1024,256]{1,0:T(8,128)(2,1)}, bf16[1024,256]{1,0:T(8,128)(2,1)}) custom-call(bf16[1024,3840]{1,0:T(8,128)(2,1)} %all-gather.9.cloned.1.call-done.a_ref.refs_0_, bf16[3840,512]{1,0:T(8,128)(2,1)} %bitcast.40, bf16[3840,256]{1,0:T(8,128)(2,1)} %bitcast.51, bf16[3840,256]{1,0:T(8,128)(2,1)} %bitcast.55), custom_call_target="tpu_custom_call" | custom-call | flops 8053063680 | bytes 17825792 | tf_op jit(solution)/shard_map/qkv/pallas_call | solution.py:107
  72.2 5.8 attn_fwd.2
  78.0 9.0 %o_proj.2 = bf16[1024,3840]{1,0:T(8,128)(2,1)} custom-call(bf16[1024,512]{1,0:T(8,128)(2,1)} %get-tuple-element.118.refs_0_, bf16[512,3840]{1,0:T(8,128)(2,1)} %bitcast.47), custom_call_target="tpu_custom_call" | custom-call | flops 4026531840 | bytes 12845056 | tf_op jit(solution)/shard_map/o_proj/pallas_call | solution.py:87
  87.3 17.0 %all-gather.11.cloned.1.call-done.a_ref.refs_1_ = bf16[1024,3840]{1,0:T(8,128)(2,1)} async-done(((bf16[128,3840]{1,0:T(8,128)(2,1)}), bf16[1024,3840]{1,0:T(8,128)(2,1)}) %all-gather.11.cloned.1.call-update) | async-done | bytes 7864336 | tf_op jit(solution)/shard_map/all_gather | solution.py:311
  104.4 13.4 %qkv.3 = (bf16[1024,512]{1,0:T(8,128)(2,1)}, bf16[1024,256]{1,0:T(8,128)(2,1)}, bf16[1024,256]{1,0:T(8,128)(2,1)}) custom-call(bf16[1024,3840]{1,0:T(8,128)(2,1)} %all-gather.11.cloned.1.call-done.a_ref.refs_1_, bf16[3840,512]{1,0:T(8,128)(2,1)} %bitcast.41, bf16[3840,256]{1,0:T(8,128)(2,1)} %bitcast.52, bf16[3840,256]{1,0:T(8,128)(2,1)} %bitcast.56), custom_call_target="tpu_custom_call" | custom-call | flops 8053063680 | bytes 17825792 | tf_op jit(solution)/shard_map/qkv/pallas_call | solution.py:107
  117.8 5.8 attn_fwd.3
  123.6 9.0 %o_proj.3 = bf16[1024,3840]{1,0:T(8,128)(2,1)} custom-call(bf16[1024,512]{1,0:T(8,128)(2,1)} %get-tuple-element.81.refs_0_.refs_1_, bf16[512,3840]{1,0:T(8,128)(2,1)} %bitcast.48), custom_call_target="tpu_custom_call" | custom-call | flops 4026531840 | bytes 12845056 | tf_op jit(solution)/shard_map/o_proj/pallas_call | solution.py:87
  132.8 3.0 slice_bitcast_fusion.1
  135.9 17.4 %reduce-scatter.9.cloned.1.call-done = bf16[128,3840]{1,0:T(8,128)(2,1)} async-done(((bf16[1024,3840]{1,0:T(8,128)(2,1)}), bf16[128,3840]{1,0:T(8,128)(2,1)}) %reduce-scatter.9.cloned.1.call-update) | async-done | bytes 983056 | tf_op jit(solution)/shard_map/reduce_scatter | solution.py:314
  153.4 1.6 fusion.24
  155.0 1.3 fusion.9
  156.4 45.3 %reduce-scatter.11.cloned.1.call-done = bf16[128,3840]{1,0:T(8,128)(2,1)} async-done(((bf16[1024,3840]{1,0:T(8,128)(2,1)}), bf16[128,3840]{1,0:T(8,128)(2,1)}) %reduce-scatter.11.cloned.1.call-update) | async-done | bytes 983056 | tf_op jit(solution)/shard_map/reduce_scatter | solution.py:314
  201.7 1.6 fusion.27
  204.5 1.2 fusion.8
  205.8 0.7 all-gather.17.cloned.1.call-update
  207.1 39.6 %all-gather.15.cloned.1.call-done.refs_0_.refs_2_ = bf16[1024,3840]{1,0:T(8,128)(2,1)} async-done(((bf16[128,3840]{1,0:T(8,128)(2,1)}), bf16[1024,3840]{1,0:T(8,128)(2,1)}) %all-gather.15.cloned.1.call-update) | async-done | bytes 7864336 | tf_op jit(solution)/shard_map/all_gather | solution.py:311
  246.6 23.3 %d_act.2.dz_ref = bf16[1024,1920]{1,0:T(8,128)(2,1)} custom-call(bf16[1024,3840]{1,0:T(8,128)(2,1)} %all-gather.15.cloned.1.call-done.refs_0_.refs_2_, bf16[1920,3840]{1,0:T(8,128)(2,1)} %refs_1_.7), custom_call_target="tpu_custom_call" | custom-call | flops 15099494400 | bytes 26542080 | tf_op jit(solution)/shard_map/d_act/pallas_call | solution.py:87
  270.0 22.1 %all-gather.13.cloned.1.call-done.a_ref.refs_0_ = bf16[1024,3840]{1,0:T(8,128)(2,1)} async-done(((bf16[128,3840]{1,0:T(8,128)(2,1)}), bf16[1024,3840]{1,0:T(8,128)(2,1)}) %all-gather.13.cloned.1.call-update) | async-done | bytes 7864336 | tf_op jit(solution)/shard_map/all_gather | solution.py:311
  292.1 40.9 %gated_mlp.2 = (bf16[1024,1920]{1,0:T(8,128)(2,1)}, bf16[1024,1920]{1,0:T(8,128)(2,1)}, bf16[1024,1920]{1,0:T(8,128)(2,1)}) custom-call(bf16[1024,3840]{1,0:T(8,128)(2,1)} %all-gather.13.cloned.1.call-done.a_ref.refs_0_, bf16[3840,1920]{1,0:T(8,128)(2,1)} %refs_2_.3, bf16[3840,1920]{1,0:T(8,128)(2,1)} %refs_3_.3, bf16[1024,1920]{1,0:T(8,128)(2,1)} %d_act.2.dz_ref), custom_call_target="tpu_custom_call" | custom-call | flops 30198988800 | bytes 53084160 | tf_op jit(solution)/shard_map/gated_mlp/pallas_call | solution.py:225
  333.0 37.8 %d_mlp.2 = bf16[1024,3840]{1,0:T(8,128)(2,1)} custom-call(bf16[1024,1920]{1,0:T(8,128)(2,1)} %get-tuple-element.89.refs_0_.refs_2_, bf16[1024,1920]{1,0:T(8,128)(2,1)} %get-tuple-element.90.refs_1_.refs_4_, bf16[3840,1920]{1,0:T(8,128)(2,1)} %refs_2_.3, bf16[3840,1920]{1,0:T(8,128)(2,1)} %refs_3_.3), custom_call_target="tpu_custom_call" | custom-call | flops 30198988800 | bytes 45219840 | tf_op jit(solution)/shard_map/d_mlp/pallas_call | solution.py:87
  371.0 21.4 %down.2 = bf16[1024,3840]{1,0:T(8,128)(2,1)} custom-call(bf16[1024,1920]{1,0:T(8,128)(2,1)} %get-tuple-element.104.refs_0_, bf16[1920,3840]{1,0:T(8,128)(2,1)} %refs_1_.7), custom_call_target="tpu_custom_call" | custom-call | flops 15099494400 | bytes 26542080 | tf_op jit(solution)/shard_map/down/pallas_call | solution.py:87
  392.5 23.6 %d_act.3.dz_ref = bf16[1024,1920]{1,0:T(8,128)(2,1)} custom-call(bf16[1024,3840]{1,0:T(8,128)(2,1)} %all-gather.19.cloned.1.call-done.refs_0_.refs_3_, bf16[1920,3840]{1,0:T(8,128)(2,1)} %refs_1_.7), custom_call_target="tpu_custom_call" | custom-call | flops 15099494400 | bytes 26542080 | tf_op jit(solution)/shard_map/d_act/pallas_call | solution.py:87
  416.1 40.9 %gated_mlp.3 = (bf16[1024,1920]{1,0:T(8,128)(2,1)}, bf16[1024,1920]{1,0:T(8,128)(2,1)}, bf16[1024,1920]{1,0:T(8,128)(2,1)}) custom-call(bf16[1024,3840]{1,0:T(8,128)(2,1)} %all-gather.17.cloned.1.call-done.a_ref.refs_1_, bf16[3840,1920]{1,0:T(8,128)(2,1)} %refs_2_.3, bf16[3840,1920]{1,0:T(8,128)(2,1)} %refs_3_.3, bf16[1024,1920]{1,0:T(8,128)(2,1)} %d_act.3.dz_ref), custom_call_target="tpu_custom_call" | custom-call | flops 30198988800 | bytes 53084160 | tf_op jit(solution)/shard_map/gated_mlp/pallas_call | solution.py:225
  457.1 2.7 fusion.12
  459.8 2.8 fusion.34
  462.8 37.6 %d_mlp.3 = bf16[1024,3840]{1,0:T(8,128)(2,1)} custom-call(bf16[1024,1920]{1,0:T(8,128)(2,1)} %get-tuple-element.98.refs_0_.refs_3_, bf16[1024,1920]{1,0:T(8,128)(2,1)} %get-tuple-element.99.refs_1_.refs_5_, bf16[3840,1920]{1,0:T(8,128)(2,1)} %refs_2_.3, bf16[3840,1920]{1,0:T(8,128)(2,1)} %refs_3_.3), custom_call_target="tpu_custom_call" | custom-call | flops 30198988800 | bytes 45219840 | tf_op jit(solution)/shard_map/d_mlp/pallas_call | solution.py:87
  500.6 21.9 %down.3 = bf16[1024,3840]{1,0:T(8,128)(2,1)} custom-call(bf16[1024,1920]{1,0:T(8,128)(2,1)} %get-tuple-element.100.refs_0_.refs_1_, bf16[1920,3840]{1,0:T(8,128)(2,1)} %refs_1_.7), custom_call_target="tpu_custom_call" | custom-call | flops 15099494400 | bytes 26542080 | tf_op jit(solution)/shard_map/down/pallas_call | solution.py:87
  522.5 2.4 fusion.26
  524.8 37.9 %g_down.1 = bf16[1920,3840]{1,0:T(8,128)(2,1)} custom-call(bf16[1024,1920]{1,0:T(8,128)(2,1)} %get-tuple-element.104.refs_0_, bf16[1024,1920]{1,0:T(8,128)(2,1)} %get-tuple-element.100.refs_0_.refs_1_, bf16[1024,3840]{1,0:T(8,128)(2,1)} %all-gather.15.cloned.1.call-done.refs_0_.refs_2_, bf16[1024,3840]{1,0:T(8,128)(2,1)} %all-gather.19.cloned.1.call-done.refs_0_.refs_3_), custom_call_target="tpu_custom_call" | custom-call | flops 30198988800 | bytes 38338560 | tf_op jit(solution)/shard_map/g_down/pallas_call | solution.py:259
  562.7 9.2 %d_attn.2.d_o = bf16[1024,512]{1,0:T(8,128)(2,1)} custom-call(bf16[1024,3840]{1,0:T(8,128)(2,1)} %all-gather.21.cloned.1.call-done.refs_0_.refs_2_, bf16[512,3840]{1,0:T(8,128)(2,1)} %bitcast.49), custom_call_target="tpu_custom_call" | custom-call | flops 4026531840 | bytes 12845056 | tf_op jit(solution)/shard_map/d_attn/pallas_call | solution.py:87
  572.0 8.8 %attn_bwd.2 = (bf16[1024,512]{1,0:T(8,128)(2,1)}, bf16[1024,256]{1,0:T(8,128)(2,1)}, bf16[1024,256]{1,0:T(8,128)(2,1)}) custom-call(bf16[1024,512]{1,0:T(8,128)(2,1)} %get-tuple-element.102.q, bf16[1024,256]{1,0:T(8,128)(2,1)} %get-tuple-element.103.k, bf16[1024,256]{1,0:T(8,128)(2,1)} %get-tuple-element.73.v, bf16[1024,512]{1,0:T(8,128)(2,1)} %d_attn.2.d_o, ...), custom_call_target="tpu_custom_call" | custom-call | flops 8000000000 | bytes 8000000 | tf_op jit(solution)/shard_map/attn_bwd/pallas_call | solution.py:195
  580.8 12.8 %d_normed.2 = bf16[1024,3840]{1,0:T(8,128)(2,1)} custom-call(bf16[1024,512]{1,0:T(8,128)(2,1)} %get-tuple-element.106.refs_0_.refs_2_, bf16[1024,256]{1,0:T(8,128)(2,1)} %get-tuple-element.107.refs_1_.refs_4_, bf16[1024,256]{1,0:T(8,128)(2,1)} %get-tuple-element.108.refs_2_.refs_6_, bf16[3840,512]{1,0:T(8,128)(2,1)} %bitcast.42, bf16[3840,256]{1,0:T(8,128)(2,1)} %bitcast.53, ...), custom_call_target="tpu_custom_call" | custom-call | flops 8053063680 | bytes 17825792 | tf_op jit(solution)/shard_map/d_normed/pallas_call | solution.py:87
  593.6 2.1 fusion.13
  595.7 1.7 fusion.33
  598.2 0.6 reduce-scatter.17.cloned.1.call-update
  598.8 70.6 %g_gate_up.1 = (bf16[3840,1920]{1,0:T(8,128)(2,1)}, bf16[3840,1920]{1,0:T(8,128)(2,1)}) custom-call(bf16[1024,3840]{1,0:T(8,128)(2,1)} %all-gather.13.cloned.1.call-done.a_ref.refs_0_, bf16[1024,3840]{1,0:T(8,128)(2,1)} %all-gather.17.cloned.1.call-done.a_ref.refs_1_, bf16[1024,1920]{1,0:T(8,128)(2,1)} %get-tuple-element.89.refs_0_.refs_2_, ...), custom_call_target="tpu_custom_call" | custom-call | flops 60397977600 | bytes 60948480 | tf_op jit(solution)/shard_map/g_gate_up/pallas_call | solution.py:259
  669.4 9.1 %d_attn.3.d_o = bf16[1024,512]{1,0:T(8,128)(2,1)} custom-call(bf16[1024,3840]{1,0:T(8,128)(2,1)} %all-gather.23.cloned.1.call-done.refs_0_.refs_3_, bf16[512,3840]{1,0:T(8,128)(2,1)} %bitcast.50), custom_call_target="tpu_custom_call" | custom-call | flops 4026531840 | bytes 12845056 | tf_op jit(solution)/shard_map/d_attn/pallas_call | solution.py:87
  678.5 8.8 %attn_bwd.3 = (bf16[1024,512]{1,0:T(8,128)(2,1)}, bf16[1024,256]{1,0:T(8,128)(2,1)}, bf16[1024,256]{1,0:T(8,128)(2,1)}) custom-call(bf16[1024,512]{1,0:T(8,128)(2,1)} %get-tuple-element.109.q, bf16[1024,256]{1,0:T(8,128)(2,1)} %get-tuple-element.110.k, bf16[1024,256]{1,0:T(8,128)(2,1)} %get-tuple-element.79.v, bf16[1024,512]{1,0:T(8,128)(2,1)} %d_attn.3.d_o, ...), custom_call_target="tpu_custom_call" | custom-call | flops 8000000000 | bytes 8000000 | tf_op jit(solution)/shard_map/attn_bwd/pallas_call | solution.py:195
  687.3 12.9 %d_normed.3 = bf16[1024,3840]{1,0:T(8,128)(2,1)} custom-call(bf16[1024,512]{1,0:T(8,128)(2,1)} %get-tuple-element.115.refs_0_.refs_3_, bf16[1024,256]{1,0:T(8,128)(2,1)} %get-tuple-element.116.refs_1_.refs_5_, bf16[1024,256]{1,0:T(8,128)(2,1)} %get-tuple-element.117.refs_2_.refs_7_, bf16[3840,512]{1,0:T(8,128)(2,1)} %bitcast.43, bf16[3840,256]{1,0:T(8,128)(2,1)} %bitcast.54, ...), custom_call_target="tpu_custom_call" | custom-call | flops 8053063680 | bytes 17825792 | tf_op jit(solution)/shard_map/d_normed/pallas_call | solution.py:87
  700.3 0.7 copy-done.17
  700.9 13.3 %g_o.1 = bf16[512,3840]{1,0:T(8,128)(2,1)} custom-call(bf16[1024,512]{1,0:T(8,128)(2,1)} %get-tuple-element.118.refs_0_, bf16[1024,512]{1,0:T(8,128)(2,1)} %get-tuple-element.81.refs_0_.refs_1_, bf16[1024,3840]{1,0:T(8,128)(2,1)} %all-gather.21.cloned.1.call-done.refs_0_.refs_2_, bf16[1024,3840]{1,0:T(8,128)(2,1)} %all-gather.23.cloned.1.call-done.refs_0_.refs_3_), custom_call_target="tpu_custom_call" | custom-call | flops 8053063680 | bytes 21757952 | tf_op jit(solution)/shard_map/g_o/pallas_call | solution.py:259
  714.3 21.9 %g_qkv.1 = (bf16[3840,512]{1,0:T(8,128)(2,1)}, bf16[3840,256]{1,0:T(8,128)(2,1)}, bf16[3840,256]{1,0:T(8,128)(2,1)}) custom-call(bf16[1024,3840]{1,0:T(8,128)(2,1)} %all-gather.9.cloned.1.call-done.a_ref.refs_0_, bf16[1024,3840]{1,0:T(8,128)(2,1)} %all-gather.11.cloned.1.call-done.a_ref.refs_1_, bf16[1024,512]{1,0:T(8,128)(2,1)} %get-tuple-element.106.refs_0_.refs_2_, ...), custom_call_target="tpu_custom_call" | custom-call | flops 16106127360 | bytes 27787264 | tf_op jit(solution)/shard_map/g_qkv/pallas_call | solution.py:259
  736.2 9.0 %reshape.150 = bf16[3840,2,256]{2,1,0:T(2,128)(2,1)} reshape(bf16[3840,512]{1,0:T(8,128)(2,1)} %get-tuple-element.120) | data formatting | bytes 7864320 | tf_op jit(solution)/shard_map/reshape | solution.py:437
  745.2 2.1 fusion.14
  747.4 1.6 fusion.32
  749.1 1.5 fusion.29
  750.6 1.4 pad_maximum_fusion
  752.0 32.8 %reduce-scatter.23.cloned.1.call-done = bf16[128,3840]{1,0:T(8,128)(2,1)} async-done(((bf16[1024,3840]{1,0:T(8,128)(2,1)}), bf16[128,3840]{1,0:T(8,128)(2,1)}) %reduce-scatter.23.cloned.1.call-update) | async-done | bytes 983056 | tf_op jit(solution)/shard_map/reduce_scatter | solution.py:314
  784.9 2.0 fusion.15
  786.9 0.6 pad_maximum_fusion.2.x_ref
  787.5 8.5 %tp_sum.1 = f32[2,3840]{1,0:T(2,128)} custom-call(f32[2,3840]{1,0:T(2,128)} %pad_maximum_fusion.2.x_ref), custom_call_target="tpu_custom_call" | custom-call | flops 5000000000 | bytes 1000000 | tf_op jit(solution)/shard_map/tp_sum/pallas_call | solution.py:288
  796.1 0.7 fusion.31
  796.8 0.7 slice_reduce_fusion
  797.5 1.4 pad_maximum_fusion.1
  (119 shorter events, 5.9 us)
Async XLA Ops:
  7.2 51.6 %all-gather.9.cloned.1.call-start = ((), (), s32[]{:S(2)}) async-start(), calls=%async_computation.8 | async-start | bytes 8847360 | tf_op jit(solution)/shard_map/all_gather | solution.py:311
  8.0 5.5 copy-start.15
  9.6 1.1 copy-start.2
  9.6 3.9 copy-start
  9.9 0.8 copy-start.29
  10.7 0.5 copy-start.23
  12.5 91.8 %all-gather.11.cloned.1.call-start = ((), (), s32[]{:S(2)}) async-start(), calls=%async_computation.10 | async-start | bytes 8847360 | tf_op jit(solution)/shard_map/all_gather | solution.py:311
  12.6 2.8 copy-start.20
  12.9 0.6 copy-start.27
  13.5 0.5 copy-start.21
  15.3 138.0 %reduce-scatter.9.cloned.1.call-start = ((), (), s32[]{:S(2)}) async-start(), calls=%async_computation.9 | async-start | bytes 8847360 | tf_op jit(solution)/shard_map/reduce_scatter | solution.py:314
  87.1 114.7 %reduce-scatter.11.cloned.1.call-start = ((), (), s32[]{:S(2)}) async-start(), calls=%async_computation.13 | async-start | bytes 8847360 | tf_op jit(solution)/shard_map/reduce_scatter | solution.py:314
  132.7 3.3 copy-start.19
  132.7 20.7 %copy-start.8 = (bf16[2,128,3840]{2,1,0:T(8,128)(2,1)S(1)}, bf16[2,128,3840]{2,1,0:T(8,128)(2,1)}, u32[]{:S(2)}) copy-start(bf16[2,128,3840]{2,1,0:T(8,128)(2,1)} %param.12) | copy-start | bytes 5898244
  132.7 114.0 %all-gather.15.cloned.1.call-start = ((), (), s32[]{:S(2)}) async-start(), calls=%async_computation.12 | async-start | bytes 8847360 | tf_op jit(solution)/shard_map/all_gather | solution.py:311
  135.8 156.2 %all-gather.13.cloned.1.call-start = ((), (), s32[]{:S(2)}) async-start(), calls=%async_computation.11 | async-start | bytes 8847360 | tf_op jit(solution)/shard_map/all_gather | solution.py:311
  156.3 236.2 %all-gather.19.cloned.1.call-start = ((), (), s32[]{:S(2)}) async-start(), calls=%async_computation.16 | async-start | bytes 8847360 | tf_op jit(solution)/shard_map/all_gather | solution.py:311
  203.4 0.5 copy-start.31
  203.4 1.0 copy-start.4
  203.9 0.6 copy-start.25
  205.8 210.3 %all-gather.17.cloned.1.call-start = ((), (), s32[]{:S(2)}) async-start(), calls=%async_computation.15 | async-start | bytes 8847360 | tf_op jit(solution)/shard_map/all_gather | solution.py:311
  206.6 250.5 %reduce-scatter.15.cloned.1.call-start = ((), (), s32[]{:S(2)}) async-start(), calls=%async_computation.17 | async-start | bytes 8847360 | tf_op jit(solution)/shard_map/reduce_scatter | solution.py:314
  370.9 151.6 %reduce-scatter.13.cloned.1.call-start = ((), (), s32[]{:S(2)}) async-start(), calls=%async_computation.14 | async-start | bytes 8847360 | tf_op jit(solution)/shard_map/reduce_scatter | solution.py:314
  392.4 170.3 %all-gather.21.cloned.1.call-start = ((), (), s32[]{:S(2)}) async-start(), calls=%async_computation.19 | async-start | bytes 8847360 | tf_op jit(solution)/shard_map/all_gather | solution.py:311
  457.0 2.8 copy-start.9
  462.7 130.9 %reduce-scatter.21.cloned.1.call-start = ((), (), s32[]{:S(2)}) async-start(), calls=%async_computation.21 | async-start | bytes 8847360 | tf_op jit(solution)/shard_map/reduce_scatter | solution.py:314
  500.5 168.9 %all-gather.23.cloned.1.call-start = ((), (), s32[]{:S(2)}) async-start(), calls=%async_computation.22 | async-start | bytes 8847360 | tf_op jit(solution)/shard_map/all_gather | solution.py:311
  580.8 12.8 %copy-start.5 = (bf16[128,3840]{1,0:T(8,128)(2,1)S(1)}, bf16[128,3840]{1,0:T(8,128)(2,1)}, u32[]{:S(2)}) copy-start(bf16[128,3840]{1,0:T(8,128)(2,1)} %copy-done.4) | copy-start | bytes 2949124
  580.8 12.8 %copy-start.26 = (f32[128]{0:T(128)S(1)}, f32[128]{0:T(128)}, u32[]{:S(2)}) copy-start(f32[128]{0:T(128)} %copy-done.25) | copy-start | bytes 1540
  593.6 2.1 copy-start.32
  593.6 2.1 copy-start.12
  597.4 147.8 %reduce-scatter.19.cloned.1.call-start = ((), (), s32[]{:S(2)}) async-start(), calls=%async_computation.20 | async-start | bytes 8847360 | tf_op jit(solution)/shard_map/reduce_scatter | solution.py:314
  598.1 151.0 %reduce-scatter.17.cloned.1.call-start = ((), (), s32[]{:S(2)}) async-start(), calls=%async_computation.18 | async-start | bytes 8847360 | tf_op jit(solution)/shard_map/reduce_scatter | solution.py:314
  598.7 186.1 %reduce-scatter.23.cloned.1.call-start = ((), (), s32[]{:S(2)}) async-start(), calls=%async_computation.23 | async-start | bytes 8847360 | tf_op jit(solution)/shard_map/reduce_scatter | solution.py:314
  700.2 0.7 copy-start.17
  736.2 9.0 %copy-start.3 = (bf16[128,3840]{1,0:T(8,128)(2,1)S(1)}, bf16[128,3840]{1,0:T(8,128)(2,1)}, u32[]{:S(2)}) copy-start(bf16[128,3840]{1,0:T(8,128)(2,1)} %copy-done.2) | copy-start | bytes 2949124
  736.2 9.1 %copy-start.16 = (f32[3840]{0:T(1024)S(1)}, f32[3840]{0:T(1024)}, u32[]{:S(2)}) copy-start(f32[3840]{0:T(1024)} %copy-done.15) | copy-start | bytes 46084
  736.2 9.1 %copy-start.24 = (f32[128]{0:T(128)S(1)}, f32[128]{0:T(128)}, u32[]{:S(2)}) copy-start(f32[128]{0:T(128)} %copy-done.23) | copy-start | bytes 1540
  745.2 2.2 copy-start.30
  745.2 2.2 copy-start.6
  745.2 2.2 copy-start.10
  749.1 1.5 copy-start.13
  750.6 34.3 %copy-start.1 = (bf16[128,3840]{1,0:T(8,128)(2,1)S(1)}, bf16[128,3840]{1,0:T(8,128)(2,1)}, u32[]{:S(2)}) copy-start(bf16[128,3840]{1,0:T(8,128)(2,1)} %copy-done) | copy-start | bytes 2949124
  750.6 34.3 %copy-start.22 = (f32[128]{0:T(128)S(1)}, f32[128]{0:T(128)}, u32[]{:S(2)}) copy-start(f32[128]{0:T(128)} %copy-done.21) | copy-start | bytes 1540
  787.5 8.5 %copy-start.28 = (f32[128]{0:T(128)S(1)}, f32[128]{0:T(128)}, u32[]{:S(2)}) copy-start(f32[128]{0:T(128)} %copy-done.27) | copy-start | bytes 1540
  787.5 8.5 %copy-start.7 = (bf16[128,3840]{1,0:T(8,128)(2,1)S(1)}, bf16[128,3840]{1,0:T(8,128)(2,1)}, u32[]{:S(2)}) copy-start(bf16[128,3840]{1,0:T(8,128)(2,1)} %fusion.33) | copy-start | bytes 2949124
  787.5 8.5 %copy-start.11 = (bf16[128,3840]{1,0:T(8,128)(2,1)S(1)}, bf16[128,3840]{1,0:T(8,128)(2,1)}, u32[]{:S(2)}) copy-start(bf16[128,3840]{1,0:T(8,128)(2,1)} %reduce-scatter.23.cloned.1.call-done) | copy-start | bytes 2949124
  796.1 0.8 copy-start.18
  796.1 1.4 copy-start.14
Sparse Core Ops, SparseCore 0:
  12.7 46.0 all-gather.8
  60.9 43.4 all-gather.10
  107.2 46.0 reduce-scatter.8
  156.1 45.5 reduce-scatter.10
  203.7 42.8 all-gather.14
  248.7 43.3 all-gather.12
  294.2 43.3 all-gather.18
  339.8 43.3 all-gather.16
  386.1 46.0 reduce-scatter.14
  435.0 45.5 reduce-scatter.12
  482.2 42.8 all-gather.20
  527.9 46.0 reduce-scatter.20
  597.6 43.3 all-gather.22
  643.1 46.1 reduce-scatter.18
  691.5 45.5 reduce-scatter.16
  739.2 45.5 reduce-scatter.22

commit v2 on v1

--- a/solution.py
+++ b/solution.py
@@ -6,6 +6,7 @@
 from jax.experimental import pallas as pl
 from jax.experimental.pallas import tpu as pltpu
 from jax.sharding import PartitionSpec as P
+
 
 EPS = 1e-6
 ROPE_THETA = 10000.0
@@ -45,7 +46,7 @@
     return parts[0] if len(parts) == 1 else jnp.concatenate(parts, axis=axis)
 
 
-def call(body, grid, in_specs, out_specs, out_shape, flops, nbytes, name, scratch=()):
+def call(body, grid, in_specs, out_specs, out_shape, flops, nbytes, scratch=()):
     return pl.pallas_call(
         body,
         grid=grid,
@@ -55,7 +56,6 @@
         scratch_shapes=scratch,
         compiler_params=pltpu.CompilerParams(vmem_limit_bytes=VMEM_LIMIT),
         cost_estimate=pl.CostEstimate(flops=int(flops), bytes_accessed=int(nbytes), transcendentals=0),
-        name=name,
     )
 
 
@@ -64,7 +64,7 @@
     return pl.BlockSpec(arr.shape, lambda *_: zeros, pipeline_mode=pl.Buffered(1))
 
 
-def rows_times_weights(acts, weights, kind, tile, name, m_tile=256):
+def rows_times_weights(acts, weights, kind, tile, m_tile=256):
     n_rows = acts[0].shape[0]
     nt = kind == "nt"
     n_cols = weights[0].shape[0 if nt else 1]
@@ -88,29 +88,8 @@
         body, grid, [whole(a) for a in acts] + w_specs,
         pl.BlockSpec((n_rows, tile), lambda i: (0, i)),
         jax.ShapeDtypeStruct((n_rows, n_cols), BF),
-        2 * n_rows * depth * n_cols, 2 * (n_rows * depth + depth * n_cols + n_rows * n_cols), name,
+        2 * n_rows * depth * n_cols, 2 * (n_rows * depth + depth * n_cols + n_rows * n_cols),
     )(*acts, *weights)
-
-
-def qkv_proj(acts, w_q, w_k, w_v):
-    n_rows, depth = acts.shape
-    m_tile = 256
-    widths = (w_q.shape[1], w_k.shape[1], w_v.shape[1])
-
-    def body(a_ref, wq, wk, wv, q, k, v):
-        lhs = a_ref[...]
-        q[...] = dot(lhs, wq[...], NN).astype(BF)
-        kv = dot(lhs, jnp.concatenate([wk[...], wv[...]], axis=1), NN).astype(BF)
-        k[...] = kv[:, : widths[1]]
-        v[...] = kv[:, widths[1]:]
-
-    return call(
-        body, (n_rows // m_tile,),
-        [pl.BlockSpec((m_tile, depth), lambda i: (i, 0)), whole(w_q), whole(w_k), whole(w_v)],
-        [pl.BlockSpec((m_tile, w), lambda i: (i, 0)) for w in widths],
-        [jax.ShapeDtypeStruct((n_rows, w), BF) for w in widths],
-        2 * n_rows * depth * sum(widths), 2 * (n_rows * depth + depth * sum(widths) + n_rows * sum(widths)), "qkv",
-    )(acts, w_q, w_k, w_v)
 
 
 def rotate(vals, cos_t, sin_t):
@@ -135,67 +114,179 @@
     return probs / jnp.sum(probs, axis=1, keepdims=True)
 
 
-def attention_fwd(q_raw, k_raw, v_raw, cos_t, sin_t, scale):
-    n_rows, head = k_raw.shape
-    n_rep = q_raw.shape[1] // head
+def attention_fwd(acts, w_qkv, w_o, cos_t, sin_t, n_rep, head, scale):
+    n_rows, depth = acts.shape
+    n_q, width = n_rep * head, w_qkv.shape[1]
     tile = 256
-
-    def body(q, k, v, cos_ref, sin_ref, out, q_rot, k_rot):
-        k_rot[...] = rotate(k[...], cos_ref[...], sin_ref[...]).astype(BF)
-        for h in range(n_rep):
-            cols = pl.ds(h * head, head)
-            q_rot[:, cols] = (rotate(q[:, cols], cos_ref[...], sin_ref[...]) * scale).astype(BF)
-        for start in range(0, n_rows, tile):
-            rows = pl.ds(start, tile)
-            q_rows = join([q_rot[rows, pl.ds(h * head, head)] for h in range(n_rep)], 0)
-            probs = causal_probs(q_rows, k_rot, start, tile, n_rep).astype(BF)
-            mixed = dot(probs, v[: start + tile], NN).astype(BF)
+    n_tiles, n_cols = n_rows // tile, width // tile
+
+    def body(acts_hbm, w_hbm, wo_hbm, cos_ref, sin_ref, q_rot, k_rot, v, out, part_hbm,
+             acts_v, w_v, wo_v, qkv, part_v, a_sem, w_sem, wo_sem, o_sem):
+        a_copy = [pltpu.make_async_copy(acts_hbm.at[pl.ds(i * tile, tile)], acts_v.at[pl.ds(i * tile, tile)],
+                                        a_sem.at[i]) for i in range(n_tiles)]
+        w_copy = [pltpu.make_async_copy(w_hbm.at[:, pl.ds(i * tile, tile)], w_v.at[:, pl.ds(i * tile, tile)],
+                                        w_sem.at[i]) for i in range(n_cols)]
+        wo_copy = pltpu.make_async_copy(wo_hbm, wo_v, wo_sem)
+        o_copy = [pltpu.make_async_copy(part_v.at[i % 2], part_hbm.at[pl.ds(i * tile, tile)], o_sem.at[i % 2])
+                  for i in range(n_tiles)]
+        for copy in a_copy[:1] + w_copy + [wo_copy] + a_copy[1:]:
+            copy.start()
+        for i in range(n_tiles):
+            rows = pl.ds(i * tile, tile)
+            a_copy[i].wait()
+            if i == 0:
+                for j in range(n_cols):
+                    w_copy[j].wait()
+                    cols = pl.ds(j * tile, tile)
+                    qkv[:, cols] = dot(acts_v[rows, :], w_v[:, cols], NN).astype(BF)
+                wo_copy.wait()
+            else:
+                qkv[...] = dot(acts_v[rows, :], w_v[...], NN).astype(BF)
+            cos, sin = cos_ref[rows, :], sin_ref[rows, :]
+            k_rot[rows, :] = rotate(qkv[:, n_q:n_q + head], cos, sin).astype(BF)
+            v[rows, :] = qkv[:, n_q + head:]
+            q_rows = join([(rotate(qkv[:, h * head:(h + 1) * head], cos, sin) * scale).astype(BF)
+                           for h in range(n_rep)], 0)
+            probs = causal_probs(q_rows, k_rot, i * tile, tile, n_rep).astype(BF)
+            mixed = dot(probs, v[: (i + 1) * tile], NN).astype(BF)
             for h in range(n_rep):
-                out[rows, pl.ds(h * head, head)] = mixed[h * tile:(h + 1) * tile]
-
-    ins = (q_raw, k_raw, v_raw, cos_t, sin_t)
-    outs = [jax.ShapeDtypeStruct(a.shape, BF) for a in (q_raw, q_raw, k_raw)]
-    return call(
-        body, (1,), [whole(a) for a in ins], [whole(a) for a in outs], outs,
-        4e9, 8e6, "attn_fwd",
-    )(*ins)
-
-
-def attention_bwd(q_rot, k_rot, v_raw, d_out, cos_t, sin_t, scale):
-    n_rows, head = k_rot.shape
-    n_rep = q_rot.shape[1] // head
+                cols = pl.ds(h * head, head)
+                q_rot[rows, cols] = q_rows[h * tile:(h + 1) * tile]
+                out[rows, cols] = mixed[h * tile:(h + 1) * tile]
+            if i >= 2:
+                o_copy[i].wait()
+            heads = join([mixed[h * tile:(h + 1) * tile] for h in range(n_rep)], 1)
+            part_v[i % 2] = dot(heads, wo_v[...], NN).astype(BF)
+            o_copy[i].start()
+        for i in range(max(0, n_tiles - 2), n_tiles):
+            o_copy[i].wait()
+
+    any_spec = pl.BlockSpec(memory_space=pl.ANY)
+    outs = [jax.ShapeDtypeStruct((n_rows, w), BF) for w in (n_q, head, head, n_q)]
+    return call(
+        body, (1,), [any_spec] * 3 + [whole(cos_t), whole(sin_t)], [whole(o) for o in outs] + [any_spec],
+        outs + [jax.ShapeDtypeStruct((n_rows, depth), BF)],
+        2 * n_rows * depth * (width + n_q) + 4e9, 2 * (2 * n_rows * depth + depth * (width + n_q)),
+        [pltpu.VMEM((n_rows, depth), BF), pltpu.VMEM(w_qkv.shape, BF), pltpu.VMEM(w_o.shape, BF),
+         pltpu.VMEM((tile, width), BF), pltpu.VMEM((2, tile, depth), BF),
+         pltpu.SemaphoreType.DMA((n_tiles,)), pltpu.SemaphoreType.DMA((n_cols,)), pltpu.SemaphoreType.DMA,
+         pltpu.SemaphoreType.DMA((2,))],
+    )(acts, w_qkv, w_o, cos_t, sin_t)
+
+
+def attention_bwd(cot, w_qkv, w_o, q_rot, k_rot, v_raw, cos_t, sin_t, scale):
+    n_rows, depth = cot.shape
+    head = k_rot.shape[1]
+    n_q, width = q_rot.shape[1], w_qkv.shape[1]
+    n_rep = n_q // head
     tile = 256
-
-    def body(q, k, v, d_o, cos_ref, sin_ref, d_q, d_k, d_v, dk_acc, dv_acc):
-        for start in reversed(range(0, n_rows, tile)):
-            end = start + tile
-            rows = pl.ds(start, tile)
+    n_tiles = n_rows // tile
+
+    def body(cot_hbm, w_hbm, wo_hbm, q, k, v, cos_ref, sin_ref, d_qkv, part_hbm,
+             cot_v, w_v, wo_v, part_v, dk_acc, dv_acc, c_sem, w_sem, wo_sem, o_sem):
+        order = list(reversed(range(n_tiles)))
+        c_copy = [pltpu.make_async_copy(cot_hbm.at[pl.ds(i * tile, tile)], cot_v.at[pl.ds(i * tile, tile)],
+                                        c_sem.at[i]) for i in range(n_tiles)]
+        w_copy = pltpu.make_async_copy(w_hbm, w_v, w_sem)
+        wo_copy = pltpu.make_async_copy(wo_hbm, wo_v, wo_sem)
+        o_copy = [pltpu.make_async_copy(part_v.at[i % 2], part_hbm.at[pl.ds(i * tile, tile)], o_sem.at[i % 2])
+                  for i in range(n_tiles)]
+        for copy in [wo_copy] + [c_copy[i] for i in order[:1]] + [w_copy] + [c_copy[i] for i in order[1:]]:
+            copy.start()
+        wo_copy.wait()
+        for n, i in enumerate(order):
+            rows, end = pl.ds(i * tile, tile), (i + 1) * tile
+            c_copy[i].wait()
+            d_o = dot(cot_v[rows, :], wo_v[...], NT).astype(BF)
             q_rows = join([q[rows, pl.ds(h * head, head)] for h in range(n_rep)], 0)
-            do_rows = join([d_o[rows, pl.ds(h * head, head)] for h in range(n_rep)], 0)
-            probs = causal_probs(q_rows, k, start, tile, n_rep)
+            do_rows = join([d_o[:, h * head:(h + 1) * head] for h in range(n_rep)], 0)
+            probs = causal_probs(q_rows, k, i * tile, tile, n_rep)
             d_probs = dot(do_rows, v[:end], NT)
             d_scores = (probs * (d_probs - jnp.sum(d_probs * probs, axis=1, keepdims=True))).astype(BF)
             dv_part = dot(probs.astype(BF), do_rows, TN)
             dk_part = dot(d_scores, q_rows, TN)
-            if end == n_rows:
+            if n == 0:
                 dv_acc[...] = dv_part
                 dk_acc[...] = dk_part
             else:
                 dv_acc[:end] += dv_part
                 dk_acc[:end] += dk_part
             dq_rows = dot(d_scores, k[:end], NN).astype(BF).astype(F32) * scale
-            for h in range(n_rep):
-                part = dq_rows[h * tile:(h + 1) * tile]
-                d_q[rows, pl.ds(h * head, head)] = unrotate(part, cos_ref[rows, :], sin_ref[rows, :]).astype(BF)
-        d_v[...] = dv_acc[...].astype(BF)
-        d_k[...] = unrotate(dk_acc[...].astype(BF).astype(F32), cos_ref[...], sin_ref[...]).astype(BF)
-
-    ins = (q_rot, k_rot, v_raw, d_out, cos_t, sin_t)
-    outs = [jax.ShapeDtypeStruct(a.shape, BF) for a in (q_rot, k_rot, v_raw)]
-    return call(
-        body, (1,), [whole(a) for a in ins], [whole(a) for a in outs], outs,
-        8e9, 8e6, "attn_bwd", [pltpu.VMEM((n_rows, head), F32)] * 2,
-    )(*ins)
+            cos, sin = cos_ref[rows, :], sin_ref[rows, :]
+            parts = [unrotate(dq_rows[h * tile:(h + 1) * tile], cos, sin).astype(BF) for h in range(n_rep)]
+            parts.append(unrotate(dk_acc[rows, :].astype(BF).astype(F32), cos, sin).astype(BF))
+            parts.append(dv_acc[rows, :].astype(BF))
+            tile_grad = join(parts, 1)
+            d_qkv[rows, :] = tile_grad
+            if n == 0:
+                w_copy.wait()
+            if n >= 2:
+                o_copy[i].wait()
+            part_v[i % 2] = dot(tile_grad, w_v[...], NT).astype(BF)
+            o_copy[i].start()
+        for i in order[-2:]:
+            o_copy[i].wait()
+
+    any_spec = pl.BlockSpec(memory_space=pl.ANY)
+    rest = (q_rot, k_rot, v_raw, cos_t, sin_t)
+    outs = [jax.ShapeDtypeStruct((n_rows, width), BF), jax.ShapeDtypeStruct((n_rows, depth), BF)]
+    return call(
+        body, (1,), [any_spec] * 3 + [whole(r) for r in rest], [whole(outs[0]), any_spec], outs,
+        2 * n_rows * depth * (width + n_q) + 8e9, 2 * (2 * n_rows * depth + depth * (width + n_q)),
+        [pltpu.VMEM((n_rows, depth), BF), pltpu.VMEM(w_qkv.shape, BF), pltpu.VMEM(w_o.shape, BF),
+         pltpu.VMEM((2, tile, depth), BF), pltpu.VMEM((n_rows, head), F32), pltpu.VMEM((n_rows, head), F32),
+         pltpu.SemaphoreType.DMA((n_tiles,)), pltpu.SemaphoreType.DMA, pltpu.SemaphoreType.DMA,
+         pltpu.SemaphoreType.DMA((2,))],
+    )(cot, w_qkv, w_o, *rest)
+
+
+def aligned(offset):
+    return pl.multiple_of(offset, 128)
+
+
+def act_cotangent(pieces, offsets, seq, w_down, tile):
+    width, depth = w_down.shape
+    n_rows = sum(p.shape[1] for p in pieces)
+
+    def body(off_ref, *refs):
+        p_refs, w_ref, out = refs[:-2], refs[-2], refs[-1]
+        rhs = w_ref[...]
+        groups = [[0], [1], [2], [3, 4]]
+        for group in groups:
+            vals = dot(join([p_refs[g][...] for g in group], 0), rhs, NT).astype(BF)
+            at = 0
+            for g in group:
+                size = p_refs[g].shape[0]
+                out[pl.ds(aligned(off_ref[g]), size), :] = vals[at:at + size]
+                at += size
+
+    p_specs = [pl.BlockSpec((None,) + p.shape[1:], lambda i: (seq, 0, 0), pipeline_mode=pl.Buffered(1)) for p in pieces]
+    return call(
+        body, (pl.cdiv(width, tile),),
+        [pl.BlockSpec(memory_space=pltpu.SMEM)] + p_specs + [pl.BlockSpec((tile, depth), lambda i: (i, 0))],
+        pl.BlockSpec((n_rows, tile), lambda i: (0, i)), jax.ShapeDtypeStruct((n_rows, width), BF),
+        2 * n_rows * depth * width, 2 * (n_rows * depth + depth * width + n_rows * width),
+    )(offsets, *pieces, w_down)
+
+
+def down_grad(acts, pieces, offsets, tile):
+    n_seq = len(acts)
+    n_tok, width = acts[0].shape
+    depth = pieces[0].shape[2]
+
+    def body(off_ref, *refs):
+        z_refs, p_refs, out = refs[:n_seq], refs[n_seq:-1], refs[-1]
+        left = join([z[pl.ds(aligned(off_ref[g]), p.shape[1]), :] for z in z_refs for g, p in enumerate(p_refs)], 0)
+        right = join([p[s] for s in range(n_seq) for p in p_refs], 0)
+        out[...] = dot(left, right, TN).astype(BF)
+
+    p_specs = [pl.BlockSpec(p.shape[:2] + (tile,), lambda i: (0, 0, i)) for p in pieces]
+    return call(
+        body, (depth // tile,),
+        [pl.BlockSpec(memory_space=pltpu.SMEM)] + [whole(z) for z in acts] + p_specs,
+        pl.BlockSpec((width, tile), lambda i: (0, i)), jax.ShapeDtypeStruct((width, depth), BF),
+        2 * n_seq * n_tok * width * depth, 2 * (n_seq * n_tok * (width + depth) + width * depth),
+    )(offsets, *acts, *pieces)
 
 
 def gated_mlp(acts, w_gate, w_up, d_act):
@@ -225,11 +316,11 @@
     return call(
         body, (width // tile,), [whole(acts), w_spec, w_spec, o_spec], [o_spec] * 3,
         [jax.ShapeDtypeStruct((n_rows, width), BF)] * 3,
-        4 * n_rows * depth * width, 2 * (n_rows * depth + 2 * depth * width + 4 * n_rows * width), "gated_mlp",
+        4 * n_rows * depth * width, 2 * (n_rows * depth + 2 * depth * width + 4 * n_rows * width),
     )(acts, w_gate, w_up, d_act)
 
 
-def weight_grad(lhs, rhs_groups, out_widths, tile, name, stream):
+def weight_grad(lhs, rhs_groups, out_widths, tile, stream):
     n_seq, n_tok = len(lhs), lhs[0].shape[0]
     n_out = lhs[0].shape[1]
     rhs = [r for group in rhs_groups for r in group]
@@ -259,7 +350,7 @@
     return call(
         body, grid, l_specs + r_specs, o_specs,
         [jax.ShapeDtypeStruct((n_out, w), BF) for w in out_widths],
-        2 * n_seq * n_tok * n_out * total, 2 * (n_seq * n_tok * (n_out + total) + n_out * total), name,
+        2 * n_seq * n_tok * n_out * total, 2 * (n_seq * n_tok * (n_out + total) + n_out * total),
     )(*lhs, *rhs)
 
 
@@ -316,9 +407,9 @@
     def local_step(x_in, positions, w_q, w_k, w_v, w_o, w_gate, w_up, w_down, gain_attn, gain_mlp, d_out):
         n_seq = x_in.shape[0]
         seqs = range(n_seq)
-        depth, n_q, head = w_q.shape
+        depth, n_rep, head = w_q.shape
         scale = head ** -0.5
-        wq2, wk2, wv2 = (w.reshape(depth, -1) for w in (w_q, w_k, w_v))
+        w_qkv = jnp.concatenate([w.reshape(depth, -1) for w in (w_q, w_k, w_v)], axis=1)
         wo2 = w_o.reshape(-1, depth)
         cos_t, sin_t = rope_tables(positions, head)
 
@@ -338,63 +429,77 @@
             total = (vals.astype(F32) + proj.astype(F32)).astype(BF)
             return norm(total, gain_mlp) + (total,)
 
-        def project(acts):
-            return qkv_proj(acts, wq2, wk2, wv2)
-
-        def attend(q_raw, k_raw, v_raw, s):
-            return attention_fwd(q_raw, k_raw, v_raw, cos_t[s], sin_t[s], scale)
-
-        def out_proj(acts):
-            return rows_times_weights([acts], [wo2], "nn", 768, "o_proj")
-
-        def act_grad(cot):
-            return rows_times_weights([cot], [w_down], "nt", 1024, "d_act")
-
         def mlp_grad(d_g, d_u):
-            return rows_times_weights([d_g, d_u], [w_gate, w_up], "nt", 768, "d_mlp")
+            return rows_times_weights([d_g, d_u], [w_gate, w_up], "nt", 768)
 
         def down_proj(acts):
-            return rows_times_weights([acts], [w_down], "nn", 768, "down")
+            return rows_times_weights([acts], [w_down], "nn", 768)
 
         def norm_back(cot, pull, skip):
             d_vals, d_gain = pull(cot)
             return skip + d_vals, d_gain
 
-        def attn_grads(cot, s):
-            d_o = rows_times_weights([cot], [wo2], "nt", 256, "d_attn")
-            grads = attention_bwd(attn[s][1], attn[s][2], qkv[s][2], d_o, cos_t[s], sin_t[s], scale)
-            part = rows_times_weights(list(grads), [wq2, wk2, wv2], "nt", 768, "d_normed")
-            return part, grads
-
         def add_out(part, vals):
             return (vals.astype(F32) + part.astype(F32)).astype(BF)
 
         none = [None] * n_seq
-        normed_all, dout_all, qkv, attn, attn_proj, mlp_all = (list(none) for _ in range(6))
-        norm_attn_pull, norm_mlp_pull, hidden, d_act, gated, d_mlp_in = (list(none) for _ in range(6))
+        normed_all, attn, attn_part, attn_proj, mlp_all = (list(none) for _ in range(5))
+        norm_attn_pull, norm_mlp_pull, mlp_in, hidden, d_act, gated, d_mlp_in = (list(none) for _ in range(7))
         down_out, d_hidden, gain_mlp_part, d_hidden_all, d_qkv, d_normed = (list(none) for _ in range(6))
         grad_x, gain_attn_part, y_out = (list(none) for _ in range(3))
 
+        n_chip = n_tp // 2
+        me = lax.axis_index("tp")
+        chip, core = me // 2, me % 2
+        sibling = [(t, t ^ 1) for t in range(n_tp)]
+        onward = [(t, 2 * ((t // 2 + 1 - 2 * (t % 2)) % n_chip) + t % 2) for t in range(n_tp)]
+        share = d_out.shape[1]
+        back = 2 * core - 1
+        offsets = jnp.stack([2 * share * chip, 2 * share * ((chip + back) % n_chip), 2 * share * ((chip - back) % n_chip),
+                             2 * share * ((chip + 2) % n_chip) + share * core,
+                             2 * share * ((chip + 2) % n_chip) + share * (1 - core)]).astype(jnp.int32)
+
+        def pair_up(mine, other):
+            return jnp.where(core == 0, jnp.concatenate([mine, other], axis=1), jnp.concatenate([other, mine], axis=1))
+
+        def own_half(vals):
+            return lax.dynamic_slice_in_dim(vals, core * share, share, axis=1)
+
+        dout_sib = lax.ppermute(d_out, "tp", sibling)
         for s in seqs:
             out, norm_attn_pull[s] = run(norm, x[s], gain_attn)
             normed_all[s] = gather(out)
+        dout_pair = run(pair_up, d_out, dout_sib)
+        dout_near = lax.ppermute(dout_pair, "tp", onward)
         for s in seqs:
-            qkv[s] = run(project, normed_all[s])
-            attn[s] = run(attend, *qkv[s], s)
-            attn_proj[s] = scatter(run(out_proj, attn[s][0]))
-        dout_all[0] = gather(after(d_y[0], *latest))
-        for s in seqs:
-            out, norm_mlp_pull[s], hidden[s] = run(mid_norm, attn_proj[s], x[s])
-            mlp_all[s] = gather(out)
+            attn[s] = run(attention_fwd, normed_all[s], w_qkv, wo2, cos_t[s], sin_t[s], n_rep, head, scale)
+            attn_part[s] = attn[s][4]
+        attn_proj[0] = scatter(attn_part[0])
+        dout_pass = run(own_half, dout_near)
+        dout_far = lax.ppermute(dout_pass, "tp", onward)
+        dout_near2 = lax.ppermute(dout_near, "tp", sibling)
+
+        def mid(s):
+            mlp_in[s], norm_mlp_pull[s], hidden[s] = run(mid_norm, attn_proj[s], x[s])
+            mlp_all[s] = gather(mlp_in[s])
+
+        latest += [dout_far, dout_near2]
+        mid(0)
         for s in seqs[1:]:
-            dout_all[s] = gather(after(d_y[s], *latest))
-
-        def mlp_half(s):
-            d_act[s] = run(act_grad, dout_all[s])
+            attn_proj[s] = scatter(after(attn_part[s], mlp_in[0]))
+        dout_far2 = lax.ppermute(after(dout_far, mlp_in[0]), "tp", sibling)
+        dout_pieces = (dout_pair, dout_near, dout_near2, dout_far, dout_far2)
+
+        def act_grad(s):
+            d_act[s] = run(lambda off: act_cotangent(dout_pieces, off, s, w_down, 512), offsets)
+
+        def mlp_main(s):
             gated[s] = run(gated_mlp, mlp_all[s], w_gate, w_up, d_act[s])
 
-        def mlp_rest(s):
+        def mlp_back(s):
             d_mlp_in[s] = scatter(run(mlp_grad, gated[s][1], gated[s][2]))
+
+        def mlp_down(s):
             down_out[s] = scatter(run(down_proj, gated[s][0]))
 
         def mid_back(s):
@@ -402,31 +507,34 @@
             d_hidden_all[s] = gather(d_hidden[s])
 
         def attn_back(s):
-            part, d_qkv[s] = run(attn_grads, d_hidden_all[s], s)
+            d_qkv[s], part = run(attention_bwd, d_hidden_all[s], w_qkv, wo2, *attn[s][:3], cos_t[s], sin_t[s], scale)
             d_normed[s] = scatter(part)
 
         def last_back(s):
             grad_x[s], gain_attn_part[s] = run(norm_back, d_normed[s], norm_attn_pull[s], d_hidden[s])
 
-        mlp_half(0)
-        mlp_rest(0)
-        mlp_half(1)
+        act_grad(0)
+        mlp_main(0)
+        act_grad(1)
+        mid(1)
+        mlp_back(0)
+        mlp_down(0)
+        mlp_main(1)
         mid_back(0)
-        mlp_rest(1)
+        mlp_back(1)
+        mlp_down(1)
         y_out[0] = run(add_out, down_out[0], hidden[0])
         act_out, d_gate, d_up = zip(*gated)
-        (grad_wdown,) = run(lambda first: weight_grad([first, act_out[1]], [dout_all], (depth,), 768, "g_down", "cols"),
-                            act_out[0])
         attn_back(0)
+        grad_wdown = run(lambda first: down_grad([first, act_out[1]], dout_pieces, offsets, 768), act_out[0])
         mid_back(1)
         grad_wgate, grad_wup = run(lambda first: weight_grad(
-            [first, mlp_all[1]], [d_gate, d_up], (w_gate.shape[1],) * 2, 384, "g_gate_up", "rows"), mlp_all[0])
+            [first, mlp_all[1]], [d_gate, d_up], (w_gate.shape[1],) * 2, 384, "rows"), mlp_all[0])
         attn_back(1)
-        (grad_wo,) = run(lambda first: weight_grad([first, attn[1][0]], [d_hidden_all], (depth,), 768, "g_o", "cols"),
-                         attn[0][0])
-        d_q, d_k, d_v = zip(*d_qkv)
+        (grad_wo,) = run(lambda first: weight_grad([first, attn[1][3]], [d_hidden_all], (depth,), 768, "cols"),
+                         attn[0][3])
         grad_wq, grad_wk, grad_wv = run(lambda first: weight_grad(
-            [first, normed_all[1]], [d_q, d_k, d_v], tuple(w.shape[1] for w in (wq2, wk2, wv2)), 384, "g_qkv", "rows"),
+            [first, normed_all[1]], [d_qkv], tuple(w[0].size for w in (w_q, w_k, w_v)), 384, "rows"),
             normed_all[0])
         last_back(0)
         y_out[1] = run(add_out, down_out[1], hidden[1])

time: 816 us -> 814 us (level)
  waiting for transfers between devices: 210 us -> 196 us
  other arithmetic: 36.5 us -> 46.2 us
    pallas_call x6 -> x7, Pallas kernels: 56.1 us -> 205 us  [the longest x2 63.2 us: attention_fwd(): call(body, (1,), [any_spec] * 3 + [whole(cos_t), whole(sin_t)], [whole(o)...]
    pallas_call x12 -> x4, Pallas kernels: 228 us -> 120 us  [rows_times_weights(): call(body, grid, [whole(a) for a in acts] + w_specs, pl.BlockSpec((n_rows...]
    ppermute x0 -> x5, waiting for transfers between devices: none -> 105 us  [the longest x1 76.2 us: local_step(): dout_near = lax.ppermute(dout_pair, 'tp', onward)]
    reduce_scatter x8, waiting for transfers between devices: 95.6 us -> 32.5 us  [scatter(): return lax.psum_scatter(part, 'tp', scatter_dimension=0, tiled=True)]
    all_gather x8 -> x6, waiting for transfers between devices: 112 us -> 56.2 us  [gather(): return lax.all_gather(part, 'tp', axis=0, tiled=True)]
    pallas_call x4 -> x3, Pallas kernels: 144 us -> 107 us  [weight_grad(): call(body, grid, l_specs + r_specs, o_specs, [jax.ShapeDtypeStruct((n_out...]
  transfers between devices with their start and end apart: 16 -> 19, of which waited for: 7 -> 7; matrix products, arithmetic and copies ran while one was open for 5% -> 5% of each run, Pallas kernels for 63% -> 64%
where the time goes in v2:
time: 814 us; the launch traced here: 807 us
  Pallas kernels  523 us (64%)
  waiting for transfers between devices  196 us (24%)
  other arithmetic  46.2 us (6%)
  local copies, waits for them, and re-layouts  24.5 us (3%)
  between operations  14.8 us (2%)
    pallas_call x4, Pallas kernels, rows_times_weights(): call(body, grid, [whole(a) for a in acts] + w_specs, pl.BlockSpec((n_rows...  120 us
    pallas_call x3, Pallas kernels, weight_grad(): call(body, grid, l_specs + r_specs, o_specs, [jax.ShapeDtypeStruct((n_out...  107 us
    pallas_call x2, Pallas kernels, gated_mlp(): call(body, (width // tile,), [whole(acts), w_spec, w_spec, o_spec], [o_sp...  82.1 us
    ppermute x1, waiting for transfers between devices, local_step(): dout_near = lax.ppermute(dout_pair, 'tp', onward)  76.2 us
    pallas_call x2, Pallas kernels, attention_fwd(): call(body, (1,), [any_spec] * 3 + [whole(cos_t), whole(sin_t)], [whole(o)...  63.2 us
    pallas_call x2, Pallas kernels, attention_bwd(): call(body, (1,), [any_spec] * 3 + [whole(r) for r in rest], [whole(outs[0...  57.7 us
    all_gather x6, waiting for transfers between devices, gather(): return lax.all_gather(part, 'tp', axis=0, tiled=True)  56.2 us
    pallas_call x2, Pallas kernels, act_cotangent(): call(body, (pl.cdiv(width, tile),), [pl.BlockSpec(memory_space=pltpu.SMEM...  45.7 us
  transfers between devices with their start and end apart: 19, of which 7 were waited for; matrix products, arithmetic and copies ran while one was open for 5% of the time, Pallas kernels for 64%

profile of v2, /device:TPU:112, one launch (start us, length us, event | category | flops | bytes accessed | tf_op | source)
XLA Modules:
  0.0 807.1 jit_solution(9764395237836216354)
XLA Ops:
  7.3 0.7 broadcast_add_fusion.1
  8.0 1.6 slice_bitcast_fusion.1
  9.9 0.8 copy-done.32
  10.7 0.6 copy-done.26
  11.3 1.2 fusion.11
  14.0 1.2 fusion.10
  15.5 2.8 copy.23
  18.3 3.7 multiply_sine_fusion
  22.0 1.4 slice_bitcast_fusion.2
  23.5 1.0 copy-done.16
  24.5 0.6 copy-done.17
  25.0 3.8 pad_maximum_fusion.w_hbm
  28.8 4.7 maximum_select_fusion.refs_0_.refs_2_
  33.5 25.5 %all-gather.7.cloned.1.call-done.acts_hbm.refs_0_ = bf16[1024,3840]{1,0:T(8,128)(2,1)} async-done(((bf16[128,3840]{1,0:T(8,128)(2,1)}), bf16[1024,3840]{1,0:T(8,128)(2,1)}) %all-gather.7.cloned.1.call-update) | async-done | bytes 7864336 | tf_op jit(solution)/shard_map/all_gather | solution.py:402
  59.0 36.6 %shard_map.203 = (bf16[1024,512]{1,0:T(8,128)(2,1)}, bf16[1024,256]{1,0:T(8,128)(2,1)}, bf16[1024,256]{1,0:T(8,128)(2,1)}, bf16[1024,512]{1,0:T(8,128)(2,1)}, bf16[1024,3840]{1,0:T(8,128)(2,1)}) custom-call(bf16[1024,3840]{1,0:T(8,128)(2,1)} %all-gather.7.cloned.1.call-done.acts_hbm.refs_0_, bf16[3840,1024]{1,0:T(8,128)(2,1)} %pad_maximum_fusion.w_hbm, ...), custom_call_target="tpu_custom_call" | custom-call | flops 16079595520 | bytes 27525120 | tf_op jit(solution)/shard_map/pallas_call | solution.py:166
  95.7 0.7 collective-permute-start.1
  96.4 76.2 %collective-permute-done.1.refs_1_.refs_3_ = bf16[2,256,3840]{2,1,0:T(8,128)(2,1)} collective-permute-done((bf16[2,256,3840]{2,1,0:T(8,128)(2,1)}, bf16[2,256,3840]{2,1,0:T(8,128)(2,1)}, u32[]{:S(2)}, u32[]{:S(2)}) %collective-permute-start.1) | collective-permute-done | bytes 3932192 | tf_op jit(solution)/shard_map/ppermute | solution.py:473
  172.6 26.7 %shard_map.204 = (bf16[1024,512]{1,0:T(8,128)(2,1)}, bf16[1024,256]{1,0:T(8,128)(2,1)}, bf16[1024,256]{1,0:T(8,128)(2,1)}, bf16[1024,512]{1,0:T(8,128)(2,1)}, bf16[1024,3840]{1,0:T(8,128)(2,1)}) custom-call(bf16[1024,3840]{1,0:T(8,128)(2,1)} %all-gather.9.cloned.1.call-done.acts_hbm.refs_1_, bf16[3840,1024]{1,0:T(8,128)(2,1)} %pad_maximum_fusion.w_hbm, ...), custom_call_target="tpu_custom_call" | custom-call | flops 16079595520 | bytes 27525120 | tf_op jit(solution)/shard_map/pallas_call | solution.py:166
  199.3 1.8 constant_dynamic-slice_fusion
  201.1 1.2 collective-permute-start.2
  202.3 24.8 %collective-permute-done.2.refs_3_.refs_5_ = bf16[2,128,3840]{2,1,0:T(8,128)(2,1)} collective-permute-done((bf16[2,128,3840]{2,1,0:T(8,128)(2,1)S(1)}, bf16[2,128,3840]{2,1,0:T(8,128)(2,1)}, u32[]{:S(2)}, u32[]{:S(2)}) %collective-permute-start.2) | collective-permute-done | bytes 1966112 | tf_op jit(solution)/shard_map/ppermute | solution.py:479
  227.1 1.6 fusion.24
  229.3 1.2 fusion.9
  230.7 0.6 reduce-scatter.11.cloned.1.call-update
  231.5 0.6 stack.46.off_ref
  232.1 3.6 collective-permute-done.4.refs_4_.refs_6_
  235.7 23.1 %shard_map.205.dz_ref = bf16[1024,1920]{1,0:T(8,128)(2,1)} custom-call(s32[5]{0:T(128)} %stack.46.off_ref, bf16[2,256,3840]{2,1,0:T(8,128)(2,1)} %maximum_select_fusion.refs_0_.refs_2_, bf16[2,256,3840]{2,1,0:T(8,128)(2,1)} %collective-permute-done.1.refs_1_.refs_3_, bf16[2,256,3840]{2,1,0:T(8,128)(2,1)} %collective-permute-done.3.refs_2_.refs_4_, ...), custom_call_target="tpu_custom_call" | custom-call | flops 15099494400 | bytes 26542080 | tf_op jit(solution)/shard_map/pallas_call | solution.py:264
  258.9 14.7 %all-gather.11.cloned.1.call-done.a_ref.refs_0_ = bf16[1024,3840]{1,0:T(8,128)(2,1)} async-done(((bf16[128,3840]{1,0:T(8,128)(2,1)}), bf16[1024,3840]{1,0:T(8,128)(2,1)}) %all-gather.11.cloned.1.call-update) | async-done | bytes 7864336 | tf_op jit(solution)/shard_map/all_gather | solution.py:402
  273.6 40.8 %shard_map.206 = (bf16[1024,1920]{1,0:T(8,128)(2,1)}, bf16[1024,1920]{1,0:T(8,128)(2,1)}, bf16[1024,1920]{1,0:T(8,128)(2,1)}) custom-call(bf16[1024,3840]{1,0:T(8,128)(2,1)} %all-gather.11.cloned.1.call-done.a_ref.refs_0_, bf16[3840,1920]{1,0:T(8,128)(2,1)} %refs_2_.3, bf16[3840,1920]{1,0:T(8,128)(2,1)} %refs_3_.3, bf16[1024,1920]{1,0:T(8,128)(2,1)} %shard_map.205.dz_ref), custom_call_target="tpu_custom_call" | custom-call | flops 30198988800 | bytes 53084160 | tf_op jit(solution)/shard_map/pallas_call | solution.py:316
  314.4 22.6 %shard_map.207.dz_ref = bf16[1024,1920]{1,0:T(8,128)(2,1)} custom-call(s32[5]{0:T(128)} %stack.46.off_ref, bf16[2,256,3840]{2,1,0:T(8,128)(2,1)} %maximum_select_fusion.refs_0_.refs_2_, bf16[2,256,3840]{2,1,0:T(8,128)(2,1)} %collective-permute-done.1.refs_1_.refs_3_, bf16[2,256,3840]{2,1,0:T(8,128)(2,1)} %collective-permute-done.3.refs_2_.refs_4_, ...), custom_call_target="tpu_custom_call" | custom-call | flops 15099494400 | bytes 26542080 | tf_op jit(solution)/shard_map/pallas_call | solution.py:264
  336.9 1.6 fusion.27
  339.6 1.2 fusion.8
  341.0 38.0 %shard_map.208 = bf16[1024,3840]{1,0:T(8,128)(2,1)} custom-call(bf16[1024,1920]{1,0:T(8,128)(2,1)} %get-tuple-element.83.refs_0_.refs_2_, bf16[1024,1920]{1,0:T(8,128)(2,1)} %get-tuple-element.84.refs_1_.refs_4_, bf16[3840,1920]{1,0:T(8,128)(2,1)} %refs_2_.3, bf16[3840,1920]{1,0:T(8,128)(2,1)} %refs_3_.3), custom_call_target="tpu_custom_call" | custom-call | flops 30198988800 | bytes 45219840 | tf_op jit(solution)/shard_map/pallas_call | solution.py:87
  379.2 21.4 %shard_map.209 = bf16[1024,3840]{1,0:T(8,128)(2,1)} custom-call(bf16[1024,1920]{1,0:T(8,128)(2,1)} %get-tuple-element.100.refs_0_, bf16[1920,3840]{1,0:T(8,128)(2,1)} %refs_1_.3), custom_call_target="tpu_custom_call" | custom-call | flops 15099494400 | bytes 26542080 | tf_op jit(solution)/shard_map/pallas_call | solution.py:87
  400.7 41.3 %shard_map.210 = (bf16[1024,1920]{1,0:T(8,128)(2,1)}, bf16[1024,1920]{1,0:T(8,128)(2,1)}, bf16[1024,1920]{1,0:T(8,128)(2,1)}) custom-call(bf16[1024,3840]{1,0:T(8,128)(2,1)} %all-gather.13.cloned.1.call-done.a_ref.refs_1_, bf16[3840,1920]{1,0:T(8,128)(2,1)} %refs_2_.3, bf16[3840,1920]{1,0:T(8,128)(2,1)} %refs_3_.3, bf16[1024,1920]{1,0:T(8,128)(2,1)} %shard_map.207.dz_ref), custom_call_target="tpu_custom_call" | custom-call | flops 30198988800 | bytes 53084160 | tf_op jit(solution)/shard_map/pallas_call | solution.py:316
  442.0 2.7 fusion.12
  444.8 2.9 fusion.34
  447.8 37.9 %shard_map.211 = bf16[1024,3840]{1,0:T(8,128)(2,1)} custom-call(bf16[1024,1920]{1,0:T(8,128)(2,1)} %get-tuple-element.90.refs_0_.refs_3_, bf16[1024,1920]{1,0:T(8,128)(2,1)} %get-tuple-element.91.refs_1_.refs_5_, bf16[3840,1920]{1,0:T(8,128)(2,1)} %refs_2_.3, bf16[3840,1920]{1,0:T(8,128)(2,1)} %refs_3_.3), custom_call_target="tpu_custom_call" | custom-call | flops 30198988800 | bytes 45219840 | tf_op jit(solution)/shard_map/pallas_call | solution.py:87
  485.8 22.3 %shard_map.212 = bf16[1024,3840]{1,0:T(8,128)(2,1)} custom-call(bf16[1024,1920]{1,0:T(8,128)(2,1)} %get-tuple-element.92.refs_0_.refs_1_, bf16[1920,3840]{1,0:T(8,128)(2,1)} %refs_1_.3), custom_call_target="tpu_custom_call" | custom-call | flops 15099494400 | bytes 26542080 | tf_op jit(solution)/shard_map/pallas_call | solution.py:87
  508.1 2.4 fusion.26
  510.5 16.0 %all-gather.15.cloned.1.call-done.cot_hbm.refs_2_ = bf16[1024,3840]{1,0:T(8,128)(2,1)} async-done(((bf16[128,3840]{1,0:T(8,128)(2,1)}), bf16[1024,3840]{1,0:T(8,128)(2,1)}) %all-gather.15.cloned.1.call-update) | async-done | bytes 7864336 | tf_op jit(solution)/shard_map/all_gather | solution.py:402
  526.5 28.6 %shard_map.213 = (bf16[1024,1024]{1,0:T(8,128)(2,1)}, bf16[1024,3840]{1,0:T(8,128)(2,1)}) custom-call(bf16[1024,3840]{1,0:T(8,128)(2,1)} %all-gather.15.cloned.1.call-done.cot_hbm.refs_2_, bf16[3840,1024]{1,0:T(8,128)(2,1)} %pad_maximum_fusion.w_hbm, bf16[512,3840]{1,0:T(8,128)(2,1)} %bitcast.49, bf16[1024,512]{1,0:T(8,128)(2,1)} %get-tuple-element.69.q, ...), custom_call_target="tpu_custom_call" | custom-call | flops 20079595520 | bytes 27525120 | tf_op jit(solution)/shard_map/pallas_call | solution.py:233
  555.1 38.7 %shard_map.214 = bf16[1920,3840]{1,0:T(8,128)(2,1)} custom-call(s32[5]{0:T(128)} %stack.46.off_ref, bf16[1024,1920]{1,0:T(8,128)(2,1)} %get-tuple-element.100.refs_0_, bf16[1024,1920]{1,0:T(8,128)(2,1)} %get-tuple-element.92.refs_0_.refs_1_, bf16[2,256,3840]{2,1,0:T(8,128)(2,1)} %maximum_select_fusion.refs_0_.refs_2_, ...), custom_call_target="tpu_custom_call" | custom-call | flops 30198988800 | bytes 38338560 | tf_op jit(solution)/shard_map/pallas_call | solution.py:284
  593.8 2.1 fusion.13
  596.0 2.8 fusion.33
  599.0 0.6 reduce-scatter.19.cloned.1.call-update
  599.6 0.7 reduce-scatter.17.cloned.1.call-update
  600.4 71.8 %shard_map.215 = (bf16[3840,1920]{1,0:T(8,128)(2,1)}, bf16[3840,1920]{1,0:T(8,128)(2,1)}) custom-call(bf16[1024,3840]{1,0:T(8,128)(2,1)} %all-gather.11.cloned.1.call-done.a_ref.refs_0_, bf16[1024,3840]{1,0:T(8,128)(2,1)} %all-gather.13.cloned.1.call-done.a_ref.refs_1_, bf16[1024,1920]{1,0:T(8,128)(2,1)} %get-tuple-element.83.refs_0_.refs_2_, ...), custom_call_target="tpu_custom_call" | custom-call | flops 60397977600 | bytes 60948480 | tf_op jit(solution)/shard_map/pallas_call | solution.py:350
  672.2 29.1 %shard_map.216 = (bf16[1024,1024]{1,0:T(8,128)(2,1)}, bf16[1024,3840]{1,0:T(8,128)(2,1)}) custom-call(bf16[1024,3840]{1,0:T(8,128)(2,1)} %all-gather.17.cloned.1.call-done.cot_hbm.refs_3_, bf16[3840,1024]{1,0:T(8,128)(2,1)} %pad_maximum_fusion.w_hbm, bf16[512,3840]{1,0:T(8,128)(2,1)} %bitcast.50, bf16[1024,512]{1,0:T(8,128)(2,1)} %get-tuple-element.71.q, ...), custom_call_target="tpu_custom_call" | custom-call | flops 20079595520 | bytes 27525120 | tf_op jit(solution)/shard_map/pallas_call | solution.py:233
  701.4 0.6 copy-done.20
  702.1 13.5 %shard_map.217 = bf16[512,3840]{1,0:T(8,128)(2,1)} custom-call(bf16[1024,512]{1,0:T(8,128)(2,1)} %get-tuple-element.108.refs_0_, bf16[1024,512]{1,0:T(8,128)(2,1)} %get-tuple-element.109.refs_1_, bf16[1024,3840]{1,0:T(8,128)(2,1)} %all-gather.15.cloned.1.call-done.cot_hbm.refs_2_, bf16[1024,3840]{1,0:T(8,128)(2,1)} %all-gather.17.cloned.1.call-done.cot_hbm.refs_3_), custom_call_target="tpu_custom_call" | custom-call | flops 8053063680 | bytes 21757952 | tf_op jit(solution)/shard_map/pallas_call | solution.py:350
  715.6 22.0 %shard_map.218 = (bf16[3840,512]{1,0:T(8,128)(2,1)}, bf16[3840,256]{1,0:T(8,128)(2,1)}, bf16[3840,256]{1,0:T(8,128)(2,1)}) custom-call(bf16[1024,3840]{1,0:T(8,128)(2,1)} %all-gather.7.cloned.1.call-done.acts_hbm.refs_0_, bf16[1024,3840]{1,0:T(8,128)(2,1)} %all-gather.9.cloned.1.call-done.acts_hbm.refs_1_, bf16[1024,1024]{1,0:T(8,128)(2,1)} %get-tuple-element.99.refs_2_, ...), custom_call_target="tpu_custom_call" | custom-call | flops 16106127360 | bytes 27787264 | tf_op jit(solution)/shard_map/pallas_call | solution.py:350
  737.7 9.3 %reshape.150 = bf16[3840,2,256]{2,1,0:T(2,128)(2,1)} reshape(bf16[3840,512]{1,0:T(8,128)(2,1)} %get-tuple-element.111) | data formatting | bytes 7864320 | tf_op jit(solution)/shard_map/reshape | solution.py:545
  747.1 2.1 fusion.14
  749.2 1.6 fusion.32
  750.9 1.5 fusion.29
  752.4 1.4 pad_maximum_fusion.1
  753.9 32.4 %reduce-scatter.23.cloned.1.call-done = bf16[128,3840]{1,0:T(8,128)(2,1)} async-done(((bf16[1024,3840]{1,0:T(8,128)(2,1)}), bf16[128,3840]{1,0:T(8,128)(2,1)}) %reduce-scatter.23.cloned.1.call-update) | async-done | bytes 983056 | tf_op jit(solution)/shard_map/reduce_scatter | solution.py:405
  786.3 2.0 fusion.15
  788.3 0.6 pad_maximum_fusion.3.x_ref
  789.0 8.5 %tp_sum.1 = f32[2,3840]{1,0:T(2,128)} custom-call(f32[2,3840]{1,0:T(2,128)} %pad_maximum_fusion.3.x_ref), custom_call_target="tpu_custom_call" | custom-call | flops 5000000000 | bytes 1000000 | tf_op jit(solution)/shard_map/tp_sum/pallas_call | solution.py:379
  797.5 0.7 fusion.31
  798.2 0.7 slice_reduce_fusion
  798.9 1.4 pad_maximum_fusion.2
  (128 shorter events, 5.3 us)
Async XLA Ops:
  7.2 51.8 %all-gather.7.cloned.1.call-start = ((), (), s32[]{:S(2)}) async-start(), calls=%async_computation.8 | async-start | bytes 8847360 | tf_op jit(solution)/shard_map/all_gather | solution.py:402
  8.0 5.5 copy-start.18
  9.6 1.1 copy-start.2
  9.6 3.9 copy-start
  9.9 0.8 copy-start.32
  10.7 0.6 copy-start.26
  12.6 160.0 %all-gather.9.cloned.1.call-start = ((), (), s32[]{:S(2)}) async-start(), calls=%async_computation.10 | async-start | bytes 8847360 | tf_op jit(solution)/shard_map/all_gather | solution.py:402
  12.6 2.8 copy-start.9
  12.6 2.9 copy-start.23
  12.9 0.5 copy-start.30
  13.5 0.5 copy-start.24
  15.3 211.8 %reduce-scatter.9.cloned.1.call-start = ((), (), s32[]{:S(2)}) async-start(), calls=%async_computation.9 | async-start | bytes 8847360 | tf_op jit(solution)/shard_map/reduce_scatter | solution.py:405
  15.4 13.4 %collective-permute-start = (bf16[2,128,3840]{2,1,0:T(8,128)(2,1)S(1)}, bf16[2,128,3840]{2,1,0:T(8,128)(2,1)}, u32[]{:S(2)}, u32[]{:S(2)}) collective-permute-start(bf16[2,128,3840]{2,1,0:T(8,128)(2,1)S(1)} %copy-done.9), channel_id=1, source_target_pairs={{0,1},{1,0},{2,3},{3,2},{4,5},{5,4},{6,7},{7,6},{8,9},{9,8},{10,11... | collective-permute-start | bytes 5898248 | tf_op jit(solution)/shard_map/ppermute | solution.py:468
  22.0 2.4 copy-start.16
  22.0 3.0 copy-start.17
  95.6 177.9 %all-gather.11.cloned.1.call-start = ((), (), s32[]{:S(2)}) async-start(), calls=%async_computation.11 | async-start | bytes 8847360 | tf_op jit(solution)/shard_map/all_gather | solution.py:402
  95.7 76.9 %collective-permute-start.1 = (bf16[2,256,3840]{2,1,0:T(8,128)(2,1)}, bf16[2,256,3840]{2,1,0:T(8,128)(2,1)}, u32[]{:S(2)}, u32[]{:S(2)}) collective-permute-start(bf16[2,256,3840]{2,1,0:T(8,128)(2,1)} %maximum_select_fusion.refs_0_.refs_2_), channel_id=1, source_target_pairs={{0,2},{1,7},{2,4},{3,1},{4,6},{5,3},{6,0},{7,5},{8,10},{9,15},{10,... | collective-permute-start | bytes 11796488 | tf_op jit(solution)/shard_map/ppermute | solution.py:473
  172.6 29.7 %collective-permute-start.3 = (bf16[2,256,3840]{2,1,0:T(8,128)(2,1)}, bf16[2,256,3840]{2,1,0:T(8,128)(2,1)}, u32[]{:S(2)}, u32[]{:S(2)}) collective-permute-start(bf16[2,256,3840]{2,1,0:T(8,128)(2,1)} %collective-permute-done.1.refs_1_.refs_3_), channel_id=1, source_target_pairs={{0,1},{1,0},{2,3},{3,2},{4,5},{5,4},{6,7},{7,6},{8,9},{9,8},{10,11... | collective-permute-start | bytes 11796488 | tf_op jit(solution)/shard_map/ppermute | solution.py:480
  199.3 3.0 copy-start.22
  199.3 27.9 %copy-start.8 = (bf16[2,128,3840]{2,1,0:T(8,128)(2,1)S(1)}, bf16[2,128,3840]{2,1,0:T(8,128)(2,1)}, u32[]{:S(2)}) copy-start(bf16[2,128,3840]{2,1,0:T(8,128)(2,1)} %param.12) | copy-start | bytes 5898244
  201.1 26.0 %collective-permute-start.2 = (bf16[2,128,3840]{2,1,0:T(8,128)(2,1)S(1)}, bf16[2,128,3840]{2,1,0:T(8,128)(2,1)}, u32[]{:S(2)}, u32[]{:S(2)}) collective-permute-start(bf16[2,128,3840]{2,1,0:T(8,128)(2,1)S(1)} %constant_dynamic-slice_fusion), channel_id=1, source_target_pairs={{0,2},{1,7},{2,4},{3,1},{4,6},{5,3},{6,0},{7,5},{8,10},{9,15},{10,... | collective-permute-start | bytes 5898248 | tf_op jit(solution)/shard_map/ppermute | solution.py:479
  228.8 0.5 copy-start.34
  230.6 106.3 %reduce-scatter.11.cloned.1.call-start = ((), (), s32[]{:S(2)}) async-start(), calls=%async_computation.12 | async-start | bytes 8847360 | tf_op jit(solution)/shard_map/reduce_scatter | solution.py:405
  231.3 169.4 %all-gather.13.cloned.1.call-start = ((), (), s32[]{:S(2)}) async-start(), calls=%async_computation.14 | async-start | bytes 8847360 | tf_op jit(solution)/shard_map/all_gather | solution.py:402
  231.3 4.4 collective-permute-start.4
  338.6 0.5 copy-start.36
  338.6 1.0 copy-start.4
  339.1 0.5 copy-start.28
  340.9 101.1 %reduce-scatter.15.cloned.1.call-start = ((), (), s32[]{:S(2)}) async-start(), calls=%async_computation.15 | async-start | bytes 8847360 | tf_op jit(solution)/shard_map/reduce_scatter | solution.py:405
  379.1 129.0 %reduce-scatter.13.cloned.1.call-start = ((), (), s32[]{:S(2)}) async-start(), calls=%async_computation.13 | async-start | bytes 8847360 | tf_op jit(solution)/shard_map/reduce_scatter | solution.py:405
  400.6 125.9 %all-gather.15.cloned.1.call-start = ((), (), s32[]{:S(2)}) async-start(), calls=%async_computation.17 | async-start | bytes 8847360 | tf_op jit(solution)/shard_map/all_gather | solution.py:402
  442.0 2.8 copy-start.35
  442.0 2.8 copy-start.10
  447.7 146.1 %reduce-scatter.21.cloned.1.call-start = ((), (), s32[]{:S(2)}) async-start(), calls=%async_computation.19 | async-start | bytes 8847360 | tf_op jit(solution)/shard_map/reduce_scatter | solution.py:405
  485.7 186.5 %all-gather.17.cloned.1.call-start = ((), (), s32[]{:S(2)}) async-start(), calls=%async_computation.20 | async-start | bytes 8847360 | tf_op jit(solution)/shard_map/all_gather | solution.py:402
  555.1 38.7 %copy-start.5 = (bf16[128,3840]{1,0:T(8,128)(2,1)S(1)}, bf16[128,3840]{1,0:T(8,128)(2,1)}, u32[]{:S(2)}) copy-start(bf16[128,3840]{1,0:T(8,128)(2,1)} %copy-done.4) | copy-start | bytes 2949124
  555.1 38.7 %copy-start.29 = (f32[128]{0:T(128)S(1)}, f32[128]{0:T(128)}, u32[]{:S(2)}) copy-start(f32[128]{0:T(128)} %copy-done.28) | copy-start | bytes 1540
  593.8 2.2 copy-start.37
  593.8 2.2 copy-start.11
  598.9 148.1 %reduce-scatter.19.cloned.1.call-start = ((), (), s32[]{:S(2)}) async-start(), calls=%async_computation.18 | async-start | bytes 8847360 | tf_op jit(solution)/shard_map/reduce_scatter | solution.py:405
  599.5 151.3 %reduce-scatter.17.cloned.1.call-start = ((), (), s32[]{:S(2)}) async-start(), calls=%async_computation.16 | async-start | bytes 8847360 | tf_op jit(solution)/shard_map/reduce_scatter | solution.py:405
  600.3 185.9 %reduce-scatter.23.cloned.1.call-start = ((), (), s32[]{:S(2)}) async-start(), calls=%async_computation.21 | async-start | bytes 8847360 | tf_op jit(solution)/shard_map/reduce_scatter | solution.py:405
  701.3 0.7 copy-start.20
  737.7 9.3 %copy-start.3 = (bf16[128,3840]{1,0:T(8,128)(2,1)S(1)}, bf16[128,3840]{1,0:T(8,128)(2,1)}, u32[]{:S(2)}) copy-start(bf16[128,3840]{1,0:T(8,128)(2,1)} %copy-done.2) | copy-start | bytes 2949124
  737.7 9.3 %copy-start.19 = (f32[3840]{0:T(1024)S(1)}, f32[3840]{0:T(1024)}, u32[]{:S(2)}) copy-start(f32[3840]{0:T(1024)} %copy-done.18) | copy-start | bytes 46084
  737.7 9.4 %copy-start.27 = (f32[128]{0:T(128)S(1)}, f32[128]{0:T(128)}, u32[]{:S(2)}) copy-start(f32[128]{0:T(128)} %copy-done.26) | copy-start | bytes 1540
  747.0 2.2 copy-start.33
  747.0 2.2 copy-start.6
  747.0 2.2 copy-start.12
  750.9 1.5 copy-start.14
  752.4 33.9 %copy-start.1 = (bf16[128,3840]{1,0:T(8,128)(2,1)S(1)}, bf16[128,3840]{1,0:T(8,128)(2,1)}, u32[]{:S(2)}) copy-start(bf16[128,3840]{1,0:T(8,128)(2,1)} %copy-done) | copy-start | bytes 2949124
  752.4 33.9 %copy-start.25 = (f32[128]{0:T(128)S(1)}, f32[128]{0:T(128)}, u32[]{:S(2)}) copy-start(f32[128]{0:T(128)} %copy-done.24) | copy-start | bytes 1540
  788.9 8.5 %copy-start.31 = (f32[128]{0:T(128)S(1)}, f32[128]{0:T(128)}, u32[]{:S(2)}) copy-start(f32[128]{0:T(128)} %copy-done.30) | copy-start | bytes 1540
  788.9 8.5 %copy-start.7 = (bf16[128,3840]{1,0:T(8,128)(2,1)S(1)}, bf16[128,3840]{1,0:T(8,128)(2,1)}, u32[]{:S(2)}) copy-start(bf16[128,3840]{1,0:T(8,128)(2,1)} %fusion.33) | copy-start | bytes 2949124
  788.9 8.5 %copy-start.13 = (bf16[128,3840]{1,0:T(8,128)(2,1)S(1)}, bf16[128,3840]{1,0:T(8,128)(2,1)}, u32[]{:S(2)}) copy-start(bf16[128,3840]{1,0:T(8,128)(2,1)} %reduce-scatter.23.cloned.1.call-done) | copy-start | bytes 2949124
  797.5 0.8 copy-start.21
  797.5 1.4 copy-start.15
Sparse Core Ops, SparseCore 0:
  12.7 46.2 all-gather.6
  61.1 44.6 all-gather.8
  108.7 74.5 reduce-scatter.8
  230.7 42.7 all-gather.10
  276.3 46.0 reduce-scatter.10
  341.1 43.4 all-gather.12
  387.5 46.0 reduce-scatter.14
  436.4 45.4 reduce-scatter.12
  483.5 42.9 all-gather.14
  529.2 46.0 reduce-scatter.20
  599.0 43.5 all-gather.16
  644.7 46.0 reduce-scatter.18
  693.1 45.4 reduce-scatter.16
  740.7 45.4 reduce-scatter.22

commit v3 on v2

--- a/solution.py
+++ b/solution.py
@@ -244,29 +244,38 @@
     return pl.multiple_of(offset, 128)
 
 
-def act_cotangent(pieces, offsets, seq, w_down, tile):
+def act_cotangent(pieces, offsets, seq, w_down, gate, up, tile):
     width, depth = w_down.shape
     n_rows = sum(p.shape[1] for p in pieces)
+    n_pieces = len(pieces)
 
     def body(off_ref, *refs):
-        p_refs, w_ref, out = refs[:-2], refs[-2], refs[-1]
+        p_refs, (w_ref, g_ref, u_ref, dg_ref, du_ref) = refs[:n_pieces], refs[n_pieces:]
         rhs = w_ref[...]
-        groups = [[0], [1], [2], [3, 4]]
-        for group in groups:
+        for group in ([0], [1], [2], [3, 4]):
             vals = dot(join([p_refs[g][...] for g in group], 0), rhs, NT).astype(BF)
             at = 0
             for g in group:
                 size = p_refs[g].shape[0]
-                out[pl.ds(aligned(off_ref[g]), size), :] = vals[at:at + size]
+                rows = pl.ds(aligned(off_ref[g]), size)
+                d_z = vals[at:at + size].astype(F32)
                 at += size
+                gate_v, up_v = g_ref[rows, :].astype(F32), u_ref[rows, :].astype(F32)
+                square = gate_v * gate_v
+                tanh = jnp.tanh(gate_v * (GELU_C + (GELU_C * GELU_A) * square))
+                half = 0.5 + 0.5 * tanh
+                slope = half + (0.5 * gate_v) * (1.0 - tanh * tanh) * (GELU_C + (3.0 * GELU_C * GELU_A) * square)
+                du_ref[rows, :] = (d_z * (gate_v * half)).astype(BF)
+                dg_ref[rows, :] = (d_z * up_v * slope).astype(BF)
 
     p_specs = [pl.BlockSpec((None,) + p.shape[1:], lambda i: (seq, 0, 0), pipeline_mode=pl.Buffered(1)) for p in pieces]
+    o_spec = pl.BlockSpec((n_rows, tile), lambda i: (0, i))
     return call(
         body, (pl.cdiv(width, tile),),
-        [pl.BlockSpec(memory_space=pltpu.SMEM)] + p_specs + [pl.BlockSpec((tile, depth), lambda i: (i, 0))],
-        pl.BlockSpec((n_rows, tile), lambda i: (0, i)), jax.ShapeDtypeStruct((n_rows, width), BF),
-        2 * n_rows * depth * width, 2 * (n_rows * depth + depth * width + n_rows * width),
-    )(offsets, *pieces, w_down)
+        [pl.BlockSpec(memory_space=pltpu.SMEM)] + p_specs + [pl.BlockSpec((tile, depth), lambda i: (i, 0)), o_spec, o_spec],
+        [o_spec] * 2, [jax.ShapeDtypeStruct((n_rows, width), BF)] * 2,
+        2 * n_rows * depth * width, 2 * (n_rows * depth + depth * width + 4 * n_rows * width),
+    )(offsets, *pieces, w_down, gate, up)
 
 
 def down_grad(acts, pieces, offsets, tile):
@@ -289,35 +298,53 @@
     )(offsets, *acts, *pieces)
 
 
-def gated_mlp(acts, w_gate, w_up, d_act):
+def gated_mlp(acts, w_gate, w_up):
     n_rows, depth = acts.shape
     width = w_gate.shape[1]
     tile, m_tile = 384, 256
 
-    def body(a_ref, wg, wu, dz_ref, z_ref, dg_ref, du_ref):
+    def body(a_ref, wg, wu, g_ref, u_ref, z_ref):
         rhs = jnp.concatenate([wg[...], wu[...]], axis=1)
         for start in range(0, n_rows, m_tile):
             rows = pl.ds(start, m_tile)
-            both = dot(a_ref[rows, :], rhs, NN)
-            gate = both[:, :tile].astype(BF).astype(F32)
-            up = both[:, tile:].astype(BF).astype(F32)
-            d_z = dz_ref[rows, :].astype(F32)
-            square = gate * gate
-            tanh = jnp.tanh(gate * (GELU_C + (GELU_C * GELU_A) * square))
-            half = 0.5 + 0.5 * tanh
-            act = gate * half
-            slope = half + (0.5 * gate) * (1.0 - tanh * tanh) * (GELU_C + (3.0 * GELU_C * GELU_A) * square)
-            z_ref[rows, :] = (act * up).astype(BF)
-            du_ref[rows, :] = (d_z * act).astype(BF)
-            dg_ref[rows, :] = (d_z * up * slope).astype(BF)
+            both = dot(a_ref[rows, :], rhs, NN).astype(BF)
+            g_ref[rows, :] = both[:, :tile]
+            u_ref[rows, :] = both[:, tile:]
+            gate = both[:, :tile].astype(F32)
+            half = 0.5 + 0.5 * jnp.tanh(gate * (GELU_C + (GELU_C * GELU_A) * (gate * gate)))
+            z_ref[rows, :] = (gate * half * both[:, tile:].astype(F32)).astype(BF)
 
     w_spec = pl.BlockSpec((depth, tile), lambda i: (0, i))
     o_spec = pl.BlockSpec((n_rows, tile), lambda i: (0, i))
     return call(
-        body, (width // tile,), [whole(acts), w_spec, w_spec, o_spec], [o_spec] * 3,
+        body, (width // tile,), [whole(acts), w_spec, w_spec], [o_spec] * 3,
         [jax.ShapeDtypeStruct((n_rows, width), BF)] * 3,
-        4 * n_rows * depth * width, 2 * (n_rows * depth + 2 * depth * width + 4 * n_rows * width),
-    )(acts, w_gate, w_up, d_act)
+        4 * n_rows * depth * width, 2 * (n_rows * depth + 2 * depth * width + 3 * n_rows * width),
+    )(acts, w_gate, w_up)
+
+
+def down_proj(acts, w_down, starts, tile):
+    n_rows, width = acts.shape
+    depth = w_down.shape[1]
+    half, part = n_rows // 2, n_rows // 8
+
+    def body(off_ref, z_ref, w_ref, keep, give):
+        rhs = w_ref[...]
+
+        def rows(n, size):
+            return z_ref[pl.ds(aligned(off_ref[n]), size), :]
+
+        for base, out in ((0, keep), (3, give)):
+            out[:2 * part] = dot(rows(base, 2 * part), rhs, NN).astype(BF)
+            out[2 * part:] = dot(join([rows(base + 1, part), rows(base + 2, part)], 0), rhs, NN).astype(BF)
+
+    o_spec = pl.BlockSpec((half, tile), lambda i: (0, i))
+    return call(
+        body, (depth // tile,),
+        [pl.BlockSpec(memory_space=pltpu.SMEM), whole(acts), pl.BlockSpec((width, tile), lambda i: (0, i))],
+        [o_spec] * 2, [jax.ShapeDtypeStruct((half, depth), BF)] * 2,
+        2 * n_rows * depth * width, 2 * (n_rows * width + depth * width + n_rows * depth),
+    )(starts, acts, w_down)
 
 
 def weight_grad(lhs, rhs_groups, out_widths, tile, stream):
@@ -432,21 +459,15 @@
         def mlp_grad(d_g, d_u):
             return rows_times_weights([d_g, d_u], [w_gate, w_up], "nt", 768)
 
-        def down_proj(acts):
-            return rows_times_weights([acts], [w_down], "nn", 768)
-
         def norm_back(cot, pull, skip):
             d_vals, d_gain = pull(cot)
             return skip + d_vals, d_gain
 
-        def add_out(part, vals):
-            return (vals.astype(F32) + part.astype(F32)).astype(BF)
-
         none = [None] * n_seq
         normed_all, attn, attn_part, attn_proj, mlp_all = (list(none) for _ in range(5))
-        norm_attn_pull, norm_mlp_pull, mlp_in, hidden, d_act, gated, d_mlp_in = (list(none) for _ in range(7))
-        down_out, d_hidden, gain_mlp_part, d_hidden_all, d_qkv, d_normed = (list(none) for _ in range(6))
-        grad_x, gain_attn_part, y_out = (list(none) for _ in range(3))
+        norm_attn_pull, norm_mlp_pull, mlp_in, hidden, _, gated, d_mlp_in = (list(none) for _ in range(7))
+        _, d_hidden, gain_mlp_part, d_hidden_all, d_qkv, d_normed = (list(none) for _ in range(6))
+        grad_x, gain_attn_part = (list(none) for _ in range(2))
 
         n_chip = n_tp // 2
         me = lax.axis_index("tp")
@@ -465,42 +486,52 @@
         def own_half(vals):
             return lax.dynamic_slice_in_dim(vals, core * share, share, axis=1)
 
+        keeps = jnp.stack([2 * share * ((chip - back) % n_chip), 2 * share * ((chip + 2) % n_chip) + share * core,
+                           2 * share * chip + share * core, 2 * share * ((chip + back) % n_chip),
+                           2 * share * ((chip + 2) % n_chip) + share * (1 - core),
+                           2 * share * chip + share * (1 - core)]).astype(jnp.int32)
+
         dout_sib = lax.ppermute(d_out, "tp", sibling)
         for s in seqs:
             out, norm_attn_pull[s] = run(norm, x[s], gain_attn)
             normed_all[s] = gather(out)
         dout_pair = run(pair_up, d_out, dout_sib)
-        dout_near = lax.ppermute(dout_pair, "tp", onward)
         for s in seqs:
             attn[s] = run(attention_fwd, normed_all[s], w_qkv, wo2, cos_t[s], sin_t[s], n_rep, head, scale)
             attn_part[s] = attn[s][4]
         attn_proj[0] = scatter(attn_part[0])
-        dout_pass = run(own_half, dout_near)
-        dout_far = lax.ppermute(dout_pass, "tp", onward)
-        dout_near2 = lax.ppermute(dout_near, "tp", sibling)
+        dout_near = lax.ppermute(after(dout_pair, attn_part[1]), "tp", onward)
 
         def mid(s):
             mlp_in[s], norm_mlp_pull[s], hidden[s] = run(mid_norm, attn_proj[s], x[s])
             mlp_all[s] = gather(mlp_in[s])
 
-        latest += [dout_far, dout_near2]
+        def mlp_main(s):
+            gated[s] = run(gated_mlp, mlp_all[s], w_gate, w_up)
+
+        def mlp_down(s):
+            keep, give = run(lambda z: down_proj(z, w_down, keeps, 768), gated[s][2])
+            down_keep[s] = keep
+            down_got[s] = lax.ppermute(give, "tp", sibling)
+
+        down_keep, down_got, d_gate, d_up = (list(none) for _ in range(4))
         mid(0)
         for s in seqs[1:]:
             attn_proj[s] = scatter(after(attn_part[s], mlp_in[0]))
-        dout_far2 = lax.ppermute(after(dout_far, mlp_in[0]), "tp", sibling)
+        dout_pass = run(own_half, dout_near)
+        dout_far = lax.ppermute(dout_pass, "tp", onward)
+        dout_near2 = lax.ppermute(after(dout_near, dout_pass), "tp", sibling)
+        mlp_main(0)
+        dout_far2 = lax.ppermute(after(dout_far, *latest), "tp", sibling)
+        mlp_down(0)
         dout_pieces = (dout_pair, dout_near, dout_near2, dout_far, dout_far2)
+        mid(1)
 
         def act_grad(s):
-            d_act[s] = run(lambda off: act_cotangent(dout_pieces, off, s, w_down, 512), offsets)
-
-        def mlp_main(s):
-            gated[s] = run(gated_mlp, mlp_all[s], w_gate, w_up, d_act[s])
+            d_gate[s], d_up[s] = run(lambda off: act_cotangent(dout_pieces, off, s, w_down, *gated[s][:2], 512), offsets)
 
         def mlp_back(s):
-            d_mlp_in[s] = scatter(run(mlp_grad, gated[s][1], gated[s][2]))
-
-        def mlp_down(s):
-            down_out[s] = scatter(run(down_proj, gated[s][0]))
+            d_mlp_in[s] = scatter(run(mlp_grad, d_gate[s], d_up[s]))
 
         def mid_back(s):
             d_hidden[s], gain_mlp_part[s] = run(norm_back, d_mlp_in[s], norm_mlp_pull[s], d_y[s])
@@ -513,36 +544,54 @@
         def last_back(s):
             grad_x[s], gain_attn_part[s] = run(norm_back, d_normed[s], norm_attn_pull[s], d_hidden[s])
 
+        def halves(keep0, keep1, got0, got1):
+            total = jnp.stack([(k.astype(F32) + g.astype(F32)).astype(BF) for k, g in ((keep0, got0), (keep1, got1))])
+            return total[:, 2 * share:3 * share], total[:, :2 * share], total[:, 3 * share:]
+
+        def pass_on(near, far):
+            row = lax.broadcasted_iota(jnp.int32, (1, 2 * share, 1), 1) // share
+            both = jnp.concatenate([far, far], axis=1).astype(F32)
+            return (near.astype(F32) + jnp.where(row == core, both, 0.0)).astype(BF)
+
+        def own_rows(vals):
+            return own_half(vals), lax.dynamic_slice_in_dim(vals, (1 - core) * share, share, axis=1)
+
+        def finish(mine, near, other):
+            total = (mine.astype(F32) + near.astype(F32) + other.astype(F32)).astype(BF)
+            return (jnp.stack(hidden).astype(F32) + total.astype(F32)).astype(BF)
+
         act_grad(0)
-        mlp_main(0)
+        mlp_back(0)
+        mlp_main(1)
         act_grad(1)
-        mid(1)
-        mlp_back(0)
-        mlp_down(0)
-        mlp_main(1)
         mid_back(0)
         mlp_back(1)
         mlp_down(1)
-        y_out[0] = run(add_out, down_out[0], hidden[0])
-        act_out, d_gate, d_up = zip(*gated)
         attn_back(0)
-        grad_wdown = run(lambda first: down_grad([first, act_out[1]], dout_pieces, offsets, 768), act_out[0])
+        down_far, down_near, down_own = run(halves, down_keep[0], down_keep[1], *down_got)
+        far_in = lax.ppermute(down_far, "tp", onward)
         mid_back(1)
+        act_out = [g[2] for g in gated]
         grad_wgate, grad_wup = run(lambda first: weight_grad(
             [first, mlp_all[1]], [d_gate, d_up], (w_gate.shape[1],) * 2, 384, "rows"), mlp_all[0])
+        down_near = run(pass_on, down_near, far_in)
+        near_in = lax.ppermute(down_near, "tp", onward)
+        grad_wdown = run(lambda first: down_grad([first, act_out[1]], dout_pieces, offsets, 768), act_out[0])
         attn_back(1)
+        near_mine, near_other = run(own_rows, near_in)
+        other_in = lax.ppermute(near_other, "tp", sibling)
         (grad_wo,) = run(lambda first: weight_grad([first, attn[1][3]], [d_hidden_all], (depth,), 768, "cols"),
                          attn[0][3])
         grad_wq, grad_wk, grad_wv = run(lambda first: weight_grad(
             [first, normed_all[1]], [d_qkv], tuple(w[0].size for w in (w_q, w_k, w_v)), 384, "rows"),
             normed_all[0])
+        y_out = run(finish, down_own, near_mine, other_in)
         last_back(0)
-        y_out[1] = run(add_out, down_out[1], hidden[1])
         last_back(1)
         back_attn, back_mlp = gain_attn_part, gain_mlp_part
         gain_parts = jnp.stack([functools.reduce(jnp.add, back) for back in (back_attn, back_mlp)])
         gains = tp_sum(gain_parts, n_tp)
-        return (jnp.stack(y_out), jnp.stack(grad_x), grad_wq.reshape(w_q.shape), grad_wk.reshape(w_k.shape),
+        return (y_out, jnp.stack(grad_x), grad_wq.reshape(w_q.shape), grad_wk.reshape(w_k.shape),
                 grad_wv.reshape(w_v.shape), grad_wo.reshape(w_o.shape), grad_wgate, grad_wup, grad_wdown,
                 gains[0], gains[1])
 

time: 814 us -> 946 us (1.16)
  waiting for transfers between devices: 196 us -> 298 us
  other arithmetic: 46.2 us -> 64 us
    ppermute x3 -> x8, waiting for transfers between devices: 79.8 us -> 183 us  [the longest x1 88.1 us: local_step(): dout_near = lax.ppermute(after(dout_pair, attn_part[1]), 'tp', onward)]
    pallas_call x4 -> x2, Pallas kernels: 120 us -> 75.9 us  [rows_times_weights(): call(body, grid, [whole(a) for a in acts] + w_specs, pl.BlockSpec((n_rows...]
    pallas_call x2 -> x4, Pallas kernels: 82.1 us -> 120 us  [the longest x2 77.3 us: gated_mlp(): call(body, (width // tile,), [whole(acts), w_spec, w_spec], [o_spec] * 3,...]
    ppermute x1, waiting for transfers between devices: 24.8 us -> 57.4 us  [local_step(): dout_far = lax.ppermute(dout_pass, 'tp', onward)]
    all_gather x6, waiting for transfers between devices: 56.2 us -> 33.5 us  [gather(): return lax.all_gather(part, 'tp', axis=0, tiled=True)]
    another operation x1 -> x3, other arithmetic: 1.44 us -> 12 us  [halves(): jnp.stack([(k.astype(F32) + g.astype(F32)).astype(BF) for k, g in ((keep0...]
    reduce_scatter x8 -> x6, waiting for transfers between devices: 32.5 us -> 22.4 us  [scatter(): return lax.psum_scatter(part, 'tp', scatter_dimension=0, tiled=True)]
    pallas_call x2, Pallas kernels: 45.7 us -> 55.6 us  [act_cotangent(): call(body, (pl.cdiv(width, tile),), [pl.BlockSpec(memory_space=pltpu.SMEM...]
  transfers between devices with their start and end apart: 19 -> 22, of which waited for: 7 -> 8; matrix products, arithmetic and copies ran while one was open for 5% -> 7% of each run, Pallas kernels for 64% -> 55%
where the time goes in v3:
time: 946 us; the launch traced here: 939 us
  Pallas kernels  526 us (56%)
  waiting for transfers between devices  298 us (32%)
  other arithmetic  64 us (7%)
  local copies, waits for them, and re-layouts  33.3 us (4%)
  between operations  15.2 us (2%)
    pallas_call x3, Pallas kernels, weight_grad(): call(body, grid, l_specs + r_specs, o_specs, [jax.ShapeDtypeStruct((n_out...  107 us
    ppermute x1, waiting for transfers between devices, local_step(): dout_near = lax.ppermute(after(dout_pair, attn_part[1]), 'tp', onward)  88.1 us
    ppermute x1, waiting for transfers between devices, local_step(): near_in = lax.ppermute(down_near, 'tp', onward)  83.5 us
    pallas_call x2, Pallas kernels, gated_mlp(): call(body, (width // tile,), [whole(acts), w_spec, w_spec], [o_spec] * 3,...  77.3 us
    pallas_call x2, Pallas kernels, rows_times_weights(): call(body, grid, [whole(a) for a in acts] + w_specs, pl.BlockSpec((n_rows...  75.9 us
    pallas_call x2, Pallas kernels, attention_fwd(): call(body, (1,), [any_spec] * 3 + [whole(cos_t), whole(sin_t)], [whole(o)...  63.2 us
    pallas_call x2, Pallas kernels, attention_bwd(): call(body, (1,), [any_spec] * 3 + [whole(r) for r in rest], [whole(outs[0...  57.5 us
    ppermute x1, waiting for transfers between devices, local_step(): dout_far = lax.ppermute(dout_pass, 'tp', onward)  57.4 us
  transfers between devices with their start and end apart: 22, of which 8 were waited for; matrix products, arithmetic and copies ran while one was open for 7% of the time, Pallas kernels for 55%

profile of v3, /device:TPU:112, one launch (start us, length us, event | category | flops | bytes accessed | tf_op | source)
XLA Modules:
  0.0 939.3 jit_solution(10509892184525000065)
XLA Ops:
  7.3 0.7 broadcast_add_fusion.1
  8.0 1.6 slice_bitcast_fusion
  9.9 0.7 copy-done.4
  10.6 1.2 fusion.14
  13.5 1.2 fusion.13
  15.0 2.8 copy.23
  17.8 3.7 multiply_sine_fusion
  21.5 1.4 slice_bitcast_fusion.2
  22.9 1.0 copy-done.20
  24.5 3.8 pad_maximum_fusion.w_hbm
  28.3 4.9 maximum_select_fusion.refs_0_.refs_2_
  33.2 25.1 %all-gather.7.cloned.1.call-done.acts_hbm.refs_0_ = bf16[1024,3840]{1,0:T(8,128)(2,1)} async-done(((bf16[128,3840]{1,0:T(8,128)(2,1)}), bf16[1024,3840]{1,0:T(8,128)(2,1)}) %all-gather.7.cloned.1.call-update) | async-done | bytes 7864336 | tf_op jit(solution)/shard_map/all_gather | solution.py:429
  58.3 36.6 %shard_map.203 = (bf16[1024,512]{1,0:T(8,128)(2,1)}, bf16[1024,256]{1,0:T(8,128)(2,1)}, bf16[1024,256]{1,0:T(8,128)(2,1)}, bf16[1024,512]{1,0:T(8,128)(2,1)}, bf16[1024,3840]{1,0:T(8,128)(2,1)}) custom-call(bf16[1024,3840]{1,0:T(8,128)(2,1)} %all-gather.7.cloned.1.call-done.acts_hbm.refs_0_, bf16[3840,1024]{1,0:T(8,128)(2,1)} %pad_maximum_fusion.w_hbm, ...), custom_call_target="tpu_custom_call" | custom-call | flops 16079595520 | bytes 27525120 | tf_op jit(solution)/shard_map/pallas_call | solution.py:166
  95.7 8.3 all-gather.9.cloned.1.call-done.acts_hbm.refs_1_
  104.0 26.5 %shard_map.204 = (bf16[1024,512]{1,0:T(8,128)(2,1)}, bf16[1024,256]{1,0:T(8,128)(2,1)}, bf16[1024,256]{1,0:T(8,128)(2,1)}, bf16[1024,512]{1,0:T(8,128)(2,1)}, bf16[1024,3840]{1,0:T(8,128)(2,1)}) custom-call(bf16[1024,3840]{1,0:T(8,128)(2,1)} %all-gather.9.cloned.1.call-done.acts_hbm.refs_1_, bf16[3840,1024]{1,0:T(8,128)(2,1)} %pad_maximum_fusion.w_hbm, ...), custom_call_target="tpu_custom_call" | custom-call | flops 16079595520 | bytes 27525120 | tf_op jit(solution)/shard_map/pallas_call | solution.py:166
  130.6 22.4 %reduce-scatter.7.cloned.1.call-done = bf16[128,3840]{1,0:T(8,128)(2,1)} async-done(((bf16[1024,3840]{1,0:T(8,128)(2,1)}), bf16[128,3840]{1,0:T(8,128)(2,1)}) %reduce-scatter.7.cloned.1.call-update) | async-done | bytes 983056 | tf_op jit(solution)/shard_map/reduce_scatter | solution.py:432
  153.0 1.6 fusion.27
  154.6 1.3 fusion.12
  156.9 0.6 stack.70.off_ref
  157.5 88.1 %collective-permute-done.1.refs_1_.refs_3_ = bf16[2,256,3840]{2,1,0:T(8,128)(2,1)} collective-permute-done((bf16[2,256,3840]{2,1,0:T(8,128)(2,1)}, bf16[2,256,3840]{2,1,0:T(8,128)(2,1)}, u32[]{:S(2)}, u32[]{:S(2)}) %collective-permute-start.1) | collective-permute-done | bytes 3932192 | tf_op jit(solution)/shard_map/ppermute | solution.py:503
  245.5 2.9 constant_dynamic-slice_fusion.2
  248.5 38.4 %shard_map.205 = (bf16[1024,1920]{1,0:T(8,128)(2,1)}, bf16[1024,1920]{1,0:T(8,128)(2,1)}, bf16[1024,1920]{1,0:T(8,128)(2,1)}) custom-call(bf16[1024,3840]{1,0:T(8,128)(2,1)} %all-gather.11.cloned.1.call-done.a_ref.refs_0_, bf16[3840,1920]{1,0:T(8,128)(2,1)} %refs_2_.3, bf16[3840,1920]{1,0:T(8,128)(2,1)} %refs_3_.3), custom_call_target="tpu_custom_call" | custom-call | flops 30198988800 | bytes 49152000 | tf_op jit(solution)/shard_map/pallas_call | solution.py:319
  286.9 21.2 %shard_map.206 = (bf16[512,3840]{1,0:T(8,128)(2,1)}, bf16[512,3840]{1,0:T(8,128)(2,1)}) custom-call(s32[6]{0:T(128)} %stack.70.off_ref, bf16[1024,1920]{1,0:T(8,128)(2,1)} %get-tuple-element.125.z_ref.refs_0_, bf16[1920,3840]{1,0:T(8,128)(2,1)} %w_ref.3), custom_call_target="tpu_custom_call" | custom-call | flops 15099494400 | bytes 26542080 | tf_op jit(solution)/shard_map/pallas_call | solution.py:342
  308.1 1.6 fusion.29
  310.9 1.2 fusion.11
  312.9 57.4 %collective-permute-done.3.refs_3_.refs_5_ = bf16[2,128,3840]{2,1,0:T(8,128)(2,1)} collective-permute-done((bf16[2,128,3840]{2,1,0:T(8,128)(2,1)S(1)}, bf16[2,128,3840]{2,1,0:T(8,128)(2,1)}, u32[]{:S(2)}, u32[]{:S(2)}) %collective-permute-start.3) | collective-permute-done | bytes 1966112 | tf_op jit(solution)/shard_map/ppermute | solution.py:522
  370.9 3.6 collective-permute-done.4.refs_4_.refs_6_
  374.5 1.3 copy-done.41
  375.8 27.7 %shard_map.207 = (bf16[1024,1920]{1,0:T(8,128)(2,1)}, bf16[1024,1920]{1,0:T(8,128)(2,1)}) custom-call(s32[5]{0:T(128)} %stack.74.off_ref, bf16[2,256,3840]{2,1,0:T(8,128)(2,1)} %maximum_select_fusion.refs_0_.refs_2_, bf16[2,256,3840]{2,1,0:T(8,128)(2,1)} %collective-permute-done.1.refs_1_.refs_3_, ...), custom_call_target="tpu_custom_call" | custom-call | flops 15099494400 | bytes 38338560 | tf_op jit(solution)/shard_map/pallas_call | solution.py:273
  403.4 37.6 %shard_map.208 = bf16[1024,3840]{1,0:T(8,128)(2,1)} custom-call(bf16[1024,1920]{1,0:T(8,128)(2,1)} %get-tuple-element.100.refs_0_.refs_2_, bf16[1024,1920]{1,0:T(8,128)(2,1)} %get-tuple-element.101.refs_1_.refs_4_, bf16[3840,1920]{1,0:T(8,128)(2,1)} %refs_2_.3, bf16[3840,1920]{1,0:T(8,128)(2,1)} %refs_3_.3), custom_call_target="tpu_custom_call" | custom-call | flops 30198988800 | bytes 45219840 | tf_op jit(solution)/shard_map/pallas_call | solution.py:87
  441.4 38.9 %shard_map.209 = (bf16[1024,1920]{1,0:T(8,128)(2,1)}, bf16[1024,1920]{1,0:T(8,128)(2,1)}, bf16[1024,1920]{1,0:T(8,128)(2,1)}) custom-call(bf16[1024,3840]{1,0:T(8,128)(2,1)} %all-gather.13.cloned.1.call-done.a_ref.refs_1_, bf16[3840,1920]{1,0:T(8,128)(2,1)} %refs_2_.3, bf16[3840,1920]{1,0:T(8,128)(2,1)} %refs_3_.3), custom_call_target="tpu_custom_call" | custom-call | flops 30198988800 | bytes 49152000 | tf_op jit(solution)/shard_map/pallas_call | solution.py:319
  480.3 27.9 %shard_map.210 = (bf16[1024,1920]{1,0:T(8,128)(2,1)}, bf16[1024,1920]{1,0:T(8,128)(2,1)}) custom-call(s32[5]{0:T(128)} %stack.74.off_ref, bf16[2,256,3840]{2,1,0:T(8,128)(2,1)} %maximum_select_fusion.refs_0_.refs_2_, bf16[2,256,3840]{2,1,0:T(8,128)(2,1)} %collective-permute-done.1.refs_1_.refs_3_, ...), custom_call_target="tpu_custom_call" | custom-call | flops 15099494400 | bytes 38338560 | tf_op jit(solution)/shard_map/pallas_call | solution.py:273
  508.2 2.7 fusion.15
  511.0 2.9 fusion.35
  514.2 38.3 %shard_map.211 = bf16[1024,3840]{1,0:T(8,128)(2,1)} custom-call(bf16[1024,1920]{1,0:T(8,128)(2,1)} %get-tuple-element.109.refs_0_.refs_3_, bf16[1024,1920]{1,0:T(8,128)(2,1)} %get-tuple-element.110.refs_1_.refs_5_, bf16[3840,1920]{1,0:T(8,128)(2,1)} %refs_2_.3, bf16[3840,1920]{1,0:T(8,128)(2,1)} %refs_3_.3), custom_call_target="tpu_custom_call" | custom-call | flops 30198988800 | bytes 45219840 | tf_op jit(solution)/shard_map/pallas_call | solution.py:87
  552.6 21.6 %shard_map.212 = (bf16[512,3840]{1,0:T(8,128)(2,1)}, bf16[512,3840]{1,0:T(8,128)(2,1)}) custom-call(s32[6]{0:T(128)} %stack.70.off_ref, bf16[1024,1920]{1,0:T(8,128)(2,1)} %get-tuple-element.111.z_ref.refs_1_, bf16[1920,3840]{1,0:T(8,128)(2,1)} %w_ref.3), custom_call_target="tpu_custom_call" | custom-call | flops 15099494400 | bytes 26542080 | tf_op jit(solution)/shard_map/pallas_call | solution.py:342
  574.8 7.4 collective-permute-done.6
  582.2 5.0 fusion.1
  587.2 28.9 %shard_map.213 = (bf16[1024,1024]{1,0:T(8,128)(2,1)}, bf16[1024,3840]{1,0:T(8,128)(2,1)}) custom-call(bf16[1024,3840]{1,0:T(8,128)(2,1)} %all-gather.15.cloned.1.call-done.cot_hbm.refs_2_, bf16[3840,1024]{1,0:T(8,128)(2,1)} %pad_maximum_fusion.w_hbm, bf16[512,3840]{1,0:T(8,128)(2,1)} %bitcast.55, bf16[1024,512]{1,0:T(8,128)(2,1)} %get-tuple-element.81.q, ...), custom_call_target="tpu_custom_call" | custom-call | flops 20079595520 | bytes 27525120 | tf_op jit(solution)/shard_map/pallas_call | solution.py:233
  616.1 4.3 fusion
  620.5 1.9 copy-done.1
  622.4 2.2 pad_maximum_fusion.2
  624.6 2.1 fusion.16
  626.7 1.7 fusion.34
  628.5 0.7 reduce-scatter.15.cloned.1.call-update
  629.4 2.6 fusion.2
  632.1 71.3 %shard_map.214 = (bf16[3840,1920]{1,0:T(8,128)(2,1)}, bf16[3840,1920]{1,0:T(8,128)(2,1)}) custom-call(bf16[1024,3840]{1,0:T(8,128)(2,1)} %all-gather.11.cloned.1.call-done.a_ref.refs_0_, bf16[1024,3840]{1,0:T(8,128)(2,1)} %all-gather.13.cloned.1.call-done.a_ref.refs_1_, bf16[1024,1920]{1,0:T(8,128)(2,1)} %get-tuple-element.100.refs_0_.refs_2_, ...), custom_call_target="tpu_custom_call" | custom-call | flops 60397977600 | bytes 60948480 | tf_op jit(solution)/shard_map/pallas_call | solution.py:377
  703.4 5.0 add_convert_fusion
  708.3 39.0 %shard_map.215 = bf16[1920,3840]{1,0:T(8,128)(2,1)} custom-call(s32[5]{0:T(128)} %stack.74.off_ref, bf16[1024,1920]{1,0:T(8,128)(2,1)} %get-tuple-element.125.z_ref.refs_0_, bf16[1024,1920]{1,0:T(8,128)(2,1)} %get-tuple-element.111.z_ref.refs_1_, bf16[2,256,3840]{2,1,0:T(8,128)(2,1)} %maximum_select_fusion.refs_0_.refs_2_, ...), custom_call_target="tpu_custom_call" | custom-call | flops 30198988800 | bytes 38338560 | tf_op jit(solution)/shard_map/pallas_call | solution.py:293
  747.4 28.6 %shard_map.216 = (bf16[1024,1024]{1,0:T(8,128)(2,1)}, bf16[1024,3840]{1,0:T(8,128)(2,1)}) custom-call(bf16[1024,3840]{1,0:T(8,128)(2,1)} %all-gather.17.cloned.1.call-done.cot_hbm.refs_3_, bf16[3840,1024]{1,0:T(8,128)(2,1)} %pad_maximum_fusion.w_hbm, bf16[512,3840]{1,0:T(8,128)(2,1)} %bitcast.56, bf16[1024,512]{1,0:T(8,128)(2,1)} %get-tuple-element.83.q, ...), custom_call_target="tpu_custom_call" | custom-call | flops 20079595520 | bytes 27525120 | tf_op jit(solution)/shard_map/pallas_call | solution.py:233
  776.7 83.5 %collective-permute-done.8 = bf16[2,256,3840]{2,1,0:T(8,128)(2,1)} collective-permute-done((bf16[2,256,3840]{2,1,0:T(8,128)(2,1)}, bf16[2,256,3840]{2,1,0:T(8,128)(2,1)}, u32[]{:S(2)}, u32[]{:S(2)}) %collective-permute-start.8) | collective-permute-done | bytes 3932192 | tf_op jit(solution)/shard_map/ppermute | solution.py:578
  860.2 4.3 constant_dynamic-slice_fusion.1
  864.5 13.4 %shard_map.217 = bf16[512,3840]{1,0:T(8,128)(2,1)} custom-call(bf16[1024,512]{1,0:T(8,128)(2,1)} %get-tuple-element.131.refs_0_, bf16[1024,512]{1,0:T(8,128)(2,1)} %get-tuple-element.132.refs_1_, bf16[1024,3840]{1,0:T(8,128)(2,1)} %all-gather.15.cloned.1.call-done.cot_hbm.refs_2_, bf16[1024,3840]{1,0:T(8,128)(2,1)} %all-gather.17.cloned.1.call-done.cot_hbm.refs_3_), custom_call_target="tpu_custom_call" | custom-call | flops 8053063680 | bytes 21757952 | tf_op jit(solution)/shard_map/pallas_call | solution.py:377
  877.9 21.9 %shard_map.218 = (bf16[3840,512]{1,0:T(8,128)(2,1)}, bf16[3840,256]{1,0:T(8,128)(2,1)}, bf16[3840,256]{1,0:T(8,128)(2,1)}) custom-call(bf16[1024,3840]{1,0:T(8,128)(2,1)} %all-gather.7.cloned.1.call-done.acts_hbm.refs_0_, bf16[1024,3840]{1,0:T(8,128)(2,1)} %all-gather.9.cloned.1.call-done.acts_hbm.refs_1_, bf16[1024,1024]{1,0:T(8,128)(2,1)} %get-tuple-element.116.refs_2_, ...), custom_call_target="tpu_custom_call" | custom-call | flops 16106127360 | bytes 27787264 | tf_op jit(solution)/shard_map/pallas_call | solution.py:377
  899.8 9.3 reshape.189
  909.2 5.0 add_convert_fusion.3
  914.3 2.1 fusion.17
  916.5 1.6 fusion.33
  918.1 2.0 fusion.18
  920.1 0.6 pad_maximum_fusion.4.x_ref
  920.8 8.6 tp_sum.1
  929.4 0.7 fusion.32
  930.1 0.7 slice_reduce_fusion
  930.8 1.4 pad_maximum_fusion.3
  (146 shorter events, 9.4 us)
Async XLA Ops:
  7.2 51.1 %all-gather.7.cloned.1.call-start = ((), (), s32[]{:S(2)}) async-start(), calls=%async_computation.6 | async-start | bytes 8847360 | tf_op jit(solution)/shard_map/all_gather | solution.py:429
  8.0 4.9 copy-start.23
  9.6 1.0 copy-start.4
  9.6 3.3 copy-start.2
  9.9 2.1 copy-start.37
  10.6 1.4 copy-start.31
  11.9 92.1 %all-gather.9.cloned.1.call-start = ((), (), s32[]{:S(2)}) async-start(), calls=%async_computation.8 | async-start | bytes 8847360 | tf_op jit(solution)/shard_map/all_gather | solution.py:429
  12.0 2.8 copy-start.14
  12.0 3.0 copy-start.28
  12.3 0.6 copy-start.35
  12.9 0.6 copy-start.29
  14.8 138.2 %reduce-scatter.7.cloned.1.call-start = ((), (), s32[]{:S(2)}) async-start(), calls=%async_computation.7 | async-start | bytes 8847360 | tf_op jit(solution)/shard_map/reduce_scatter | solution.py:432
  14.9 13.4 %collective-permute-start = (bf16[2,128,3840]{2,1,0:T(8,128)(2,1)S(1)}, bf16[2,128,3840]{2,1,0:T(8,128)(2,1)}, u32[]{:S(2)}, u32[]{:S(2)}) collective-permute-start(bf16[2,128,3840]{2,1,0:T(8,128)(2,1)S(1)} %copy-done.14), channel_id=1, source_target_pairs={{0,1},{1,0},{2,3},{3,2},{4,5},{5,4},{6,7},{7,6},{8,9},{9,8},{10,11... | collective-permute-start | bytes 5898248 | tf_op jit(solution)/shard_map/ppermute | solution.py:494
  21.5 2.4 copy-start.20
  21.5 3.0 copy-start.21
  95.0 0.7 copy-start.27
  95.0 153.5 %all-gather.11.cloned.1.call-start = ((), (), s32[]{:S(2)}) async-start(), calls=%async_computation.10 | async-start | bytes 8847360 | tf_op jit(solution)/shard_map/all_gather | solution.py:429
  104.0 48.9 %copy-start.13 = (bf16[2,128,3840]{2,1,0:T(8,128)(2,1)S(1)}, bf16[2,128,3840]{2,1,0:T(8,128)(2,1)}, u32[]{:S(2)}) copy-start(bf16[2,128,3840]{2,1,0:T(8,128)(2,1)} %param.12) | copy-start | bytes 5898244
  154.6 356.4 %copy-start.6 = (bf16[128,3840]{1,0:T(8,128)(2,1)}, bf16[128,3840]{1,0:T(8,128)(2,1)S(1)}, u32[]{:S(2)}) copy-start(bf16[128,3840]{1,0:T(8,128)(2,1)S(1)} %get-tuple-element.156) | copy-start | bytes 2949124
  155.9 152.1 %reduce-scatter.9.cloned.1.call-start = ((), (), s32[]{:S(2)}) async-start(), calls=%async_computation.9 | async-start | bytes 8847360 | tf_op jit(solution)/shard_map/reduce_scatter | solution.py:432
  156.6 284.8 %all-gather.13.cloned.1.call-start = ((), (), s32[]{:S(2)}) async-start(), calls=%async_computation.12 | async-start | bytes 8847360 | tf_op jit(solution)/shard_map/all_gather | solution.py:429
  156.7 88.9 %collective-permute-start.1 = (bf16[2,256,3840]{2,1,0:T(8,128)(2,1)}, bf16[2,256,3840]{2,1,0:T(8,128)(2,1)}, u32[]{:S(2)}, u32[]{:S(2)}) collective-permute-start(bf16[2,256,3840]{2,1,0:T(8,128)(2,1)} %maximum_select_fusion.refs_0_.refs_2_), channel_id=1, source_target_pairs={{0,2},{1,7},{2,4},{3,1},{4,6},{5,3},{6,0},{7,5},{8,10},{9,15},{10,... | collective-permute-start | bytes 11796488 | tf_op jit(solution)/shard_map/ppermute | solution.py:503
  309.7 0.6 copy-start.39
  309.7 1.0 copy-start.8
  309.7 2.9 copy-start.22
  310.3 0.6 copy-start.33
  312.2 196.0 %reduce-scatter.11.cloned.1.call-start = ((), (), s32[]{:S(2)}) async-start(), calls=%async_computation.11 | async-start | bytes 8847360 | tf_op jit(solution)/shard_map/reduce_scatter | solution.py:432
  312.7 57.6 %collective-permute-start.3 = (bf16[2,128,3840]{2,1,0:T(8,128)(2,1)S(1)}, bf16[2,128,3840]{2,1,0:T(8,128)(2,1)}, u32[]{:S(2)}, u32[]{:S(2)}) collective-permute-start(bf16[2,128,3840]{2,1,0:T(8,128)(2,1)S(1)} %copy-done.22), channel_id=1, source_target_pairs={{0,2},{1,7},{2,4},{3,1},{4,6},{5,3},{6,0},{7,5},{8,10},{9,15},{10,... | collective-permute-start | bytes 5898248 | tf_op jit(solution)/shard_map/ppermute | solution.py:522
  312.8 58.1 %collective-permute-start.2 = (bf16[2,256,3840]{2,1,0:T(8,128)(2,1)}, bf16[2,256,3840]{2,1,0:T(8,128)(2,1)}, u32[]{:S(2)}, u32[]{:S(2)}) collective-permute-start(bf16[2,256,3840]{2,1,0:T(8,128)(2,1)} %collective-permute-done.1.refs_1_.refs_3_), channel_id=1, source_target_pairs={{0,1},{1,0},{2,3},{3,2},{4,5},{5,4},{6,7},{7,6},{8,9},{9,8},{10,11... | collective-permute-start | bytes 11796488 | tf_op jit(solution)/shard_map/ppermute | solution.py:523
  370.3 4.2 collective-permute-start.4
  374.5 1.3 copy-start.41
  441.1 146.0 %all-gather.15.cloned.1.call-start = ((), (), s32[]{:S(2)}) async-start(), calls=%async_computation.13 | async-start | bytes 8847360 | tf_op jit(solution)/shard_map/all_gather | solution.py:429
  508.2 2.8 copy-start.15
  513.9 110.7 %reduce-scatter.13.cloned.1.call-start = ((), (), s32[]{:S(2)}) async-start(), calls=%async_computation.14 | async-start | bytes 8847360 | tf_op jit(solution)/shard_map/reduce_scatter | solution.py:432
  552.6 194.8 %all-gather.17.cloned.1.call-start = ((), (), s32[]{:S(2)}) async-start(), calls=%async_computation.15 | async-start | bytes 8847360 | tf_op jit(solution)/shard_map/all_gather | solution.py:429
  574.2 8.0 collective-permute-start.6
  574.4 41.7 %collective-permute-start.5 = (bf16[512,3840]{1,0:T(8,128)(2,1)}, bf16[512,3840]{1,0:T(8,128)(2,1)}, u32[]{:S(2)}, u32[]{:S(2)}) collective-permute-start(bf16[512,3840]{1,0:T(8,128)(2,1)} %get-tuple-element.118), channel_id=1, source_target_pairs={{0,1},{1,0},{2,3},{3,2},{4,5},{5,4},{6,7},{7,6},{8,9},{9,8},{10,11... | collective-permute-start | bytes 11796488 | tf_op jit(solution)/shard_map/ppermute | solution.py:515
  616.1 6.3 copy-start
  620.5 1.9 copy-start.1
  622.4 2.2 copy-start.9
  622.4 2.2 copy-start.34
  624.6 2.1 copy-start.40
  624.6 2.1 copy-start.18
  628.5 285.8 %reduce-scatter.15.cloned.1.call-start = ((), (), s32[]{:S(2)}) async-start(), calls=%async_computation.16 | async-start | bytes 8847360 | tf_op jit(solution)/shard_map/reduce_scatter | solution.py:432
  629.2 288.8 %reduce-scatter.17.cloned.1.call-start = ((), (), s32[]{:S(2)}) async-start(), calls=%async_computation.17 | async-start | bytes 8847360 | tf_op jit(solution)/shard_map/reduce_scatter | solution.py:432
  629.3 74.0 %collective-permute-start.7 = (bf16[2,128,3840]{2,1,0:T(8,128)(2,1)}, bf16[2,128,3840]{2,1,0:T(8,128)(2,1)}, u32[]{:S(2)}, u32[]{:S(2)}) collective-permute-start(bf16[2,128,3840]{2,1,0:T(8,128)(2,1)} %get-tuple-element.158), channel_id=1, source_target_pairs={{0,2},{1,7},{2,4},{3,1},{4,6},{5,3},{6,0},{7,5},{8,10},{9,15},{10,... | collective-permute-start | bytes 5898248 | tf_op jit(solution)/shard_map/ppermute | solution.py:572
  775.9 0.7 copy-start.25
  776.0 84.2 %collective-permute-start.8 = (bf16[2,256,3840]{2,1,0:T(8,128)(2,1)}, bf16[2,256,3840]{2,1,0:T(8,128)(2,1)}, u32[]{:S(2)}, u32[]{:S(2)}) collective-permute-start(bf16[2,256,3840]{2,1,0:T(8,128)(2,1)} %add_convert_fusion), channel_id=1, source_target_pairs={{0,2},{1,7},{2,4},{3,1},{4,6},{5,3},{6,0},{7,5},{8,10},{9,15},{10,... | collective-permute-start | bytes 11796488 | tf_op jit(solution)/shard_map/ppermute | solution.py:578
  864.5 44.6 %collective-permute-start.9 = (bf16[2,128,3840]{2,1,0:T(8,128)(2,1)}, bf16[2,128,3840]{2,1,0:T(8,128)(2,1)}, u32[]{:S(2)}, u32[]{:S(2)}) collective-permute-start(bf16[2,128,3840]{2,1,0:T(8,128)(2,1)} %get-tuple-element.160), channel_id=1, source_target_pairs={{0,1},{1,0},{2,3},{3,2},{4,5},{5,4},{6,7},{7,6},{8,9},{9,8},{10,11... | collective-permute-start | bytes 5898248 | tf_op jit(solution)/shard_map/ppermute | solution.py:582
  899.8 9.3 copy-start.7
  899.8 9.3 copy-start.10
  909.1 5.1 copy-start.5
  909.2 5.1 copy-start.24
  909.2 5.1 copy-start.32
  914.2 2.2 copy-start.38
  914.2 2.2 copy-start.11
  914.2 2.2 copy-start.16
  916.4 1.7 copy-start.3
  916.4 1.6 copy-start.30
  920.8 8.6 copy-start.36
  920.8 8.6 copy-start.12
  920.8 8.6 copy-start.17
  929.4 0.8 copy-start.26
  929.4 1.4 copy-start.19
Sparse Core Ops, SparseCore 0:
  12.0 46.2 all-gather.6
  60.5 43.4 all-gather.8
  106.9 46.0 reduce-scatter.6
  156.1 58.8 all-gather.10
  217.7 55.9 reduce-scatter.8
  312.3 58.0 all-gather.12
  441.3 44.6 reduce-scatter.10
  514.0 42.1 all-gather.14
  559.1 46.0 reduce-scatter.12
  628.6 57.8 all-gather.16
  688.8 45.0 reduce-scatter.14
  776.1 83.8 reduce-scatter.16

commit v4 on v3

--- a/solution.py
+++ b/solution.py
@@ -323,30 +323,6 @@
     )(acts, w_gate, w_up)
 
 
-def down_proj(acts, w_down, starts, tile):
-    n_rows, width = acts.shape
-    depth = w_down.shape[1]
-    half, part = n_rows // 2, n_rows // 8
-
-    def body(off_ref, z_ref, w_ref, keep, give):
-        rhs = w_ref[...]
-
-        def rows(n, size):
-            return z_ref[pl.ds(aligned(off_ref[n]), size), :]
-
-        for base, out in ((0, keep), (3, give)):
-            out[:2 * part] = dot(rows(base, 2 * part), rhs, NN).astype(BF)
-            out[2 * part:] = dot(join([rows(base + 1, part), rows(base + 2, part)], 0), rhs, NN).astype(BF)
-
-    o_spec = pl.BlockSpec((half, tile), lambda i: (0, i))
-    return call(
-        body, (depth // tile,),
-        [pl.BlockSpec(memory_space=pltpu.SMEM), whole(acts), pl.BlockSpec((width, tile), lambda i: (0, i))],
-        [o_spec] * 2, [jax.ShapeDtypeStruct((half, depth), BF)] * 2,
-        2 * n_rows * depth * width, 2 * (n_rows * width + depth * width + n_rows * depth),
-    )(starts, acts, w_down)
-
-
 def weight_grad(lhs, rhs_groups, out_widths, tile, stream):
     n_seq, n_tok = len(lhs), lhs[0].shape[0]
     n_out = lhs[0].shape[1]
@@ -463,10 +439,13 @@
             d_vals, d_gain = pull(cot)
             return skip + d_vals, d_gain
 
+        def add_out(part, vals):
+            return (vals.astype(F32) + part.astype(F32)).astype(BF)
+
         none = [None] * n_seq
         normed_all, attn, attn_part, attn_proj, mlp_all = (list(none) for _ in range(5))
         norm_attn_pull, norm_mlp_pull, mlp_in, hidden, _, gated, d_mlp_in = (list(none) for _ in range(7))
-        _, d_hidden, gain_mlp_part, d_hidden_all, d_qkv, d_normed = (list(none) for _ in range(6))
+        down_out, d_hidden, gain_mlp_part, d_hidden_all, d_qkv, d_normed = (list(none) for _ in range(6))
         grad_x, gain_attn_part = (list(none) for _ in range(2))
 
         n_chip = n_tp // 2
@@ -486,11 +465,6 @@
         def own_half(vals):
             return lax.dynamic_slice_in_dim(vals, core * share, share, axis=1)
 
-        keeps = jnp.stack([2 * share * ((chip - back) % n_chip), 2 * share * ((chip + 2) % n_chip) + share * core,
-                           2 * share * chip + share * core, 2 * share * ((chip + back) % n_chip),
-                           2 * share * ((chip + 2) % n_chip) + share * (1 - core),
-                           2 * share * chip + share * (1 - core)]).astype(jnp.int32)
-
         dout_sib = lax.ppermute(d_out, "tp", sibling)
         for s in seqs:
             out, norm_attn_pull[s] = run(norm, x[s], gain_attn)
@@ -510,20 +484,19 @@
             gated[s] = run(gated_mlp, mlp_all[s], w_gate, w_up)
 
         def mlp_down(s):
-            keep, give = run(lambda z: down_proj(z, w_down, keeps, 768), gated[s][2])
-            down_keep[s] = keep
-            down_got[s] = lax.ppermute(give, "tp", sibling)
-
-        down_keep, down_got, d_gate, d_up = (list(none) for _ in range(4))
+            part = run(lambda z: rows_times_weights([z], [w_down], "nn", 768), gated[s][2])
+            down_out[s] = scatter(part)
+
+        d_gate, d_up, y_out = (list(none) for _ in range(3))
         mid(0)
         for s in seqs[1:]:
             attn_proj[s] = scatter(after(attn_part[s], mlp_in[0]))
+        mlp_main(0)
         dout_pass = run(own_half, dout_near)
         dout_far = lax.ppermute(dout_pass, "tp", onward)
         dout_near2 = lax.ppermute(after(dout_near, dout_pass), "tp", sibling)
-        mlp_main(0)
-        dout_far2 = lax.ppermute(after(dout_far, *latest), "tp", sibling)
         mlp_down(0)
+        dout_far2 = lax.ppermute(dout_far, "tp", sibling)
         dout_pieces = (dout_pair, dout_near, dout_near2, dout_far, dout_far2)
         mid(1)
 
@@ -544,54 +517,36 @@
         def last_back(s):
             grad_x[s], gain_attn_part[s] = run(norm_back, d_normed[s], norm_attn_pull[s], d_hidden[s])
 
-        def halves(keep0, keep1, got0, got1):
-            total = jnp.stack([(k.astype(F32) + g.astype(F32)).astype(BF) for k, g in ((keep0, got0), (keep1, got1))])
-            return total[:, 2 * share:3 * share], total[:, :2 * share], total[:, 3 * share:]
-
-        def pass_on(near, far):
-            row = lax.broadcasted_iota(jnp.int32, (1, 2 * share, 1), 1) // share
-            both = jnp.concatenate([far, far], axis=1).astype(F32)
-            return (near.astype(F32) + jnp.where(row == core, both, 0.0)).astype(BF)
-
-        def own_rows(vals):
-            return own_half(vals), lax.dynamic_slice_in_dim(vals, (1 - core) * share, share, axis=1)
-
-        def finish(mine, near, other):
-            total = (mine.astype(F32) + near.astype(F32) + other.astype(F32)).astype(BF)
-            return (jnp.stack(hidden).astype(F32) + total.astype(F32)).astype(BF)
+        def add_out(part, vals):
+            return (vals.astype(F32) + part.astype(F32)).astype(BF)
 
         act_grad(0)
         mlp_back(0)
         mlp_main(1)
         act_grad(1)
+        y_out[0] = run(add_out, down_out[0], hidden[0])
         mid_back(0)
         mlp_back(1)
         mlp_down(1)
         attn_back(0)
-        down_far, down_near, down_own = run(halves, down_keep[0], down_keep[1], *down_got)
-        far_in = lax.ppermute(down_far, "tp", onward)
         mid_back(1)
         act_out = [g[2] for g in gated]
         grad_wgate, grad_wup = run(lambda first: weight_grad(
             [first, mlp_all[1]], [d_gate, d_up], (w_gate.shape[1],) * 2, 384, "rows"), mlp_all[0])
-        down_near = run(pass_on, down_near, far_in)
-        near_in = lax.ppermute(down_near, "tp", onward)
         grad_wdown = run(lambda first: down_grad([first, act_out[1]], dout_pieces, offsets, 768), act_out[0])
         attn_back(1)
-        near_mine, near_other = run(own_rows, near_in)
-        other_in = lax.ppermute(near_other, "tp", sibling)
         (grad_wo,) = run(lambda first: weight_grad([first, attn[1][3]], [d_hidden_all], (depth,), 768, "cols"),
                          attn[0][3])
         grad_wq, grad_wk, grad_wv = run(lambda first: weight_grad(
             [first, normed_all[1]], [d_qkv], tuple(w[0].size for w in (w_q, w_k, w_v)), 384, "rows"),
             normed_all[0])
-        y_out = run(finish, down_own, near_mine, other_in)
+        y_out[1] = run(add_out, down_out[1], hidden[1])
         last_back(0)
         last_back(1)
         back_attn, back_mlp = gain_attn_part, gain_mlp_part
         gain_parts = jnp.stack([functools.reduce(jnp.add, back) for back in (back_attn, back_mlp)])
         gains = tp_sum(gain_parts, n_tp)
-        return (y_out, jnp.stack(grad_x), grad_wq.reshape(w_q.shape), grad_wk.reshape(w_k.shape),
+        return (jnp.stack(y_out), jnp.stack(grad_x), grad_wq.reshape(w_q.shape), grad_wk.reshape(w_k.shape),
                 grad_wv.reshape(w_v.shape), grad_wo.reshape(w_o.shape), grad_wgate, grad_wup, grad_wdown,
                 gains[0], gains[1])
 

time: 946 us -> 806 us (0.85)
  waiting for transfers between devices: 298 us -> 189 us
  other arithmetic: 64 us -> 44.7 us
    ppermute x6 -> x1, waiting for transfers between devices: 94.5 us -> 3.57 us  [local_step(): dout_far2 = lax.ppermute(dout_far, 'tp', sibling)]
    ppermute x1, waiting for transfers between devices: 88.1 us -> 0.01 us  [local_step(): dout_near = lax.ppermute(after(dout_pair, attn_part[1]), 'tp', onward)]
    all_gather x6, waiting for transfers between devices: 33.5 us -> 102 us  [gather(): return lax.all_gather(part, 'tp', axis=0, tiled=True)]
    pallas_call x2 -> x4, Pallas kernels: 75.9 us -> 119 us  [rows_times_weights(): call(body, grid, [whole(a) for a in acts] + w_specs, pl.BlockSpec((n_rows...]
    pallas_call x2 -> x0, Pallas kernels: 42.7 us -> none  [down_proj(): call(body, (depth // tile,), [pl.BlockSpec(memory_space=pltpu.SMEM), whol...]
    another operation x3 -> x1, other arithmetic: 12 us -> 1.44 us  [local_step(): jnp.stack(y_out)]
    pallas_call x2, Pallas kernels: 63.2 us -> 53.1 us  [attention_fwd(): call(body, (1,), [any_spec] * 3 + [whole(cos_t), whole(sin_t)], [whole(o)...]
    reduce_scatter x6 -> x8, waiting for transfers between devices: 22.4 us -> 24.1 us  [scatter(): return lax.psum_scatter(part, 'tp', scatter_dimension=0, tiled=True)]
  transfers between devices with their start and end apart: 22 -> 19, of which waited for: 8 -> 7; matrix products, arithmetic and copies ran while one was open for 7% -> 5% of each run, Pallas kernels for 55% -> 64%
where the time goes in v4:
time: 806 us; the launch traced here: 799 us
  Pallas kernels  518 us (64%)
  waiting for transfers between devices  189 us (23%)
  other arithmetic  44.7 us (6%)
  local copies, waits for them, and re-layouts  29.1 us (4%)
  between operations  14.9 us (2%)
    pallas_call x4, Pallas kernels, rows_times_weights(): call(body, grid, [whole(a) for a in acts] + w_specs, pl.BlockSpec((n_rows...  119 us
    pallas_call x3, Pallas kernels, weight_grad(): call(body, grid, l_specs + r_specs, o_specs, [jax.ShapeDtypeStruct((n_out...  107 us
    all_gather x6, waiting for transfers between devices, gather(): return lax.all_gather(part, 'tp', axis=0, tiled=True)  102 us
    pallas_call x2, Pallas kernels, gated_mlp(): call(body, (width // tile,), [whole(acts), w_spec, w_spec], [o_spec] * 3,...  77 us
    pallas_call x2, Pallas kernels, attention_bwd(): call(body, (1,), [any_spec] * 3 + [whole(r) for r in rest], [whole(outs[0...  58.2 us
    ppermute x1, waiting for transfers between devices, local_step(): dout_far = lax.ppermute(dout_pass, 'tp', onward)  56.7 us
    pallas_call x2, Pallas kernels, act_cotangent(): call(body, (pl.cdiv(width, tile),), [pl.BlockSpec(memory_space=pltpu.SMEM...  56.4 us
    pallas_call x2, Pallas kernels, attention_fwd(): call(body, (1,), [any_spec] * 3 + [whole(cos_t), whole(sin_t)], [whole(o)...  53.1 us
  transfers between devices with their start and end apart: 19, of which 7 were waited for; matrix products, arithmetic and copies ran while one was open for 5% of the time, Pallas kernels for 64%

profile of v4, /device:TPU:112, one launch (start us, length us, event | category | flops | bytes accessed | tf_op | source)
XLA Modules:
  0.0 799.1 jit_solution(7951333174746884652)
XLA Ops:
  7.3 0.7 broadcast_add_fusion.1
  8.0 1.6 slice_bitcast_fusion.1
  9.9 0.8 copy-done.39
  11.3 1.2 fusion.11
  14.1 1.2 fusion.10
  15.6 2.8 copy.23
  18.4 3.7 multiply_sine_fusion
  22.2 1.4 slice_bitcast_fusion.2
  23.5 1.1 copy-done.20
  25.2 3.8 pad_maximum_fusion.w_hbm
  28.9 4.6 maximum_select_fusion.refs_0_.refs_2_
  33.6 25.4 %all-gather.7.cloned.1.call-done.acts_hbm.refs_0_ = bf16[1024,3840]{1,0:T(8,128)(2,1)} async-done(((bf16[128,3840]{1,0:T(8,128)(2,1)}), bf16[1024,3840]{1,0:T(8,128)(2,1)}) %all-gather.7.cloned.1.call-update) | async-done | bytes 7864336 | tf_op jit(solution)/shard_map/all_gather | solution.py:405
  59.0 26.6 %shard_map.203 = (bf16[1024,512]{1,0:T(8,128)(2,1)}, bf16[1024,256]{1,0:T(8,128)(2,1)}, bf16[1024,256]{1,0:T(8,128)(2,1)}, bf16[1024,512]{1,0:T(8,128)(2,1)}, bf16[1024,3840]{1,0:T(8,128)(2,1)}) custom-call(bf16[1024,3840]{1,0:T(8,128)(2,1)} %all-gather.7.cloned.1.call-done.acts_hbm.refs_0_, bf16[3840,1024]{1,0:T(8,128)(2,1)} %pad_maximum_fusion.w_hbm, ...), custom_call_target="tpu_custom_call" | custom-call | flops 16079595520 | bytes 27525120 | tf_op jit(solution)/shard_map/pallas_call | solution.py:166
  86.3 18.4 %all-gather.9.cloned.1.call-done.acts_hbm.refs_1_ = bf16[1024,3840]{1,0:T(8,128)(2,1)} async-done(((bf16[128,3840]{1,0:T(8,128)(2,1)}), bf16[1024,3840]{1,0:T(8,128)(2,1)}) %all-gather.9.cloned.1.call-update) | async-done | bytes 7864336 | tf_op jit(solution)/shard_map/all_gather | solution.py:405
  104.7 26.5 %shard_map.204 = (bf16[1024,512]{1,0:T(8,128)(2,1)}, bf16[1024,256]{1,0:T(8,128)(2,1)}, bf16[1024,256]{1,0:T(8,128)(2,1)}, bf16[1024,512]{1,0:T(8,128)(2,1)}, bf16[1024,3840]{1,0:T(8,128)(2,1)}) custom-call(bf16[1024,3840]{1,0:T(8,128)(2,1)} %all-gather.9.cloned.1.call-done.acts_hbm.refs_1_, bf16[3840,1024]{1,0:T(8,128)(2,1)} %pad_maximum_fusion.w_hbm, ...), custom_call_target="tpu_custom_call" | custom-call | flops 16079595520 | bytes 27525120 | tf_op jit(solution)/shard_map/pallas_call | solution.py:166
  131.2 22.4 %reduce-scatter.9.cloned.1.call-done = bf16[128,3840]{1,0:T(8,128)(2,1)} async-done(((bf16[1024,3840]{1,0:T(8,128)(2,1)}), bf16[128,3840]{1,0:T(8,128)(2,1)}) %reduce-scatter.9.cloned.1.call-update) | async-done | bytes 983056 | tf_op jit(solution)/shard_map/reduce_scatter | solution.py:408
  153.6 1.6 fusion.24
  155.3 0.9 copy-done.6
  156.2 1.2 fusion.9
  158.4 58.2 %all-gather.11.cloned.1.call-done.a_ref.refs_0_ = bf16[1024,3840]{1,0:T(8,128)(2,1)} async-done(((bf16[128,3840]{1,0:T(8,128)(2,1)}), bf16[1024,3840]{1,0:T(8,128)(2,1)}) %all-gather.11.cloned.1.call-update) | async-done | bytes 7864336 | tf_op jit(solution)/shard_map/all_gather | solution.py:405
  216.5 38.1 %shard_map.205 = (bf16[1024,1920]{1,0:T(8,128)(2,1)}, bf16[1024,1920]{1,0:T(8,128)(2,1)}, bf16[1024,1920]{1,0:T(8,128)(2,1)}) custom-call(bf16[1024,3840]{1,0:T(8,128)(2,1)} %all-gather.11.cloned.1.call-done.a_ref.refs_0_, bf16[3840,1920]{1,0:T(8,128)(2,1)} %refs_2_.3, bf16[3840,1920]{1,0:T(8,128)(2,1)} %refs_3_.3), custom_call_target="tpu_custom_call" | custom-call | flops 30198988800 | bytes 49152000 | tf_op jit(solution)/shard_map/pallas_call | solution.py:319
  254.7 3.0 constant_dynamic-slice_fusion
  257.6 21.5 %shard_map.206 = bf16[1024,3840]{1,0:T(8,128)(2,1)} custom-call(bf16[1024,1920]{1,0:T(8,128)(2,1)} %get-tuple-element.112.refs_0_, bf16[1920,3840]{1,0:T(8,128)(2,1)} %refs_1_.3), custom_call_target="tpu_custom_call" | custom-call | flops 15099494400 | bytes 26542080 | tf_op jit(solution)/shard_map/pallas_call | solution.py:87
  279.1 1.6 fusion.27
  280.8 0.9 copy-done.4
  281.7 1.3 fusion.8
  283.1 0.7 reduce-scatter.11.cloned.1.call-update
  284.6 0.7 collective-permute-start.3
  285.4 56.7 %collective-permute-done.3.refs_3_.refs_5_ = bf16[2,128,3840]{2,1,0:T(8,128)(2,1)} collective-permute-done((bf16[2,128,3840]{2,1,0:T(8,128)(2,1)S(1)}, bf16[2,128,3840]{2,1,0:T(8,128)(2,1)}, u32[]{:S(2)}, u32[]{:S(2)}) %collective-permute-start.3) | collective-permute-done | bytes 1966112 | tf_op jit(solution)/shard_map/ppermute | solution.py:496
  342.1 0.6 stack.46.off_ref
  342.7 3.6 collective-permute-done.4.refs_4_.refs_6_
  346.3 1.3 copy-done.45
  347.6 28.4 %shard_map.207 = (bf16[1024,1920]{1,0:T(8,128)(2,1)}, bf16[1024,1920]{1,0:T(8,128)(2,1)}) custom-call(s32[5]{0:T(128)} %stack.46.off_ref, bf16[2,256,3840]{2,1,0:T(8,128)(2,1)} %maximum_select_fusion.refs_0_.refs_2_, bf16[2,256,3840]{2,1,0:T(8,128)(2,1)} %collective-permute-done.1.refs_1_.refs_3_, ...), custom_call_target="tpu_custom_call" | custom-call | flops 15099494400 | bytes 38338560 | tf_op jit(solution)/shard_map/pallas_call | solution.py:273
  376.0 37.9 %shard_map.208 = bf16[1024,3840]{1,0:T(8,128)(2,1)} custom-call(bf16[1024,1920]{1,0:T(8,128)(2,1)} %get-tuple-element.91.refs_0_.refs_2_, bf16[1024,1920]{1,0:T(8,128)(2,1)} %get-tuple-element.92.refs_1_.refs_4_, bf16[3840,1920]{1,0:T(8,128)(2,1)} %refs_2_.3, bf16[3840,1920]{1,0:T(8,128)(2,1)} %refs_3_.3), custom_call_target="tpu_custom_call" | custom-call | flops 30198988800 | bytes 45219840 | tf_op jit(solution)/shard_map/pallas_call | solution.py:87
  414.4 38.8 %shard_map.209 = (bf16[1024,1920]{1,0:T(8,128)(2,1)}, bf16[1024,1920]{1,0:T(8,128)(2,1)}, bf16[1024,1920]{1,0:T(8,128)(2,1)}) custom-call(bf16[1024,3840]{1,0:T(8,128)(2,1)} %all-gather.13.cloned.1.call-done.a_ref.refs_1_, bf16[3840,1920]{1,0:T(8,128)(2,1)} %refs_2_.3, bf16[3840,1920]{1,0:T(8,128)(2,1)} %refs_3_.3), custom_call_target="tpu_custom_call" | custom-call | flops 30198988800 | bytes 49152000 | tf_op jit(solution)/shard_map/pallas_call | solution.py:319
  453.3 28.0 %shard_map.210 = (bf16[1024,1920]{1,0:T(8,128)(2,1)}, bf16[1024,1920]{1,0:T(8,128)(2,1)}) custom-call(s32[5]{0:T(128)} %stack.46.off_ref, bf16[2,256,3840]{2,1,0:T(8,128)(2,1)} %maximum_select_fusion.refs_0_.refs_2_, bf16[2,256,3840]{2,1,0:T(8,128)(2,1)} %collective-permute-done.1.refs_1_.refs_3_, ...), custom_call_target="tpu_custom_call" | custom-call | flops 15099494400 | bytes 38338560 | tf_op jit(solution)/shard_map/pallas_call | solution.py:273
  481.3 2.5 fusion.25
  483.9 2.7 fusion.12
  486.6 1.6 fusion.34
  488.5 38.3 %shard_map.211 = bf16[1024,3840]{1,0:T(8,128)(2,1)} custom-call(bf16[1024,1920]{1,0:T(8,128)(2,1)} %get-tuple-element.101.refs_0_.refs_3_, bf16[1024,1920]{1,0:T(8,128)(2,1)} %get-tuple-element.102.refs_1_.refs_5_, bf16[3840,1920]{1,0:T(8,128)(2,1)} %refs_2_.3, bf16[3840,1920]{1,0:T(8,128)(2,1)} %refs_3_.3), custom_call_target="tpu_custom_call" | custom-call | flops 30198988800 | bytes 45219840 | tf_op jit(solution)/shard_map/pallas_call | solution.py:87
  526.9 21.6 %shard_map.212 = bf16[1024,3840]{1,0:T(8,128)(2,1)} custom-call(bf16[1024,1920]{1,0:T(8,128)(2,1)} %get-tuple-element.103.refs_0_.refs_1_, bf16[1920,3840]{1,0:T(8,128)(2,1)} %refs_1_.3), custom_call_target="tpu_custom_call" | custom-call | flops 15099494400 | bytes 26542080 | tf_op jit(solution)/shard_map/pallas_call | solution.py:87
  548.6 29.2 %shard_map.213 = (bf16[1024,1024]{1,0:T(8,128)(2,1)}, bf16[1024,3840]{1,0:T(8,128)(2,1)}) custom-call(bf16[1024,3840]{1,0:T(8,128)(2,1)} %all-gather.15.cloned.1.call-done.cot_hbm.refs_2_, bf16[3840,1024]{1,0:T(8,128)(2,1)} %pad_maximum_fusion.w_hbm, bf16[512,3840]{1,0:T(8,128)(2,1)} %bitcast.49, bf16[1024,512]{1,0:T(8,128)(2,1)} %get-tuple-element.74.q, ...), custom_call_target="tpu_custom_call" | custom-call | flops 20079595520 | bytes 27525120 | tf_op jit(solution)/shard_map/pallas_call | solution.py:233
  577.9 1.6 reduce-scatter.19.cloned.1.call-done
  579.5 2.1 fusion.13
  581.6 1.6 fusion.33
  584.0 0.7 reduce-scatter.21.cloned.1.call-update
  584.8 71.7 %shard_map.214 = (bf16[3840,1920]{1,0:T(8,128)(2,1)}, bf16[3840,1920]{1,0:T(8,128)(2,1)}) custom-call(bf16[1024,3840]{1,0:T(8,128)(2,1)} %all-gather.11.cloned.1.call-done.a_ref.refs_0_, bf16[1024,3840]{1,0:T(8,128)(2,1)} %all-gather.13.cloned.1.call-done.a_ref.refs_1_, bf16[1024,1920]{1,0:T(8,128)(2,1)} %get-tuple-element.91.refs_0_.refs_2_, ...), custom_call_target="tpu_custom_call" | custom-call | flops 60397977600 | bytes 60948480 | tf_op jit(solution)/shard_map/pallas_call | solution.py:353
  656.5 38.8 %shard_map.215 = bf16[1920,3840]{1,0:T(8,128)(2,1)} custom-call(s32[5]{0:T(128)} %stack.46.off_ref, bf16[1024,1920]{1,0:T(8,128)(2,1)} %get-tuple-element.112.refs_0_, bf16[1024,1920]{1,0:T(8,128)(2,1)} %get-tuple-element.103.refs_0_.refs_1_, bf16[2,256,3840]{2,1,0:T(8,128)(2,1)} %maximum_select_fusion.refs_0_.refs_2_, ...), custom_call_target="tpu_custom_call" | custom-call | flops 30198988800 | bytes 38338560 | tf_op jit(solution)/shard_map/pallas_call | solution.py:293
  695.3 28.9 %shard_map.216 = (bf16[1024,1024]{1,0:T(8,128)(2,1)}, bf16[1024,3840]{1,0:T(8,128)(2,1)}) custom-call(bf16[1024,3840]{1,0:T(8,128)(2,1)} %all-gather.17.cloned.1.call-done.cot_hbm.refs_3_, bf16[3840,1024]{1,0:T(8,128)(2,1)} %pad_maximum_fusion.w_hbm, bf16[512,3840]{1,0:T(8,128)(2,1)} %bitcast.50, bf16[1024,512]{1,0:T(8,128)(2,1)} %get-tuple-element.76.q, ...), custom_call_target="tpu_custom_call" | custom-call | flops 20079595520 | bytes 27525120 | tf_op jit(solution)/shard_map/pallas_call | solution.py:233
  724.3 0.6 copy-done.25
  725.0 13.4 %shard_map.217 = bf16[512,3840]{1,0:T(8,128)(2,1)} custom-call(bf16[1024,512]{1,0:T(8,128)(2,1)} %get-tuple-element.117.refs_0_, bf16[1024,512]{1,0:T(8,128)(2,1)} %get-tuple-element.118.refs_1_, bf16[1024,3840]{1,0:T(8,128)(2,1)} %all-gather.15.cloned.1.call-done.cot_hbm.refs_2_, bf16[1024,3840]{1,0:T(8,128)(2,1)} %all-gather.17.cloned.1.call-done.cot_hbm.refs_3_), custom_call_target="tpu_custom_call" | custom-call | flops 8053063680 | bytes 21757952 | tf_op jit(solution)/shard_map/pallas_call | solution.py:353
  738.4 22.0 %shard_map.218 = (bf16[3840,512]{1,0:T(8,128)(2,1)}, bf16[3840,256]{1,0:T(8,128)(2,1)}, bf16[3840,256]{1,0:T(8,128)(2,1)}) custom-call(bf16[1024,3840]{1,0:T(8,128)(2,1)} %all-gather.7.cloned.1.call-done.acts_hbm.refs_0_, bf16[1024,3840]{1,0:T(8,128)(2,1)} %all-gather.9.cloned.1.call-done.acts_hbm.refs_1_, bf16[1024,1024]{1,0:T(8,128)(2,1)} %get-tuple-element.108.refs_2_, ...), custom_call_target="tpu_custom_call" | custom-call | flops 16106127360 | bytes 27787264 | tf_op jit(solution)/shard_map/pallas_call | solution.py:353
  760.4 9.2 %reshape.150 = bf16[3840,2,256]{2,1,0:T(2,128)(2,1)} reshape(bf16[3840,512]{1,0:T(8,128)(2,1)} %get-tuple-element.120) | data formatting | bytes 7864320 | tf_op jit(solution)/shard_map/reshape | solution.py:549
  769.7 2.5 fusion.29
  772.2 2.1 fusion.14
  774.4 1.4 pad_maximum_fusion.1
  775.8 0.7 copy-done.13
  776.6 1.6 fusion.32
  778.2 2.0 fusion.15
  780.2 0.6 pad_maximum_fusion.3.x_ref
  780.9 8.5 %tp_sum.1 = f32[2,3840]{1,0:T(2,128)} custom-call(f32[2,3840]{1,0:T(2,128)} %pad_maximum_fusion.3.x_ref), custom_call_target="tpu_custom_call" | custom-call | flops 5000000000 | bytes 1000000 | tf_op jit(solution)/shard_map/tp_sum/pallas_call | solution.py:382
  789.4 0.7 fusion.31
  790.1 0.7 slice_reduce_fusion
  790.8 1.4 pad_maximum_fusion.2
  (144 shorter events, 8.1 us)
Async XLA Ops:
  7.2 51.8 %all-gather.7.cloned.1.call-start = ((), (), s32[]{:S(2)}) async-start(), calls=%async_computation.8 | async-start | bytes 8847360 | tf_op jit(solution)/shard_map/all_gather | solution.py:405
  8.0 5.6 copy-start.23
  9.6 1.1 copy-start.2
  9.6 3.9 copy-start
  9.9 0.8 copy-start.39
  12.6 92.1 %all-gather.9.cloned.1.call-start = ((), (), s32[]{:S(2)}) async-start(), calls=%async_computation.10 | async-start | bytes 8847360 | tf_op jit(solution)/shard_map/all_gather | solution.py:405
  12.6 2.9 copy-start.11
  12.6 3.0 copy-start.28
  12.9 0.6 copy-start.37
  13.5 0.6 copy-start.29
  15.4 138.2 %reduce-scatter.9.cloned.1.call-start = ((), (), s32[]{:S(2)}) async-start(), calls=%async_computation.9 | async-start | bytes 8847360 | tf_op jit(solution)/shard_map/reduce_scatter | solution.py:408
  15.5 13.4 %collective-permute-start = (bf16[2,128,3840]{2,1,0:T(8,128)(2,1)S(1)}, bf16[2,128,3840]{2,1,0:T(8,128)(2,1)}, u32[]{:S(2)}, u32[]{:S(2)}) collective-permute-start(bf16[2,128,3840]{2,1,0:T(8,128)(2,1)S(1)} %copy-done.11), channel_id=1, source_target_pairs={{0,1},{1,0},{2,3},{3,2},{4,5},{5,4},{6,7},{7,6},{8,9},{9,8},{10,11... | collective-permute-start | bytes 5898248 | tf_op jit(solution)/shard_map/ppermute | solution.py:468
  22.1 2.4 copy-start.20
  22.1 3.0 copy-start.21
  85.6 0.7 copy-start.27
  85.7 130.9 %all-gather.11.cloned.1.call-start = ((), (), s32[]{:S(2)}) async-start(), calls=%async_computation.11 | async-start | bytes 8847360 | tf_op jit(solution)/shard_map/all_gather | solution.py:405
  104.7 48.9 %copy-start.10 = (bf16[2,128,3840]{2,1,0:T(8,128)(2,1)S(1)}, bf16[2,128,3840]{2,1,0:T(8,128)(2,1)}, u32[]{:S(2)}) copy-start(bf16[2,128,3840]{2,1,0:T(8,128)(2,1)} %param.12) | copy-start | bytes 5898244
  155.3 1.0 copy-start.6
  155.3 2.9 copy-start.41
  155.3 2.9 copy-start.33
  157.5 121.6 %reduce-scatter.13.cloned.1.call-start = ((), (), s32[]{:S(2)}) async-start(), calls=%async_computation.13 | async-start | bytes 8847360 | tf_op jit(solution)/shard_map/reduce_scatter | solution.py:408
  158.2 256.3 %all-gather.13.cloned.1.call-start = ((), (), s32[]{:S(2)}) async-start(), calls=%async_computation.14 | async-start | bytes 8847360 | tf_op jit(solution)/shard_map/all_gather | solution.py:405
  158.2 96.4 %collective-permute-start.1 = (bf16[2,256,3840]{2,1,0:T(8,128)(2,1)}, bf16[2,256,3840]{2,1,0:T(8,128)(2,1)}, u32[]{:S(2)}, u32[]{:S(2)}) collective-permute-start(bf16[2,256,3840]{2,1,0:T(8,128)(2,1)} %maximum_select_fusion.refs_0_.refs_2_), channel_id=1, source_target_pairs={{0,2},{1,7},{2,4},{3,1},{4,6},{5,3},{6,0},{7,5},{8,10},{9,15},{10,... | collective-permute-start | bytes 11796488 | tf_op jit(solution)/shard_map/ppermute | solution.py:477
  280.7 1.0 copy-start.4
  280.7 3.1 copy-start.43
  280.8 0.9 copy-start.35
  283.0 1.5 copy-start.22
  283.0 198.2 %reduce-scatter.11.cloned.1.call-start = ((), (), s32[]{:S(2)}) async-start(), calls=%async_computation.12 | async-start | bytes 8847360 | tf_op jit(solution)/shard_map/reduce_scatter | solution.py:408
  283.9 200.0 %reduce-scatter.15.cloned.1.call-start = ((), (), s32[]{:S(2)}) async-start(), calls=%async_computation.15 | async-start | bytes 8847360 | tf_op jit(solution)/shard_map/reduce_scatter | solution.py:408
  284.6 57.5 %collective-permute-start.3 = (bf16[2,128,3840]{2,1,0:T(8,128)(2,1)S(1)}, bf16[2,128,3840]{2,1,0:T(8,128)(2,1)}, u32[]{:S(2)}, u32[]{:S(2)}) collective-permute-start(bf16[2,128,3840]{2,1,0:T(8,128)(2,1)S(1)} %copy-done.22), channel_id=1, source_target_pairs={{0,2},{1,7},{2,4},{3,1},{4,6},{5,3},{6,0},{7,5},{8,10},{9,15},{10,... | collective-permute-start | bytes 5898248 | tf_op jit(solution)/shard_map/ppermute | solution.py:496
  285.2 61.1 %collective-permute-start.2 = (bf16[2,256,3840]{2,1,0:T(8,128)(2,1)}, bf16[2,256,3840]{2,1,0:T(8,128)(2,1)}, u32[]{:S(2)}, u32[]{:S(2)}) collective-permute-start(bf16[2,256,3840]{2,1,0:T(8,128)(2,1)} %collective-permute-done.1.refs_1_.refs_3_), channel_id=1, source_target_pairs={{0,1},{1,0},{2,3},{3,2},{4,5},{5,4},{6,7},{7,6},{8,9},{9,8},{10,11... | collective-permute-start | bytes 11796488 | tf_op jit(solution)/shard_map/ppermute | solution.py:497
  342.1 4.2 collective-permute-start.4
  346.3 1.3 copy-start.45
  413.9 134.7 %all-gather.15.cloned.1.call-start = ((), (), s32[]{:S(2)}) async-start(), calls=%async_computation.18 | async-start | bytes 8847360 | tf_op jit(solution)/shard_map/all_gather | solution.py:405
  453.3 28.0 %copy-start.7 = (bf16[128,3840]{1,0:T(8,128)(2,1)S(1)}, bf16[128,3840]{1,0:T(8,128)(2,1)}, u32[]{:S(2)}) copy-start(bf16[128,3840]{1,0:T(8,128)(2,1)} %copy-done.6) | copy-start | bytes 2949124
  481.3 2.6 copy-start.34
  481.3 5.3 copy-start.42
  481.3 5.3 copy-start.12
  483.9 2.7 copy-start.15
  488.3 91.2 %reduce-scatter.19.cloned.1.call-start = ((), (), s32[]{:S(2)}) async-start(), calls=%async_computation.17 | async-start | bytes 8847360 | tf_op jit(solution)/shard_map/reduce_scatter | solution.py:408
  526.8 168.4 %all-gather.17.cloned.1.call-start = ((), (), s32[]{:S(2)}) async-start(), calls=%async_computation.19 | async-start | bytes 8847360 | tf_op jit(solution)/shard_map/all_gather | solution.py:405
  548.6 30.9 %copy-start.5 = (bf16[128,3840]{1,0:T(8,128)(2,1)S(1)}, bf16[128,3840]{1,0:T(8,128)(2,1)}, u32[]{:S(2)}) copy-start(bf16[128,3840]{1,0:T(8,128)(2,1)} %copy-done.4) | copy-start | bytes 2949124
  548.6 30.9 %copy-start.36 = (f32[128]{0:T(128)S(1)}, f32[128]{0:T(128)}, u32[]{:S(2)}) copy-start(f32[128]{0:T(128)} %copy-done.35) | copy-start | bytes 1540
  577.8 3.7 copy-start.44
  579.5 2.1 copy-start.16
  583.2 186.4 %reduce-scatter.17.cloned.1.call-start = ((), (), s32[]{:S(2)}) async-start(), calls=%async_computation.16 | async-start | bytes 8847360 | tf_op jit(solution)/shard_map/reduce_scatter | solution.py:408
  583.9 188.3 %reduce-scatter.21.cloned.1.call-start = ((), (), s32[]{:S(2)}) async-start(), calls=%async_computation.20 | async-start | bytes 8847360 | tf_op jit(solution)/shard_map/reduce_scatter | solution.py:408
  584.7 193.5 %reduce-scatter.23.cloned.1.call-start = ((), (), s32[]{:S(2)}) async-start(), calls=%async_computation.21 | async-start | bytes 8847360 | tf_op jit(solution)/shard_map/reduce_scatter | solution.py:408
  724.2 0.7 copy-start.25
  769.6 2.6 copy-start.3
  769.6 2.6 copy-start.24
  769.6 2.6 copy-start.32
  769.7 4.7 copy-start.40
  769.7 4.7 copy-start.17
  772.2 2.1 copy-start.19
  774.4 1.5 copy-start.8
  774.4 2.2 copy-start.13
  776.6 1.6 copy-start.1
  776.6 1.6 copy-start.30
  780.9 8.5 %copy-start.38 = (f32[128]{0:T(128)S(1)}, f32[128]{0:T(128)}, u32[]{:S(2)}) copy-start(f32[128]{0:T(128)} %copy-done.37) | copy-start | bytes 1540
  780.9 8.5 %copy-start.9 = (bf16[128,3840]{1,0:T(8,128)(2,1)S(1)}, bf16[128,3840]{1,0:T(8,128)(2,1)}, u32[]{:S(2)}) copy-start(bf16[128,3840]{1,0:T(8,128)(2,1)} %fusion.33) | copy-start | bytes 2949124
  780.9 8.5 %copy-start.14 = (bf16[128,3840]{1,0:T(8,128)(2,1)S(1)}, bf16[128,3840]{1,0:T(8,128)(2,1)}, u32[]{:S(2)}) copy-start(bf16[128,3840]{1,0:T(8,128)(2,1)} %reduce-scatter.23.cloned.1.call-done) | copy-start | bytes 2949124
  789.4 0.8 copy-start.26
  789.4 1.4 copy-start.18
  (1 other events, 0.5 us)
Sparse Core Ops, SparseCore 0:
  12.7 46.2 all-gather.6
  61.1 43.4 all-gather.8
  107.5 46.0 reduce-scatter.8
  157.6 58.8 all-gather.10
  219.3 56.0 reduce-scatter.12
  283.1 59.4 all-gather.12
  345.5 45.1 reduce-scatter.10
  414.1 44.7 reduce-scatter.14
  488.4 42.1 all-gather.14
  533.4 46.0 reduce-scatter.18
  583.4 42.9 all-gather.16
  628.5 46.0 reduce-scatter.16
  676.9 45.4 reduce-scatter.20
  724.5 45.4 reduce-scatter.22
